TPU v7x, 8 devices: a whole 2x2x1 slice. The times are simulated.
8 devices in a mesh: dp: 1 (over z), ep: 8 (over y, x, core).
Axes of the slice: x: 2, y: 2, z: 1, core: 2. Of those that a mesh axis runs over, the one named last changes fastest.
Arguments:
- x_in: bfloat16 [4096, 1536], P(('dp', 'ep'))
- k_cache: bfloat16 [4096, 64, 8, 64], P(('dp', 'ep'))
- v_cache: bfloat16 [4096, 64, 8, 64], P(('dp', 'ep'))
- cache_len: int32 [4096], P(('dp', 'ep'))
- topk_idx: int32 [4096, 8], P(('dp', 'ep'))
- ln_attn: bfloat16 [1536], replicated
- w_q: bfloat16 [1536, 1536], replicated
- w_k: bfloat16 [1536, 512], replicated
- w_v: bfloat16 [1536, 512], replicated
- q_norm: bfloat16 [64], replicated
- k_norm: bfloat16 [64], replicated
- w_o: bfloat16 [1536, 1536], replicated
- ln_moe: bfloat16 [1536], replicated
- w_router: bfloat16 [1536, 40], replicated
- w_gate: bfloat16 [40, 1536, 512], P('ep')
- w_up: bfloat16 [40, 1536, 512], P('ep')
- w_down: bfloat16 [40, 512, 1536], P('ep')
Outputs:
- output 1: bfloat16 [4096, 1536], P(('dp', 'ep'))
- output 2: bfloat16 [4096, 64, 8, 64], P(('dp', 'ep'))
- output 3: bfloat16 [4096, 64, 8, 64], P(('dp', 'ep'))
All inputs are finite; a program needn't handle non-finite values.
Results may differ from a plain program's by a relative error of at most 0.0144126.
Values are sent between devices in bfloat16 or wider.
A program may use at most 1 GiB of HBM per device.

v0:
```python
import jax
import jax.numpy as jnp
from jax import lax
from jax.sharding import PartitionSpec as P

ROPE_BASE = 1000000.0
NORM_EPS = 1e-6


def norm_scale(values, gain_vec):
    return values * lax.rsqrt(jnp.mean(values * values, axis=-1, keepdims=True) + NORM_EPS) * gain_vec.astype(jnp.float32)


def rotate_halves(values, positions):
    half_dim = values.shape[-1] // 2
    freq_vec = ROPE_BASE ** (-jnp.arange(half_dim, dtype=jnp.float32) * 2.0 / values.shape[-1])
    angles = positions.astype(jnp.float32)[:, None, None] * freq_vec
    cosine = jnp.cos(angles)
    sine_val = jnp.sin(angles)
    lo_half = values[..., :half_dim]
    hi_half = values[..., half_dim:]
    return jnp.concatenate([lo_half * cosine - hi_half * sine_val, hi_half * cosine + lo_half * sine_val], axis=-1)


def attend_block(x_in, k_cache, v_cache, cache_len, ln_attn, w_q, w_k, w_v, q_norm, k_norm, w_o):
    n_batch, n_slots, kv_heads, head_dim = k_cache.shape
    q_heads = w_q.shape[1] // head_dim
    resid_in = x_in.astype(jnp.float32)
    normed = norm_scale(resid_in, ln_attn).astype(jnp.bfloat16)
    q_proj = jnp.dot(normed, w_q, preferred_element_type=jnp.float32).reshape(n_batch, q_heads, head_dim)
    k_proj = jnp.dot(normed, w_k, preferred_element_type=jnp.float32).reshape(n_batch, kv_heads, head_dim)
    v_new = jnp.dot(normed, w_v, preferred_element_type=jnp.float32).astype(jnp.bfloat16).reshape(n_batch, kv_heads, head_dim)
    q_rot = rotate_halves(norm_scale(q_proj, q_norm), cache_len).astype(jnp.bfloat16).reshape(n_batch, kv_heads, q_heads // kv_heads, head_dim)
    k_new = rotate_halves(norm_scale(k_proj, k_norm), cache_len).astype(jnp.bfloat16)
    len_col = cache_len[:, None, None, None]
    is_new = lax.broadcasted_iota(jnp.int32, (1, n_slots, 1, 1), 1) == len_col
    k_full = jnp.where(is_new, k_new[:, None], k_cache)
    v_full = jnp.where(is_new, v_new[:, None], v_cache)
    scores = jnp.einsum('bgrd,bsgd->bgrs', q_rot, k_full, preferred_element_type=jnp.float32) * head_dim ** -0.5
    seen = lax.broadcasted_iota(jnp.int32, (1, 1, 1, n_slots), 3) <= len_col
    attn_prob = jax.nn.softmax(jnp.where(seen, scores, -1e30), axis=-1).astype(jnp.bfloat16)
    attn_out = jnp.einsum('bgrs,bsgd->bgrd', attn_prob, v_full, preferred_element_type=jnp.float32).astype(jnp.bfloat16).reshape(n_batch, q_heads * head_dim)
    x_mid = (resid_in + jnp.dot(attn_out, w_o, preferred_element_type=jnp.float32)).astype(jnp.bfloat16)
    return x_mid, k_full, v_full


def route_gate(x_mid, ln_moe, w_router, topk_idx):
    resid_mid = x_mid.astype(jnp.float32)
    h_moe = norm_scale(resid_mid, ln_moe).astype(jnp.bfloat16)
    logits = jnp.dot(h_moe, w_router, preferred_element_type=jnp.float32)
    gate_wts = jax.nn.softmax(jnp.take_along_axis(logits, topk_idx, axis=1), axis=-1)
    return resid_mid, h_moe, gate_wts


def pack_rows(h_moe, topk_idx, ep_size, e_local, cap_rows):
    b_dev, top_k = topk_idx.shape
    pair_count = b_dev * top_k
    flat_idx = topk_idx.reshape(pair_count)
    dest_dev = flat_idx // e_local
    dest_hot = (dest_dev[:, None] == jnp.arange(ep_size)[None, :]).astype(jnp.int32)
    dev_counts = jnp.sum(dest_hot, axis=0)
    slot_rank = jnp.sum(jnp.cumsum(dest_hot, axis=0) * dest_hot, axis=1) - 1
    dev_start = jnp.cumsum(dev_counts) - dev_counts
    sort_order = jnp.argsort(dest_dev, stable=True)
    seat_ids = jnp.arange(cap_rows)
    pair_at = sort_order[jnp.minimum(dev_start[:, None] + seat_ids[None, :], pair_count - 1)]
    filled = seat_ids[None, :] < dev_counts[:, None]
    send_rows = jnp.where(filled[:, :, None], h_moe[pair_at // top_k], jnp.zeros((), jnp.bfloat16))
    send_ids = jnp.where(filled, (flat_idx % e_local)[pair_at], e_local - 1)
    return send_rows, send_ids, dest_dev * cap_rows + slot_rank


def group_count(row_ids, e_local):
    return jnp.sum((row_ids[:, None] == jnp.arange(e_local)[None, :]).astype(jnp.int32), axis=0)


def expert_sorted(sorted_rows, group_sizes, w_gate, w_up, w_down):
    gate_act = lax.ragged_dot(sorted_rows, w_gate, group_sizes, preferred_element_type=jnp.float32)
    up_act = lax.ragged_dot(sorted_rows, w_up, group_sizes, preferred_element_type=jnp.float32)
    hidden_act = (jax.nn.silu(gate_act) * up_act).astype(jnp.bfloat16)
    return lax.ragged_dot(hidden_act, w_down, group_sizes, preferred_element_type=jnp.float32).astype(jnp.bfloat16)


def expert_rows(tok_rows, row_ids, w_gate, w_up, w_down):
    sort_order = jnp.argsort(row_ids, stable=True)
    sorted_out = expert_sorted(tok_rows[sort_order], group_count(row_ids, w_gate.shape[0]), w_gate, w_up, w_down)
    return sorted_out[jnp.argsort(sort_order, stable=True)]


def unpack_rows(back_rows, flat_slot, gate_wts):
    b_dev, top_k = gate_wts.shape
    picked = back_rows[flat_slot].reshape(b_dev, top_k, back_rows.shape[1])
    return jnp.sum(picked.astype(jnp.float32) * gate_wts[:, :, None], axis=1)


def solution(mesh):
    ep_size = mesh.shape['ep']
    row_spec = P(('dp', 'ep'))
    replicated = P()
    expert_spec = P('ep')
    in_specs = (row_spec, row_spec, row_spec, row_spec, row_spec, replicated, replicated, replicated, replicated, replicated, replicated, replicated, replicated, replicated, expert_spec, expert_spec, expert_spec)
    out_specs = (row_spec, row_spec, row_spec)

    def device_step(x_in, k_cache, v_cache, cache_len, topk_idx, ln_attn, w_q, w_k, w_v, q_norm, k_norm, w_o, ln_moe, w_router, w_gate, w_up, w_down):
        x_mid, k_full, v_full = attend_block(x_in, k_cache, v_cache, cache_len, ln_attn, w_q, w_k, w_v, q_norm, k_norm, w_o)
        resid_mid, h_moe, gate_wts = route_gate(x_mid, ln_moe, w_router, topk_idx)
        b_dev, top_k = topk_idx.shape
        hidden = h_moe.shape[1]
        e_local = w_gate.shape[0]
        cap_rows = min(b_dev, 2 * b_dev * top_k // ep_size)
        send_rows, send_ids, flat_slot = pack_rows(h_moe, topk_idx, ep_size, e_local, cap_rows)
        recv_rows = lax.all_to_all(send_rows, 'ep', 0, 0, tiled=True).reshape(ep_size * cap_rows, hidden)
        recv_ids = lax.all_to_all(send_ids, 'ep', 0, 0, tiled=True).reshape(ep_size * cap_rows)
        expert_out = expert_rows(recv_rows, recv_ids, w_gate, w_up, w_down)
        back_rows = lax.all_to_all(expert_out.reshape(ep_size, cap_rows, hidden), 'ep', 0, 0, tiled=True).reshape(ep_size * cap_rows, hidden)
        moe_out = unpack_rows(back_rows, flat_slot, gate_wts)
        return (resid_mid + moe_out).astype(jnp.bfloat16), k_full, v_full

    return jax.shard_map(device_step, mesh=mesh, in_specs=in_specs, out_specs=out_specs, check_vma=False)
```

profile of v0, /device:TPU:0, one launch (start us, length us, event | category | flops | bytes accessed | tf_op | source)
XLA Modules:
  0.0 937.1 jit_solution(1593762273344074364)
XLA Ops:
  0.6 0.8 broadcast_divide_fusion
  1.5 0.7 compare_and_fusion
  3.5 2.3 reduce-window.19
  7.1 0.7 fusion.16
  8.1 5.8 sort.45
  13.9 23.0 %gather_fusion = s32[4096]{0:T(1024)S(1)} fusion(s32[4096]{0:T(1024)S(1)} %get-tuple-element.6, s32[4096]{0:T(1024)S(1)} %broadcast_clamp_fusion.2), kind=kCustom, calls=%fused_computation | custom fusion | bytes 49152 | tf_op jit(solution)/shard_map/gather | solution.py:66
  36.9 0.6 fusion.23
  37.6 23.0 %gather_fusion.2 = s32[4096]{0:T(1024)S(1)} fusion(s32[4096]{0:T(1024)S(1)} %get-tuple-element.34, s32[4096]{0:T(1024)S(1)} %broadcast_clamp_fusion.3), kind=kCustom, calls=%fused_computation.2 | custom fusion | bytes 49152 | tf_op jit(solution)/shard_map/gather | solution.py:69
  60.6 0.7 compare_select_fusion.1
  61.3 4.8 all-to-all-start.1
  66.3 0.7 iota_compare_fusion.5
  67.4 2.1 multiply_reduce_fusion.1
  69.5 1.9 convolution_convert_fusion.1
  71.9 1.5 multiply_multiply_fusion.1
  73.6 44.5 %broadcast_select_fusion.1 = (bf16[512,64,8,64]{0,3,2,1:T(8,128)(2,1)}, bf16[512,64,8,64]{0,3,2,1:T(8,128)(2,1)}) fusion(bf16[512,64,8,64]{0,3,2,1:T(8,128)(2,1)} %param.18, pred[512,64]{0,1:T(8,128)(4,1)S(1)} %copy.70, bf16[512,8,64]{0,2,1:T(8,128)(2,1)S(1)} %pad_maximum_fusion.1, bf16[512,64,8,64]{0,3,2,1:T(8,128)(2,1)} %param.19, ...), kind=kLoop, calls=%fused_computation.9 | loop fusion | flops 33554432 | bytes 135299072 | tf_op jit(solution)/shard_map/jit(_where)/select_n | solution.py:37
  118.1 91.4 %copy.72 = bf16[512,64,8,64]{3,1,2,0:T(8,128)(2,1)} copy(bf16[512,64,8,64]{0,3,2,1:T(8,128)(2,1)} %get-tuple-element.29) | data formatting | bytes 67108864 | tf_op jit(solution)/shard_map/jit(_where)/select_n | solution.py:37
  209.5 4.7 fusion.35
  214.9 0.6 multiply_multiply_fusion
  215.5 0.5 subtract_convert_fusion
  216.2 5.6 copy.71
  221.8 91.4 %copy.73 = bf16[512,64,8,64]{3,1,2,0:T(8,128)(2,1)} copy(bf16[512,64,8,64]{0,3,2,1:T(8,128)(2,1)} %get-tuple-element.30) | data formatting | bytes 67108864 | tf_op jit(solution)/shard_map/jit(_where)/select_n | solution.py:38
  313.2 43.9 %fusion.37 = (f32[512,8,3]{2,1,0:T(8,128)}, f32[512,8,3,64]{3,2,1,0:T(4,128)}) fusion(pred[512,64]{1,0:T(8,128)(4,1)S(1)} %get-tuple-element.39, bf16[512,8,3,64]{3,2,1,0:T(4,128)(2,1)} %copy.71, bf16[512,64,8,64]{3,1,2,0:T(8,128)(2,1)} %copy.72), kind=kOutput, calls=%fused_computation.116 | convolution fusion | flops 103809088 | bytes 38354944 | tf_op jit(solution)/shard_map/sub | solution.py:41
  357.1 29.6 %convolution_convert_fusion = bf16[512,8,3,64]{3,2,1,0:T(4,128)(2,1)} fusion(bf16[512,64,8,64]{3,1,2,0:T(8,128)(2,1)} %copy.73, f32[512,8,3,64]{3,2,1,0:T(4,128)} %get-tuple-element.44, f32[512,8,3]{2,1,0:T(8,128)} %get-tuple-element.43), kind=kOutput, calls=%fused_computation.24 | convolution fusion | flops 103022592 | bytes 38322176 | tf_op jit(solution)/shard_map/bgrs,bsgd->bgrd/dot_general | solution.py:42
  386.7 5.6 copy.74
  392.4 5.3 fusion.10
  397.7 1.1 copy-done.2
  399.2 19.2 %gather_fusion.1 = bf16[4096,1536]{1,0:T(8,128)(2,1)} fusion(bf16[512,1536]{1,0:T(8,128)(2,1)S(1)} %fusion.12, s32[4096]{0:T(1024)S(1)} %broadcast_clamp_fusion), kind=kCustom, calls=%fused_computation.1 | custom fusion | bytes 25182208 | tf_op jit(solution)/shard_map/gather | solution.py:68
  418.5 10.9 %broadcast_select_fusion.2 = bf16[8,512,1536]{2,1,0:T(8,128)(2,1)} fusion(bf16[8,512,1536]{2,1,0:T(8,128)(2,1)} %bitcast.64, pred[8,512]{1,0:T(8,128)(4,1)S(1)} %copy-done.13), kind=kLoop, calls=%fused_computation.12 | loop fusion | flops 6291456 | bytes 25169920 | tf_op jit(solution)/shard_map/jit(_where)/select_n | solution.py:68
  429.4 4.1 all-to-all-start
  433.5 6.5 sort.46
  440.0 1.4 convert_reduce_fusion
  441.4 1.5 ragged-dot-metadata
  442.9 5.8 sort.47
  448.7 123.8 %all-to-all-done = bf16[8,512,1536]{2,1,0:T(8,128)(2,1)} async-done(((bf16[8,512,1536]{2,1,0:T(8,128)(2,1)}), bf16[8,512,1536]{2,1,0:T(8,128)(2,1)}, u32[]{:S(2)}, u32[]{:S(2)}) %all-to-all-start) | async-done | bytes 12582944 | tf_op jit(solution)/shard_map/all_to_all | solution.py:112
  572.4 31.5 %gather_fusion.3 = bf16[4096,1536]{1,0:T(8,128)(2,1)} fusion(bf16[4096,1536]{1,0:T(8,128)(2,1)} %bitcast.11, s32[4096]{0:T(1024)S(1)} %fusion.24), kind=kCustom, calls=%fused_computation.3 | custom fusion | bytes 25182208 | tf_op jit(solution)/shard_map/gather | solution.py:86
  604.0 24.0 %ragged-dot-none.2 = f32[4096,512]{1,0:T(8,128)} custom-call(s32[1]{0:T(128)} %get-tuple-element.9, s32[6]{0:T(128)} %get-tuple-element.10, s32[20]{0:T(128)} %get-tuple-element.11, s32[20]{0:T(128)} %get-tuple-element.12, s32[1]{0:T(128)} %get-tuple-element.9, bf16[4096,1536]{1,0:T(8,128)(2,1)} %gather_fusion.3, bf16[5,1536,512]{2,1,0:T(8,128)(2,1)} %param.31), custom_call_target="tpu_custom_call" | custom-call | flops 6442450944 | bytes 28835860 | tf_op jit(solution)/shard_map/ragged_dot_general/ragged-dot-none
  628.0 24.0 %ragged-dot-none.1 = f32[4096,512]{1,0:T(8,128)} custom-call(s32[1]{0:T(128)} %get-tuple-element.9, s32[6]{0:T(128)} %get-tuple-element.10, s32[20]{0:T(128)} %get-tuple-element.11, s32[20]{0:T(128)} %get-tuple-element.12, s32[1]{0:T(128)} %get-tuple-element.9, bf16[4096,1536]{1,0:T(8,128)(2,1)} %gather_fusion.3, bf16[5,1536,512]{2,1,0:T(8,128)(2,1)} %param.32), custom_call_target="tpu_custom_call" | custom-call | flops 6442450944 | bytes 28835860 | tf_op jit(solution)/shard_map/ragged_dot_general/ragged-dot-none
  652.0 8.8 multiply_convert_fusion
  660.8 25.3 %ragged-dot-none = f32[4096,1536]{1,0:T(8,128)} custom-call(s32[1]{0:T(128)} %get-tuple-element.9, s32[6]{0:T(128)} %get-tuple-element.10, s32[20]{0:T(128)} %get-tuple-element.11, s32[20]{0:T(128)} %get-tuple-element.12, s32[1]{0:T(128)} %get-tuple-element.9, bf16[4096,512]{1,0:T(8,128)(2,1)} %multiply_convert_fusion, bf16[5,512,1536]{2,1,0:T(8,128)(2,1)} %param.33), custom_call_target="tpu_custom_call" | custom-call | flops 6442450944 | bytes 37224468 | tf_op jit(solution)/shard_map/ragged_dot_general/ragged-dot-none
  686.0 13.3 %convert_element_type.88 = bf16[4096,1536]{1,0:T(8,128)(2,1)} convert(f32[4096,1536]{1,0:T(8,128)} %ragged-dot-none) | non-fusion elementwise | flops 6291456 | bytes 37748736 | tf_op jit(solution)/shard_map/convert_element_type | solution.py:81
  699.3 31.5 %gather_fusion.4 = bf16[4096,1536]{1,0:T(8,128)(2,1)} fusion(bf16[4096,1536]{1,0:T(8,128)(2,1)} %convert_element_type.88, s32[4096]{0:T(1024)S(1)} %fusion.25), kind=kCustom, calls=%fused_computation.4 | custom fusion | bytes 25182208 | tf_op jit(solution)/shard_map/gather | solution.py:87
  730.8 4.2 all-to-all-start.2
  735.7 0.6 fusion.40
  736.3 33.0 %gather_fusion.6 = f32[4096]{0:T(1024)S(1)} fusion(f32[512,40]{0,1:T(8,128)S(1)} %fusion.40, s32[4096]{0:T(1024)S(1)} %reshape.598), kind=kCustom, calls=%fused_computation.6 | custom fusion | bytes 65536 | tf_op jit(solution)/shard_map/jit(take_along_axis)/gather | solution.py:51
  769.9 104.1 %all-to-all-done.2 = bf16[8,512,1536]{2,1,0:T(8,128)(2,1)} async-done(((bf16[8,512,1536]{2,1,0:T(8,128)(2,1)}), bf16[8,512,1536]{2,1,0:T(8,128)(2,1)}, u32[]{:S(2)}, u32[]{:S(2)}) %all-to-all-start.2) | async-done | bytes 12582944 | tf_op jit(solution)/shard_map/all_to_all | solution.py:115
  874.0 31.5 %gather_fusion.5 = bf16[4096,1536]{1,0:T(8,128)(2,1)} fusion(bf16[4096,1536]{1,0:T(8,128)(2,1)} %bitcast.13, s32[4096]{0:T(1024)S(1)} %broadcast_clamp_fusion.1), kind=kCustom, calls=%fused_computation.5 | custom fusion | bytes 25182208 | tf_op jit(solution)/shard_map/gather | solution.py:92
  905.5 29.6 %fusion.1 = f32[512,1536]{1,0:T(8,128)S(1)} fusion(bf16[4096,1536]{1,0:T(8,128)(2,1)} %gather_fusion.5, f32[512,8]{1,0:T(8,128)S(1)} %copy.84), kind=kLoop, calls=%fused_computation.11 | loop fusion | flops 18087936 | bytes 15745024 | tf_op jit(solution)/shard_map/reduce_sum | solution.py:93
  935.1 1.6 fusion.13
  (103 shorter events, 6.4 us)
Async XLA Ops:
  0.6 66.8 %copy-start = (bf16[1536,512]{1,0:T(8,128)(2,1)S(1)}, bf16[1536,512]{1,0:T(8,128)(2,1)}, u32[]{:S(2)}) copy-start(bf16[1536,512]{1,0:T(8,128)(2,1)} %param.24) | copy-start | bytes 4718596
  2.4 4.5 copy-start.4
  2.9 0.6 copy-start.7
  37.5 28.6 %copy-start.14 = (s32[512]{0:T(512)S(1)}, s32[512]{0:T(512)}, u32[]{:S(2)}) copy-start(s32[512]{0:T(512)} %param.20) | copy-start | bytes 6148
  37.5 29.4 %copy-start.15 = (bf16[1536]{0:T(1024)(128)(2,1)S(1)}, bf16[1536]{0:T(1024)(128)(2,1)}, u32[]{:S(2)}) copy-start(bf16[1536]{0:T(1024)(128)(2,1)} %param.22) | copy-start | bytes 9220
  37.6 29.4 %copy-start.6 = (bf16[512,1536]{1,0:T(8,128)(2,1)S(1)}, bf16[512,1536]{1,0:T(8,128)(2,1)}, u32[]{:S(2)}) copy-start(bf16[512,1536]{1,0:T(8,128)(2,1)} %param.17) | copy-start | bytes 4718596
  61.3 368.1 %all-to-all-start.1 = ((s32[8,1,512]{2,1,0:T(1,128)}), s32[8,1,512]{2,1,0:T(1,128)}, u32[]{:S(2)}, u32[]{:S(2)}) async-start(s32[8,1,512]{2,1,0:T(1,128)} %compare_select_fusion.1), calls=%async_computation.1 | async-start | bytes 32768 | tf_op jit(solution)/shard_map/all_to_all | solution.py:113
  67.3 2.1 copy-start.18
  67.4 2.2 copy-start.17
  214.2 0.7 copy-start.19
  392.4 5.3 copy-start.16
  392.4 5.3 copy-start.12
  397.7 1.1 copy-start.2
  399.2 19.2 %copy-start.13 = (pred[8,512]{1,0:T(8,128)(4,1)S(1)}, pred[8,512]{1,0:T(8,128)(4,1)}, u32[]{:S(2)}) copy-start(pred[8,512]{1,0:T(8,128)(4,1)} %iota_compare_fusion.5) | copy-start | bytes 12292
  429.4 143.1 %all-to-all-start = ((bf16[8,512,1536]{2,1,0:T(8,128)(2,1)}), bf16[8,512,1536]{2,1,0:T(8,128)(2,1)}, u32[]{:S(2)}, u32[]{:S(2)}) async-start(bf16[8,512,1536]{2,1,0:T(8,128)(2,1)} %broadcast_select_fusion.2), calls=%async_computation | async-start | bytes 25165824 | tf_op jit(solution)/shard_map/all_to_all | solution.py:112
  730.8 4.2 copy-start.5
  730.8 4.4 copy-start.8
  730.8 4.6 copy-start.9
  730.8 4.9 copy-start.10
  730.8 143.2 %all-to-all-start.2 = ((bf16[8,512,1536]{2,1,0:T(8,128)(2,1)}), bf16[8,512,1536]{2,1,0:T(8,128)(2,1)}, u32[]{:S(2)}, u32[]{:S(2)}) async-start(bf16[8,512,1536]{2,1,0:T(8,128)(2,1)} %bitcast.63), calls=%async_computation.2 | async-start | bytes 25165824 | tf_op jit(solution)/shard_map/all_to_all | solution.py:115
  736.3 33.5 %copy-start.11 = (s32[4096]{0:T(1024)S(1)}, s32[4096]{0:T(1024)}, u32[]{:S(2)}) copy-start(s32[4096]{0:T(1024)} %get-tuple-element.21) | copy-start | bytes 49156
  905.5 29.6 %copy-start.3 = (bf16[512,1536]{1,0:T(8,128)(2,1)S(1)}, bf16[512,1536]{1,0:T(8,128)(2,1)}, u32[]{:S(2)}) copy-start(bf16[512,1536]{1,0:T(8,128)(2,1)} %copy-done.2) | copy-start | bytes 4718596
  905.5 31.2 %copy-start.1 = (bf16[1536,512]{1,0:T(8,128)(2,1)S(1)}, bf16[1536,512]{1,0:T(8,128)(2,1)}, u32[]{:S(2)}) copy-start(bf16[1536,512]{1,0:T(8,128)(2,1)} %param.24) | copy-start | bytes 4718596
where the time goes:
time: 947 us; the launch traced here: 937 us
  local copies, waits for them, and re-layouts  391 us (41%)
  waiting for transfers between devices  228 us (24%)
  other arithmetic  140 us (15%)
  matrix products  88.1 us (9%)
  Pallas kernels  74.8 us (8%)
  starting transfers between devices  13.2 us (1%)
    all_to_all x1, waiting for transfers between devices, device_step(): lax.all_to_all(send_rows, 'ep', 0, 0, tiled=True)  124 us
    all_to_all x1, waiting for transfers between devices, device_step(): lax.all_to_all(expert_out.reshape(ep_size, cap_rows, hidden), 'ep', 0, 0,...  104 us
    select_n x1, local copies, waits for them, and re-layouts, attend_block(): v_full = jnp.where(is_new, v_new[:, None], v_cache)  91.4 us
    select_n x1, local copies, waits for them, and re-layouts, attend_block(): k_full = jnp.where(is_new, k_new[:, None], k_cache)  91.4 us
    another operation x3, Pallas kernels  73.3 us
    select_n x1, other arithmetic, attend_block(): k_full = jnp.where(is_new, k_new[:, None], k_cache)  44.5 us
    sub x1, matrix products, attend_block(): jax.nn.softmax(jnp.where(seen, scores, -1e+30), axis=-1)  43.9 us
    gather x5, local copies, waits for them, and re-layouts, route_gate(): jnp.take_along_axis(logits, topk_idx, axis=1)  33.6 us
  transfers between devices with their start and end apart: 3, of which 2 were waited for; matrix products, arithmetic and copies ran while one was open for 44% of the time, Pallas kernels for 0%

commit v1 on v0

v1 whole, which is shorter than its diff:
```python
import functools

import jax
import jax.numpy as jnp
from jax import lax
from jax.experimental import pallas as pl
from jax.experimental.pallas import tpu as pltpu
from jax.sharding import PartitionSpec as P


ROPE_BASE = 1000000.0
NORM_EPS = 1e-6
PIECE = 128
SORTED = 640
ROOM = 768


def norm_scale(values, gain_vec):
    return values * lax.rsqrt(jnp.mean(values * values, axis=-1, keepdims=True) + NORM_EPS) * gain_vec.astype(jnp.float32)


def attend_kernel(len_ref, cos_ref, sin_ref, qn_ref, kn_ref, q_ref, k_ref, v_ref, kc_ref, vc_ref, ko_ref, vo_ref, o_ref, part_ref, p_ref):
    n_rep = q_ref.shape[0]
    n_slots = kc_ref.shape[0]
    n_batch = q_ref.shape[2]
    unroll = 4

    def norm_rope(values, gain, cosine, sine):
        ms = jnp.mean(values * values, axis=0, keepdims=True)
        values = values * lax.rsqrt(ms + NORM_EPS) * gain
        half = values.shape[0] // 2
        lo, hi = values[:half], values[half:]
        return jnp.concatenate([lo * cosine - hi * sine, hi * cosine + lo * sine], axis=0).astype(jnp.bfloat16)

    for bt in range(n_batch // 128):
        lanes = pl.ds(bt * 128, 128)
        cosine, sine = cos_ref[:, lanes], sin_ref[:, lanes]
        lens = len_ref[:, lanes]
        left0 = jnp.broadcast_to(lens.astype(jnp.float32), (16, 128)).astype(jnp.bfloat16)
        k_new = norm_rope(k_ref[0, :, lanes], kn_ref[...], cosine, sine).reshape(4, 16, 128)
        v_new = v_ref[0, :, lanes].reshape(4, 16, 128)
        qs = [norm_rope(q_ref[r, :, lanes], qn_ref[...], cosine, sine).astype(jnp.float32).reshape(8, 8, 128) for r in range(n_rep)]

        def k_step(i, left):
            for u in range(unroll):
                s = i * unroll + u
                tile = jnp.where((left == 0)[None], k_new, kc_ref[s, 0, :, :, lanes])
                ko_ref[s, 0, :, :, lanes] = tile
                wide = tile.astype(jnp.float32).reshape(8, 8, 128)
                for r in range(n_rep):
                    part_ref[r, pl.ds(pl.multiple_of(s * 8, 8), 8), :] = jnp.sum(wide * qs[r], axis=0)
                left = left - jnp.ones_like(left)
            return left

        lax.fori_loop(0, n_slots // unroll, k_step, left0)
        seen = lax.broadcasted_iota(jnp.int32, (n_slots, 128), 0) <= lens
        for r in range(n_rep):
            scores = part_ref[r, pl.ds(0, n_slots, stride=8), :]
            for sub in range(1, 8):
                scores = scores + part_ref[r, pl.ds(sub, n_slots, stride=8), :]
            scores = jnp.where(seen, scores * (q_ref.shape[1] ** -0.5), -1e30)
            expd = jnp.exp(scores - jnp.max(scores, axis=0, keepdims=True))
            prob = expd / jnp.sum(expd, axis=0, keepdims=True)
            p_ref[r] = prob.astype(jnp.bfloat16).astype(jnp.float32)

        def v_step(i, carry):
            left, accs = carry
            for u in range(unroll):
                s = i * unroll + u
                tile = jnp.where((left == 0)[None], v_new, vc_ref[s, 0, :, :, lanes])
                vo_ref[s, 0, :, :, lanes] = tile
                wide = tile.astype(jnp.float32).reshape(8, 8, 128)
                accs = tuple(accs[r] + wide * p_ref[r, pl.ds(s, 1), :][None] for r in range(n_rep))
                left = left - jnp.ones_like(left)
            return left, accs

        zero = jnp.zeros((8, 8, 128), jnp.float32)
        _, accs = lax.fori_loop(0, n_slots // unroll, v_step, (left0, (zero,) * n_rep))
        for r in range(n_rep):
            o_ref[r, :, lanes] = accs[r].reshape(64, 128).astype(jnp.bfloat16)


def attend(x_in, k_cache, v_cache, cache_len, len_row, ln_attn, w_q, w_k, w_v, q_norm, k_norm):
    n_batch, n_slots, kv_heads, head_dim = k_cache.shape
    q_heads = w_q.shape[1] // head_dim
    n_rep = q_heads // kv_heads
    normed = norm_scale(x_in.astype(jnp.float32), ln_attn).astype(jnp.bfloat16)

    def proj(w):
        return jnp.dot(normed, w, preferred_element_type=jnp.float32).T.reshape(-1, head_dim, n_batch)

    q_t, k_t, v_t = proj(w_q), proj(w_k), proj(w_v).astype(jnp.bfloat16)
    half = head_dim // 2
    freq = ROPE_BASE ** (-jnp.arange(half, dtype=jnp.float32) * 2.0 / head_dim)
    angles = freq[:, None] * cache_len.astype(jnp.float32)[None, :]

    def by_slot(c):
        return c.transpose(1, 2, 3, 0).reshape(n_slots, kv_heads, 4, 16, n_batch)

    full = lambda *shape: pl.BlockSpec(shape, lambda g: (0,) * len(shape))
    cache_spec = pl.BlockSpec((n_slots, 1, 4, 16, n_batch), lambda g: (0, g, 0, 0, 0))
    head_spec = lambda n: pl.BlockSpec((n, head_dim, n_batch), lambda g: (g, 0, 0))
    cache_shape = jax.ShapeDtypeStruct((n_slots, kv_heads, 4, 16, n_batch), jnp.bfloat16)
    k_new, v_new, o_t = pl.pallas_call(
        attend_kernel,
        grid=(kv_heads,),
        in_specs=[full(1, n_batch), full(half, n_batch), full(half, n_batch), full(head_dim, 1), full(head_dim, 1),
                  head_spec(n_rep), head_spec(1), head_spec(1), cache_spec, cache_spec],
        out_specs=[cache_spec, cache_spec, head_spec(n_rep)],
        out_shape=[cache_shape, cache_shape, jax.ShapeDtypeStruct((q_heads, head_dim, n_batch), jnp.bfloat16)],
        scratch_shapes=[pltpu.VMEM((n_rep, n_slots * 8, 128), jnp.float32), pltpu.VMEM((n_rep, n_slots, 128), jnp.float32)],
        compiler_params=pltpu.CompilerParams(dimension_semantics=("arbitrary",), vmem_limit_bytes=50 * 2**20),
        cost_estimate=pl.CostEstimate(flops=50_000_000_000, bytes_accessed=140_000_000, transcendentals=0),
        name="attend",
    )(len_row[None, :], jnp.cos(angles), jnp.sin(angles), q_norm.astype(jnp.float32)[:, None], k_norm.astype(jnp.float32)[:, None],
      q_t, k_t, v_t, by_slot(k_cache), by_slot(v_cache))

    def by_row(c):
        return c.reshape(n_slots, kv_heads, head_dim, n_batch).transpose(3, 0, 1, 2)

    return o_t.reshape(q_heads * head_dim, n_batch), by_row(k_new), by_row(v_new)


def expert_kernel(n_sub, e_local, start_ref, count_ref, prow_ref, pcol_ref, r_ref, *refs):
    h_refs = refs[:2 * n_sub]
    w_refs = refs[2 * n_sub:2 * n_sub + 6]
    o_refs = refs[2 * n_sub + 6:4 * n_sub + 6]
    xs_ref, ys_ref = refs[4 * n_sub + 6:]
    step = pl.program_id(0)
    src = step // e_local
    half = h_refs[0].shape[0]
    hidden = h_refs[0].shape[1]

    @pl.when(step == 0)
    def _():
        ys_ref[...] = jnp.zeros_like(ys_ref)
        for j in range(n_sub):
            xs_ref[j, SORTED:, :] = jnp.zeros((ROOM - SORTED, hidden), jnp.bfloat16)

    @pl.when(step % e_local == 0)
    def _():
        for j in range(n_sub):
            prow = prow_ref[2 * j + src]
            for c in range(SORTED // PIECE):
                seat = lax.broadcasted_iota(jnp.int32, (PIECE, 2 * half), 0) + c * PIECE
                hot = jnp.where(seat == prow, 1.0, 0.0).astype(jnp.bfloat16)
                rows = jnp.dot(hot[:, :half], h_refs[2 * j][...], preferred_element_type=jnp.float32)
                rows = rows + jnp.dot(hot[:, half:], h_refs[2 * j + 1][...], preferred_element_type=jnp.float32)
                xs_ref[j, c * PIECE:(c + 1) * PIECE, :] = rows.astype(jnp.bfloat16)

    counts = [count_ref[j * 2 * e_local + step] for j in range(n_sub)]
    trips = functools.reduce(jnp.maximum, counts)

    def run(wg_ref, wu_ref, wd_ref):
        def piece(c, carry):
            offs = [pl.multiple_of(jnp.minimum(start_ref[j * 2 * e_local + step] + c * PIECE, SORTED), 16) for j in range(n_sub)]
            rows = jnp.concatenate([xs_ref[j, pl.ds(offs[j], PIECE), :] for j in range(n_sub)], axis=0)
            gate = jnp.dot(rows, wg_ref[0], preferred_element_type=jnp.float32)
            up = jnp.dot(rows, wu_ref[0], preferred_element_type=jnp.float32)
            act = (jax.nn.silu(gate) * up).astype(jnp.bfloat16)
            out = jnp.dot(act, wd_ref[0], preferred_element_type=jnp.float32).astype(jnp.bfloat16)
            for j in range(n_sub):
                @pl.when(c < counts[j])
                def _(j=j):
                    ys_ref[j, pl.ds(offs[j], PIECE), :] = out[j * PIECE:(j + 1) * PIECE]
            return carry

        lax.fori_loop(0, trips, piece, 0)

    def back(which, first):
        for j in range(n_sub):
            for c in range(2 * half // PIECE):
                rows = slice(c * PIECE, (c + 1) * PIECE)
                seat = lax.broadcasted_iota(jnp.int32, (PIECE, SORTED), 1)
                hot = jnp.where(seat == pcol_ref[2 * j + which, rows, :], 1.0, 0.0).astype(jnp.bfloat16)
                mine = jnp.dot(hot, ys_ref[j, :SORTED, :], preferred_element_type=jnp.float32) * r_ref[2 * j + which, rows, :]
                o_ref = o_refs[2 * j + c * PIECE // half]
                at = slice(c * PIECE % half, c * PIECE % half + PIECE)
                if first:
                    o_ref[at, :] = mine
                else:
                    o_ref[at, :] = o_ref[at, :] + mine

    @pl.when(src == 0)
    def _():
        run(*w_refs[:3])

    @pl.when(src == 1)
    def _():
        run(*w_refs[3:])

    @pl.when(step == e_local - 1)
    def _():
        back(0, True)

    @pl.when(step == 2 * e_local - 1)
    def _():
        back(1, False)


def experts(blocks, starts, counts, prow, pcol, r_col, w_own, w_par):
    n_sub = len(blocks)
    half, hidden = blocks[0][0].shape
    e_local, _, ff = w_own[0].shape
    once = pl.Buffered(1)
    full = lambda *shape: pl.BlockSpec(shape, lambda e, *_: (0,) * len(shape), pipeline_mode=once)
    own = lambda a, b: pl.BlockSpec((1, a, b), lambda e, *_: (jnp.minimum(e, e_local - 1), 0, 0))
    par = lambda a, b: pl.BlockSpec((1, a, b), lambda e, *_: (jnp.maximum(e - e_local, 0), 0, 0))
    flat = [h for block in blocks for h in block]
    out = pl.pallas_call(
        functools.partial(expert_kernel, n_sub, e_local),
        grid_spec=pltpu.PrefetchScalarGridSpec(
            num_scalar_prefetch=2,
            grid=(2 * e_local,),
            in_specs=[full(2 * n_sub, 1, 2 * half), full(2 * n_sub, 2 * half, 1), full(2 * n_sub, 2 * half, 1)]
            + [full(half, hidden)] * (2 * n_sub)
            + [own(hidden, ff), own(hidden, ff), own(ff, hidden), par(hidden, ff), par(hidden, ff), par(ff, hidden)],
            out_specs=[full(half, hidden)] * (2 * n_sub),
            scratch_shapes=[pltpu.VMEM((n_sub, ROOM, hidden), jnp.bfloat16)] * 2,
        ),
        out_shape=[jax.ShapeDtypeStruct((half, hidden), jnp.float32)] * (2 * n_sub),
        compiler_params=pltpu.CompilerParams(dimension_semantics=("arbitrary",), vmem_limit_bytes=60 * 2**20),
        cost_estimate=pl.CostEstimate(flops=n_sub * 16_000_000_000, bytes_accessed=60_000_000, transcendentals=0),
    )(starts.reshape(-1), counts.reshape(-1), prow.reshape(2 * n_sub, 1, 2 * half), pcol.reshape(2 * n_sub, 2 * half, 1), r_col.reshape(2 * n_sub, 2 * half, 1),
      *flat, *w_own, *w_par)
    return [(out[2 * j], out[2 * j + 1]) for j in range(n_sub)]


def seats(topk_blocks, me, e_local):
    n_rows = topk_blocks.shape[1]
    dev = topk_blocks // e_local
    loc = topk_blocks % e_local
    both = jnp.stack([me, me ^ 1])
    loc_src = jnp.sum(jnp.where(dev[:, None] == both[None, :, None, None], loc[:, None], 0), axis=-1)
    hot = (loc_src[:, :, None, :] == jnp.arange(e_local)[None, None, :, None])
    before = (jnp.arange(n_rows)[:, None] < jnp.arange(n_rows)[None, :]).astype(jnp.bfloat16)
    rank = lax.dot_general(hot.astype(jnp.bfloat16), before, (((3,), (0,)), ((), ())), preferred_element_type=jnp.float32).astype(jnp.int32)
    count = jnp.sum(hot.astype(jnp.int32), axis=-1)
    padded = (count + 15) // 16 * 16
    starts = [jnp.zeros_like(count[..., 0])]
    for e in range(1, e_local):
        starts.append(starts[-1] + padded[..., e - 1])
    start = jnp.stack(starts, axis=-1)
    seat = jnp.sum(jnp.where(hot, start[..., None] + rank, 0), axis=2)
    return seat, start, (count + PIECE - 1) // PIECE


def solution(mesh):
    ep_size = mesh.shape['ep']
    row_spec = P(('dp', 'ep'))
    replicated = P()
    expert_spec = P('ep')
    in_specs = (row_spec, row_spec, row_spec, row_spec, row_spec, replicated, replicated, replicated, replicated, replicated, replicated, replicated, replicated, replicated, expert_spec, expert_spec, expert_spec)
    out_specs = (row_spec, row_spec, row_spec)

    def swap(value, bit):
        return lax.ppermute(value, 'ep', [(i, i ^ bit) for i in range(ep_size)])

    def device_step(x_in, k_cache, v_cache, cache_len, topk_idx, ln_attn, w_q, w_k, w_v, q_norm, k_norm, w_o, ln_moe, w_router, w_gate, w_up, w_down):
        me = lax.axis_index('ep')
        e_local = w_gate.shape[0]
        half = x_in.shape[0] // 2
        w_own = (w_gate, w_up, w_down)
        w_par = tuple(swap(w, 1) for w in w_own)
        t_y = swap(topk_idx, 4)
        topk_blocks = jnp.stack([topk_idx, swap(topk_idx, 2), t_y, swap(t_y, 2)])
        seat, start, count = seats(topk_blocks, me, e_local)

        len_row, seat, start, count = lax.optimization_barrier((cache_len, seat, start, count))
        attn_t, k_full, v_full = attend(x_in, k_cache, v_cache, cache_len, len_row, ln_attn, w_q, w_k, w_v, q_norm, k_norm)
        resid = x_in.astype(jnp.float32)
        o_proj = lax.dot_general(attn_t, w_o, (((0,), (0,)), ((), ())), preferred_element_type=jnp.float32)
        x_mid = (resid + o_proj).astype(jnp.bfloat16)
        resid_mid = x_mid.astype(jnp.float32)
        h_moe = norm_scale(resid_mid, ln_moe).astype(jnp.bfloat16)
        h_a, h_b = h_moe[:half], h_moe[half:]

        h_xb, h_ya = swap(h_b, 2), swap(h_a, 4)
        h_xa, h_yb = swap(h_a, 2), swap(h_b, 4)
        h_da, h_db = swap(h_ya, 2), swap(h_xb, 4)

        logits = jnp.dot(h_moe, w_router, preferred_element_type=jnp.float32)
        chosen = jnp.any(topk_idx[:, :, None] == jnp.arange(logits.shape[1])[None, None, :], axis=1)
        top = jnp.max(jnp.where(chosen, logits, -jnp.inf), axis=1, keepdims=True)
        expd = jnp.where(chosen, jnp.exp(jnp.where(chosen, logits - top, 0.0)), 0.0)
        gate = expd / jnp.sum(expd, axis=1, keepdims=True)
        r_dev = jnp.sum(gate.reshape(-1, ep_size, e_local), axis=-1).T
        r_y = swap(r_dev, 4)
        r_x = swap(r_dev, 2)
        r_d = swap(r_y, 2)

        def mine(r):
            rows = lax.broadcasted_iota(jnp.int32, r.shape, 0)
            return jnp.stack([jnp.sum(jnp.where(rows == d, r, 0.0), axis=0) for d in (me, me ^ 1)])

        def call(ids, blocks, rs):
            pick = slice(ids[0], ids[-1] + 1)
            return experts(blocks, start[pick], count[pick], seat[pick], seat[pick], jnp.stack([mine(r) for r in rs]), w_own, w_par)

        (s_o,) = call((0,), [(h_a, h_b)], [r_dev])
        h_xa, h_xb, h_ya, h_yb, s_o = lax.optimization_barrier((h_xa, h_xb, h_ya, h_yb, s_o))
        s_x, s_y = call((1, 2), [(h_xa, h_xb), (h_ya, h_yb)], [r_x, r_y])
        h_da, h_db, s_x, s_y = lax.optimization_barrier((h_da, h_db, s_x, s_y))
        u_x = swap(s_x[0], 2)
        u_y = swap(s_y[1], 4)
        (s_d,) = call((3,), [(h_da, h_db)], [r_d])
        d_x, d_y = swap(s_d[0], 2), swap(s_d[1], 4)
        m_x, m_y = swap(s_x[1] + d_y, 2), swap(s_y[0] + d_x, 4)
        moe_a = s_o[0] + u_x + m_y
        moe_b = s_o[1] + u_y + m_x
        x_out = (resid_mid + jnp.concatenate([moe_a, moe_b], axis=0)).astype(jnp.bfloat16)
        return x_out, k_full, v_full

    return jax.shard_map(device_step, mesh=mesh, in_specs=in_specs, out_specs=out_specs, check_vma=False)
```

time: 947 us -> 328 us (0.35)
  local copies, waits for them, and re-layouts: 391 us -> 20.1 us
  other arithmetic: 140 us -> 7.76 us
  waiting for transfers between devices: 228 us -> 99.8 us
  Pallas kernels: 74.8 us -> 163 us
  matrix products: 88.1 us -> 15.1 us
    all_to_all x3 -> x0, waiting for transfers between devices: 228 us -> none  [the longest x1 124 us: device_step(): lax.all_to_all(send_rows, 'ep', 0, 0, tiled=True)]
    gather x12 -> x0, local copies, waits for them, and re-layouts: 193 us -> none  [the longest x5 33.6 us: route_gate(): jnp.take_along_axis(logits, topk_idx, axis=1)]
    select_n x2 -> x0, local copies, waits for them, and re-layouts: 183 us -> none  [the longest x1 91.4 us: attend_block(): v_full = jnp.where(is_new, v_new[:, None], v_cache)]
    pallas_call x0 -> x4, Pallas kernels: none -> 163 us  [the longest x3 95.9 us: experts(): pl.pallas_call(functools.partial(expert_kernel, n_sub, e_local), grid_spe...]
    ppermute x0 -> x21, waiting for transfers between devices: none -> 99.8 us  [swap(): return lax.ppermute(value, 'ep', [(i, i ^ bit) for i in range(ep_size)])]
    another operation x3 -> x0, Pallas kernels: 73.3 us -> none
    select_n x6 -> x2, other arithmetic: 56.1 us -> 0.1 us  [the longest x1 0.07 us: seats(): dev = topk_blocks // e_local]
    sub x1 -> x0, matrix products: 43.9 us -> none  [attend_block(): jax.nn.softmax(jnp.where(seen, scores, -1e+30), axis=-1)]
  transfers between devices with their start and end apart: 3 -> 21, of which waited for: 2 -> 8; matrix products, arithmetic and copies ran while one was open for 44% -> 12% of each run, Pallas kernels for 0% -> 41%
where the time goes in v1:
time: 328 us; the launch traced here: 327 us
  Pallas kernels  163 us (50%)
  waiting for transfers between devices  99.8 us (30%)
  starting transfers between devices  20.8 us (6%)
  local copies, waits for them, and re-layouts  20.1 us (6%)
  matrix products  15.1 us (5%)
  other arithmetic  7.76 us (2%)
    ppermute x21, waiting for transfers between devices, swap(): return lax.ppermute(value, 'ep', [(i, i ^ bit) for i in range(ep_size)])  99.8 us
    pallas_call x3, Pallas kernels, experts(): pl.pallas_call(functools.partial(expert_kernel, n_sub, e_local), grid_spe...  95.9 us
    pallas_call x1, Pallas kernels, attend(): pl.pallas_call(attend_kernel, grid=(kv_heads,), in_specs=[full(1, n_batch...  67 us
    ppermute x21, starting transfers between devices, swap(): return lax.ppermute(value, 'ep', [(i, i ^ bit) for i in range(ep_size)])  20.8 us
    dot_general x3, matrix products, proj(): jnp.dot(normed, w, preferred_element_type=jnp.float32)  9.05 us
  transfers between devices with their start and end apart: 21, of which 8 were waited for; matrix products, arithmetic and copies ran while one was open for 12% of the time, Pallas kernels for 41%

profile of v1, /device:TPU:0, one launch (start us, length us, event | category | flops | bytes accessed | tf_op | source)
XLA Modules:
  0.0 327.5 jit_solution(11221239595048196150)
XLA Ops:
  0.7 3.4 %collective-permute-start.1 = (s32[512,8]{0,1:T(8,128)}, s32[512,8]{0,1:T(8,128)S(1)}, u32[]{:S(2)}, u32[]{:S(2)}) collective-permute-start(s32[512,8]{0,1:T(8,128)} %param.21), channel_id=1, source_target_pairs={{0,4},{1,5},{2,6},{3,7},{4,0},{5,1},{6,2},{7,3}} | collective-permute-start | bytes 49160 | tf_op jit(solution)/shard_map/ppermute | solution.py:257
  4.0 1.5 collective-permute-start
  6.0 0.8 fusion.13
  6.8 0.7 convert_element_type.49
  7.5 1.8 fusion
  9.4 6.8 %convolution_bitcast_fusion = f32[1536,512]{0,1:T(8,128)} fusion(bf16[1536,1536]{1,0:T(8,128)(2,1)} %param.23, bf16[512,1536]{1,0:T(8,128)(2,1)S(1)} %copy-done.3, f32[1536]{0:T(1024)S(1)} %convert_element_type.49, f32[512]{0:T(512)S(1)} %add_rsqrt_fusion.1), kind=kOutput, calls=%fused_computation.6 | convolution fusion | flops 2419064832 | bytes 9445376 | tf_op jit(solution)/shard_map/dot_general | solution.py:90
  16.1 1.1 fusion.20
  17.6 1.1 convolution_convert_fusion
  19.7 3.7 %copy.86 = f32[1536,512]{1,0:T(8,128)} copy(f32[1536,512]{0,1:T(8,128)} %convolution_bitcast_fusion) | data formatting | bytes 6291456 | tf_op jit(solution)/shard_map/transpose | solution.py:90
  24.6 67.0 %attend.1 = (bf16[64,8,4,16,512]{4,3,2,1,0:T(8,128)(2,1)}, bf16[64,8,4,16,512]{4,3,2,1,0:T(8,128)(2,1)}, bf16[24,64,512]{2,1,0:T(8,128)(2,1)S(1)}) custom-call(s32[1,512]{1,0:T(1,128)S(1)} %bitcast.72, f32[32,512]{1,0:T(8,128)S(1)} %get-tuple-element.90.cos_ref, f32[32,512]{1,0:T(8,128)S(1)} %get-tuple-element.89.sin_ref, f32[64,1]{1,0:T(8,128)S(1)} %copy.87.qn_ref, ...), custom_call_target="tpu_custom_call" | custom-call | flops 49999998976 | bytes 140000000 | tf_op jit(solution)/shard_map/attend/pallas_call | solution.py:104
  91.6 5.2 %fusion.3 = (f32[512]{0:T(512)S(1)}, bf16[512,1536]{1,0:T(8,128)(2,1)S(1)}) fusion(bf16[1536,512]{1,0:T(8,128)(2,1)S(1)} %bitcast.73, bf16[1536,1536]{1,0:T(8,128)(2,1)} %param.28, bf16[512,1536]{1,0:T(8,128)(2,1)S(1)} %copy-done.5), kind=kOutput, calls=%fused_computation.10 | convolution fusion | flops 2420637184 | bytes 9439232 | tf_op jit(solution)/shard_map/dot_general | solution.py:272
  98.6 2.0 collective-permute-start.12
  100.5 1.2 fusion.23
  102.3 1.5 collective-permute-start.15
  103.8 0.6 slice_reduce_fusion
  104.9 1.1 collective-permute-done.15
  106.0 1.2 collective-permute-start.5
  107.3 1.9 reshape.244.pcol_ref
  109.2 0.6 reshape.243.prow_ref
  109.8 0.7 reshape.223.start_ref
  110.4 0.6 reshape.224.count_ref
  111.1 1.0 reshape.242.pcol_ref
  112.1 0.7 reshape.228.start_ref
  112.8 0.7 reshape.229.count_ref
  113.4 0.6 reshape.233.start_ref
  114.1 0.7 reshape.234.count_ref
  114.7 1.0 reshape.246.pcol_ref
  115.9 1.0 copy.97.r_ref
  116.9 1.0 copy.91.r_ref
  118.0 1.9 reshape.245.r_ref
  119.9 2.9 collective-permute-done.4.refs_1_
  122.9 0.8 collective-permute-start.3
  123.8 1.5 collective-permute-start.6
  125.9 1.3 collective-permute-start.11
  127.2 28.6 %shard_map.184 = (f32[256,1536]{1,0:T(8,128)}, f32[256,1536]{1,0:T(8,128)}) custom-call(s32[10]{0:T(128)} %reshape.223.start_ref, s32[10]{0:T(128)} %reshape.224.count_ref, s32[2,1,512]{2,1,0:T(1,128)} %get-tuple-element.81.prow_ref, s32[2,512,1]{2,1,0:T(8,128)} %reshape.242.pcol_ref, f32[2,512,1]{2,1,0:T(8,128)} %copy.91.r_ref, ...), custom_call_target="tpu_custom_call" | custom-call | flops 16000000000 | bytes 60000000 | tf_op jit(solution)/shard_map/pallas_call | solution.py:210
  155.8 38.5 %shard_map.185 = (f32[256,1536]{1,0:T(8,128)}, f32[256,1536]{1,0:T(8,128)}, f32[256,1536]{1,0:T(8,128)}, f32[256,1536]{1,0:T(8,128)}) custom-call(s32[20]{0:T(128)} %reshape.228.start_ref, s32[20]{0:T(128)} %reshape.229.count_ref, s32[4,1,512]{2,1,0:T(1,128)} %reshape.243.prow_ref, s32[4,512,1]{2,1,0:T(8,128)} %reshape.244.pcol_ref, ...), custom_call_target="tpu_custom_call" | custom-call | flops 32000000000 | bytes 60000000 | tf_op jit(solution)/shard_map/pallas_call | solution.py:210
  194.4 0.9 copy-done.16
  195.3 28.8 %shard_map.186 = (f32[256,1536]{1,0:T(8,128)}, f32[256,1536]{1,0:T(8,128)}) custom-call(s32[10]{0:T(128)} %reshape.233.start_ref, s32[10]{0:T(128)} %reshape.234.count_ref, s32[2,1,512]{2,1,0:T(1,128)} %get-tuple-element.80.prow_ref, s32[2,512,1]{2,1,0:T(8,128)} %reshape.246.pcol_ref, f32[2,512,1]{2,1,0:T(8,128)} %copy.97.r_ref, ...), custom_call_target="tpu_custom_call" | custom-call | flops 16000000000 | bytes 60000000 | tf_op jit(solution)/shard_map/pallas_call | solution.py:210
  224.1 0.7 collective-permute-start.16
  224.8 1.7 collective-permute-start.19
  226.8 34.8 %collective-permute-done.16 = f32[256,1536]{1,0:T(8,128)S(1)} collective-permute-done((f32[256,1536]{1,0:T(8,128)}, f32[256,1536]{1,0:T(8,128)S(1)}, u32[]{:S(2)}, u32[]{:S(2)}) %collective-permute-start.16) | collective-permute-done | bytes 1572896 | tf_op jit(solution)/shard_map/ppermute | solution.py:257
  261.8 0.7 collective-permute-start.17
  262.5 1.3 collective-permute-start.18
  264.1 0.7 collective-permute-start.20
  264.8 30.5 %collective-permute-done.14 = f32[256,1536]{1,0:T(8,128)S(1)} collective-permute-done((f32[256,1536]{1,0:T(8,128)}, f32[256,1536]{1,0:T(8,128)S(1)}, u32[]{:S(2)}, u32[]{:S(2)}) %collective-permute-start.14) | collective-permute-done | bytes 1572896 | tf_op jit(solution)/shard_map/ppermute | solution.py:257
  295.3 3.8 %collective-permute-done.17 = f32[256,1536]{1,0:T(8,128)S(1)} collective-permute-done((f32[256,1536]{1,0:T(8,128)S(1)}, f32[256,1536]{1,0:T(8,128)S(1)}, u32[]{:S(2)}, u32[]{:S(2)}) %collective-permute-start.17) | collective-permute-done | bytes 1572896 | tf_op jit(solution)/shard_map/ppermute | solution.py:257
  299.5 26.0 %collective-permute-done.18 = f32[256,1536]{1,0:T(8,128)S(1)} collective-permute-done((f32[256,1536]{1,0:T(8,128)S(1)}, f32[256,1536]{1,0:T(8,128)S(1)}, u32[]{:S(2)}, u32[]{:S(2)}) %collective-permute-start.18) | collective-permute-done | bytes 1572896 | tf_op jit(solution)/shard_map/ppermute | solution.py:257
  325.9 1.6 fusion.6
  (101 shorter events, 8.1 us)
Async XLA Ops:
  0.6 15.5 %copy-start = (bf16[1536,512]{1,0:T(8,128)(2,1)S(1)}, bf16[1536,512]{1,0:T(8,128)(2,1)}, u32[]{:S(2)}) copy-start(bf16[1536,512]{1,0:T(8,128)(2,1)} %param.24) | copy-start | bytes 4718596
  0.6 8.7 %copy-start.3 = (bf16[512,1536]{1,0:T(8,128)(2,1)S(1)}, bf16[512,1536]{1,0:T(8,128)(2,1)}, u32[]{:S(2)}) copy-start(bf16[512,1536]{1,0:T(8,128)(2,1)} %param.17) | copy-start | bytes 4718596
  0.7 18.4 %collective-permute-start.1 = (s32[512,8]{0,1:T(8,128)}, s32[512,8]{0,1:T(8,128)S(1)}, u32[]{:S(2)}, u32[]{:S(2)}) collective-permute-start(s32[512,8]{0,1:T(8,128)} %param.21), channel_id=1, source_target_pairs={{0,4},{1,5},{2,6},{3,7},{4,0},{5,1},{6,2},{7,3}} | collective-permute-start | bytes 49160 | tf_op jit(solution)/shard_map/ppermute | solution.py:257
  4.0 19.7 %collective-permute-start = (s32[512,8]{0,1:T(8,128)}, s32[512,8]{0,1:T(8,128)S(1)}, u32[]{:S(2)}, u32[]{:S(2)}) collective-permute-start(s32[512,8]{0,1:T(8,128)} %param.21), channel_id=1, source_target_pairs={{0,2},{1,3},{2,0},{3,1},{4,6},{5,7},{6,4},{7,5}} | collective-permute-start | bytes 49160 | tf_op jit(solution)/shard_map/ppermute | solution.py:257
  5.5 119.9 %collective-permute-start.7 = (bf16[5,1536,512]{2,1,0:T(8,128)(2,1)}, bf16[5,1536,512]{2,1,0:T(8,128)(2,1)}, u32[]{:S(2)}, u32[]{:S(2)}) collective-permute-start(bf16[5,1536,512]{2,1,0:T(8,128)(2,1)} %refs_2_.3), channel_id=1, source_target_pairs={{0,1},{1,0},{2,3},{3,2},{4,5},{5,4},{6,7},{7,6}} | collective-permute-start | bytes 23592968 | tf_op jit(solution)/shard_map/ppermute | solution.py:257
  5.5 120.4 %collective-permute-start.8 = (bf16[5,1536,512]{2,1,0:T(8,128)(2,1)}, bf16[5,1536,512]{2,1,0:T(8,128)(2,1)}, u32[]{:S(2)}, u32[]{:S(2)}) collective-permute-start(bf16[5,1536,512]{2,1,0:T(8,128)(2,1)} %refs_3_.3), channel_id=1, source_target_pairs={{0,1},{1,0},{2,3},{3,2},{4,5},{5,4},{6,7},{7,6}} | collective-permute-start | bytes 23592968 | tf_op jit(solution)/shard_map/ppermute | solution.py:257
  6.0 121.2 %collective-permute-start.9 = (bf16[5,512,1536]{2,1,0:T(8,128)(2,1)}, bf16[5,512,1536]{2,1,0:T(8,128)(2,1)}, u32[]{:S(2)}, u32[]{:S(2)}) collective-permute-start(bf16[5,512,1536]{2,1,0:T(8,128)(2,1)} %refs_4_.5), channel_id=1, source_target_pairs={{0,1},{1,0},{2,3},{3,2},{4,5},{5,4},{6,7},{7,6}} | collective-permute-start | bytes 23592968 | tf_op jit(solution)/shard_map/ppermute | solution.py:257
  9.3 6.8 %copy-start.4 = (bf16[512,1536]{1,0:T(8,128)(2,1)S(1)}, bf16[512,1536]{1,0:T(8,128)(2,1)}, u32[]{:S(2)}) copy-start(bf16[512,1536]{1,0:T(8,128)(2,1)} %param.17) | copy-start | bytes 4718596
  16.1 1.4 copy-start.13
  17.5 1.2 copy-start.2
  17.5 1.2 copy-start.17
  17.5 1.2 copy-start.18
  19.1 4.6 %collective-permute-start.2 = (s32[512,8]{0,1:T(8,128)S(1)}, s32[512,8]{0,1:T(8,128)S(1)}, u32[]{:S(2)}, u32[]{:S(2)}) collective-permute-start(s32[512,8]{0,1:T(8,128)S(1)} %collective-permute-done.1), channel_id=1, source_target_pairs={{0,2},{1,3},{2,0},{3,1},{4,6},{5,7},{6,4},{7,5}} | collective-permute-start | bytes 49160 | tf_op jit(solution)/shard_map/ppermute | solution.py:257
  19.7 3.9 %copy-start.12 = (bf16[1536]{0:T(1024)(128)(2,1)S(1)}, bf16[1536]{0:T(1024)(128)(2,1)}, u32[]{:S(2)}) copy-start(bf16[1536]{0:T(1024)(128)(2,1)} %param.29) | copy-start | bytes 9220
  19.7 4.0 %copy-start.11 = (s32[512,8]{0,1:T(8,128)S(1)}, s32[512,8]{0,1:T(8,128)}, u32[]{:S(2)}) copy-start(s32[512,8]{0,1:T(8,128)} %param.21) | copy-start | bytes 49156
  24.6 67.0 %copy-start.5 = (bf16[512,1536]{1,0:T(8,128)(2,1)S(1)}, bf16[512,1536]{1,0:T(8,128)(2,1)}, u32[]{:S(2)}) copy-start(bf16[512,1536]{1,0:T(8,128)(2,1)} %param.17) | copy-start | bytes 4718596
  96.9 0.9 copy-start.10
  98.5 3.8 %collective-permute-start.13 = (f32[8,512]{1,0:T(8,128)S(1)}, f32[8,512]{1,0:T(8,128)S(1)}, u32[]{:S(2)}, u32[]{:S(2)}) collective-permute-start(f32[8,512]{1,0:T(8,128)S(1)} %bitcast.78), channel_id=1, source_target_pairs={{0,4},{1,5},{2,6},{3,7},{4,0},{5,1},{6,2},{7,3}} | collective-permute-start | bytes 49160 | tf_op jit(solution)/shard_map/ppermute | solution.py:257
  98.6 5.8 %collective-permute-start.12 = (f32[8,512]{1,0:T(8,128)S(1)}, f32[8,512]{1,0:T(8,128)S(1)}, u32[]{:S(2)}, u32[]{:S(2)}) collective-permute-start(f32[8,512]{1,0:T(8,128)S(1)} %bitcast.79), channel_id=1, source_target_pairs={{0,2},{1,3},{2,0},{3,1},{4,6},{5,7},{6,4},{7,5}} | collective-permute-start | bytes 49160 | tf_op jit(solution)/shard_map/ppermute | solution.py:257
  102.3 3.8 %collective-permute-start.15 = (f32[8,512]{1,0:T(8,128)S(1)}, f32[8,512]{1,0:T(8,128)S(1)}, u32[]{:S(2)}, u32[]{:S(2)}) collective-permute-start(f32[8,512]{1,0:T(8,128)S(1)} %collective-permute-done.13), channel_id=1, source_target_pairs={{0,2},{1,3},{2,0},{3,1},{4,6},{5,7},{6,4},{7,5}} | collective-permute-start | bytes 49160 | tf_op jit(solution)/shard_map/ppermute | solution.py:257
  104.4 18.5 %collective-permute-start.4 = (bf16[256,1536]{1,0:T(8,128)(2,1)}, bf16[256,1536]{1,0:T(8,128)(2,1)S(1)}, u32[]{:S(2)}, u32[]{:S(2)}) collective-permute-start(bf16[256,1536]{1,0:T(8,128)(2,1)} %get-tuple-element.76.refs_1_), channel_id=1, source_target_pairs={{0,2},{1,3},{2,0},{3,1},{4,6},{5,7},{6,4},{7,5}} | collective-permute-start | bytes 2359304 | tf_op jit(solution)/shard_map/ppermute | solution.py:257
  106.0 17.8 %collective-permute-start.5 = (bf16[256,1536]{1,0:T(8,128)(2,1)}, bf16[256,1536]{1,0:T(8,128)(2,1)}, u32[]{:S(2)}, u32[]{:S(2)}) collective-permute-start(bf16[256,1536]{1,0:T(8,128)(2,1)} %get-tuple-element.77.refs_0_), channel_id=1, source_target_pairs={{0,4},{1,5},{2,6},{3,7},{4,0},{5,1},{6,2},{7,3}} | collective-permute-start | bytes 2359304 | tf_op jit(solution)/shard_map/ppermute | solution.py:257
  122.9 33.0 %copy-start.15 = (bf16[256,1536]{1,0:T(8,128)(2,1)}, bf16[256,1536]{1,0:T(8,128)(2,1)S(1)}, u32[]{:S(2)}) copy-start(bf16[256,1536]{1,0:T(8,128)(2,1)S(1)} %collective-permute-done.4.refs_1_) | copy-start | bytes 2359300
  122.9 33.0 %collective-permute-start.3 = (bf16[256,1536]{1,0:T(8,128)(2,1)}, bf16[256,1536]{1,0:T(8,128)(2,1)}, u32[]{:S(2)}, u32[]{:S(2)}) collective-permute-start(bf16[256,1536]{1,0:T(8,128)(2,1)} %get-tuple-element.77.refs_0_), channel_id=1, source_target_pairs={{0,2},{1,3},{2,0},{3,1},{4,6},{5,7},{6,4},{7,5}} | collective-permute-start | bytes 2359304 | tf_op jit(solution)/shard_map/ppermute | solution.py:257
  123.8 32.0 %collective-permute-start.6 = (bf16[256,1536]{1,0:T(8,128)(2,1)}, bf16[256,1536]{1,0:T(8,128)(2,1)}, u32[]{:S(2)}, u32[]{:S(2)}) collective-permute-start(bf16[256,1536]{1,0:T(8,128)(2,1)} %get-tuple-element.76.refs_1_), channel_id=1, source_target_pairs={{0,4},{1,5},{2,6},{3,7},{4,0},{5,1},{6,2},{7,3}} | collective-permute-start | bytes 2359304 | tf_op jit(solution)/shard_map/ppermute | solution.py:257
  125.4 69.0 %collective-permute-start.10 = (bf16[256,1536]{1,0:T(8,128)(2,1)}, bf16[256,1536]{1,0:T(8,128)(2,1)S(1)}, u32[]{:S(2)}, u32[]{:S(2)}) collective-permute-start(bf16[256,1536]{1,0:T(8,128)(2,1)} %collective-permute-done.5.refs_2_), channel_id=1, source_target_pairs={{0,2},{1,3},{2,0},{3,1},{4,6},{5,7},{6,4},{7,5}} | collective-permute-start | bytes 2359304 | tf_op jit(solution)/shard_map/ppermute | solution.py:257
  125.9 68.5 %collective-permute-start.11 = (bf16[256,1536]{1,0:T(8,128)(2,1)S(1)}, bf16[256,1536]{1,0:T(8,128)(2,1)}, u32[]{:S(2)}, u32[]{:S(2)}) collective-permute-start(bf16[256,1536]{1,0:T(8,128)(2,1)S(1)} %collective-permute-done.4.refs_1_), channel_id=1, source_target_pairs={{0,4},{1,5},{2,6},{3,7},{4,0},{5,1},{6,2},{7,3}} | collective-permute-start | bytes 2359304 | tf_op jit(solution)/shard_map/ppermute | solution.py:257
  194.4 0.9 copy-start.16
  195.3 66.3 %copy-start.9 = (f32[256,1536]{1,0:T(8,128)S(1)}, f32[256,1536]{1,0:T(8,128)}, u32[]{:S(2)}) copy-start(f32[256,1536]{1,0:T(8,128)} %get-tuple-element.47) | copy-start | bytes 4718596
  224.1 37.5 %collective-permute-start.16 = (f32[256,1536]{1,0:T(8,128)}, f32[256,1536]{1,0:T(8,128)S(1)}, u32[]{:S(2)}, u32[]{:S(2)}) collective-permute-start(f32[256,1536]{1,0:T(8,128)} %get-tuple-element.50), channel_id=1, source_target_pairs={{0,2},{1,3},{2,0},{3,1},{4,6},{5,7},{6,4},{7,5}} | collective-permute-start | bytes 4718600 | tf_op jit(solution)/shard_map/ppermute | solution.py:257
  224.8 37.8 %copy-start.14 = (f32[256,1536]{1,0:T(8,128)S(1)}, f32[256,1536]{1,0:T(8,128)}, u32[]{:S(2)}) copy-start(f32[256,1536]{1,0:T(8,128)} %get-tuple-element.52) | copy-start | bytes 4718596
  224.8 39.1 %copy-start.8 = (f32[256,1536]{1,0:T(8,128)S(1)}, f32[256,1536]{1,0:T(8,128)}, u32[]{:S(2)}) copy-start(f32[256,1536]{1,0:T(8,128)} %get-tuple-element.53) | copy-start | bytes 4718596
  224.8 39.1 %collective-permute-start.19 = (f32[256,1536]{1,0:T(8,128)}, f32[256,1536]{1,0:T(8,128)S(1)}, u32[]{:S(2)}, u32[]{:S(2)}) collective-permute-start(f32[256,1536]{1,0:T(8,128)} %get-tuple-element.54), channel_id=1, source_target_pairs={{0,4},{1,5},{2,6},{3,7},{4,0},{5,1},{6,2},{7,3}} | collective-permute-start | bytes 4718600 | tf_op jit(solution)/shard_map/ppermute | solution.py:257
  226.4 68.8 %collective-permute-start.14 = (f32[256,1536]{1,0:T(8,128)}, f32[256,1536]{1,0:T(8,128)S(1)}, u32[]{:S(2)}, u32[]{:S(2)}) collective-permute-start(f32[256,1536]{1,0:T(8,128)} %get-tuple-element.46), channel_id=1, source_target_pairs={{0,2},{1,3},{2,0},{3,1},{4,6},{5,7},{6,4},{7,5}} | collective-permute-start | bytes 4718600 | tf_op jit(solution)/shard_map/ppermute | solution.py:257
  261.8 37.3 %copy-start.7 = (f32[256,1536]{1,0:T(8,128)S(1)}, f32[256,1536]{1,0:T(8,128)}, u32[]{:S(2)}) copy-start(f32[256,1536]{1,0:T(8,128)} %get-tuple-element.37) | copy-start | bytes 4718596
  261.8 37.3 %collective-permute-start.17 = (f32[256,1536]{1,0:T(8,128)S(1)}, f32[256,1536]{1,0:T(8,128)S(1)}, u32[]{:S(2)}, u32[]{:S(2)}) collective-permute-start(f32[256,1536]{1,0:T(8,128)S(1)} %add.103), channel_id=1, source_target_pairs={{0,4},{1,5},{2,6},{3,7},{4,0},{5,1},{6,2},{7,3}} | collective-permute-start | bytes 4718600 | tf_op jit(solution)/shard_map/ppermute | solution.py:257
  262.5 63.0 %collective-permute-start.18 = (f32[256,1536]{1,0:T(8,128)S(1)}, f32[256,1536]{1,0:T(8,128)S(1)}, u32[]{:S(2)}, u32[]{:S(2)}) collective-permute-start(f32[256,1536]{1,0:T(8,128)S(1)} %copy-done.14), channel_id=1, source_target_pairs={{0,4},{1,5},{2,6},{3,7},{4,0},{5,1},{6,2},{7,3}} | collective-permute-start | bytes 4718600 | tf_op jit(solution)/shard_map/ppermute | solution.py:257
  264.1 61.4 %copy-start.6 = (f32[256,1536]{1,0:T(8,128)S(1)}, f32[256,1536]{1,0:T(8,128)}, u32[]{:S(2)}) copy-start(f32[256,1536]{1,0:T(8,128)} %get-tuple-element.51) | copy-start | bytes 4718596
  264.1 61.4 %collective-permute-start.20 = (f32[256,1536]{1,0:T(8,128)S(1)}, f32[256,1536]{1,0:T(8,128)S(1)}, u32[]{:S(2)}, u32[]{:S(2)}) collective-permute-start(f32[256,1536]{1,0:T(8,128)S(1)} %add.106), channel_id=1, source_target_pairs={{0,2},{1,3},{2,0},{3,1},{4,6},{5,7},{6,4},{7,5}} | collective-permute-start | bytes 4718600 | tf_op jit(solution)/shard_map/ppermute | solution.py:257
  325.9 1.6 copy-start.1

commit v2 on v1

v2 whole, which is shorter than its diff:
```python
import functools

import jax
import jax.numpy as jnp
from jax import lax
from jax.experimental import pallas as pl
from jax.experimental.layout import Layout, with_layout_constraint
from jax.experimental.pallas import tpu as pltpu
from jax.sharding import PartitionSpec as P


ROPE_BASE = 1000000.0
NORM_EPS = 1e-6
PIECE = 128
SORTED = 640
ROOM = 768
CHUNKS = 2


def norm_scale(values, gain_vec):
    return values * lax.rsqrt(jnp.mean(values * values, axis=-1, keepdims=True) + NORM_EPS) * gain_vec.astype(jnp.float32)


def attend_kernel(len_ref, cos_ref, sin_ref, qn_ref, kn_ref, q_ref, k_ref, v_ref, kc_ref, vc_ref, ko_ref, vo_ref, o_ref, part_ref, p_ref):
    n_rep = q_ref.shape[0]
    n_slots = kc_ref.shape[0]
    n_batch = q_ref.shape[2]
    unroll = 4

    def norm_rope(values, gain, cosine, sine):
        ms = jnp.mean(values * values, axis=0, keepdims=True)
        values = values * lax.rsqrt(ms + NORM_EPS) * gain
        half = values.shape[0] // 2
        lo, hi = values[:half], values[half:]
        return jnp.concatenate([lo * cosine - hi * sine, hi * cosine + lo * sine], axis=0).astype(jnp.bfloat16)

    for bt in range(n_batch // 128):
        lanes = pl.ds(bt * 128, 128)
        cosine, sine = cos_ref[:, lanes], sin_ref[:, lanes]
        lens = len_ref[:, lanes]
        left0 = jnp.broadcast_to(lens.astype(jnp.float32), (16, 128)).astype(jnp.bfloat16)
        k_new = norm_rope(k_ref[0, :, lanes], kn_ref[...], cosine, sine).reshape(4, 16, 128)
        v_new = v_ref[0, :, lanes].reshape(4, 16, 128)
        qs = [norm_rope(q_ref[r, :, lanes], qn_ref[...], cosine, sine).astype(jnp.float32).reshape(8, 8, 128) for r in range(n_rep)]

        def k_step(i, left):
            for u in range(unroll):
                s = i * unroll + u
                tile = jnp.where((left == 0)[None], k_new, kc_ref[s, 0, :, :, lanes])
                ko_ref[s, 0, :, :, lanes] = tile
                wide = tile.astype(jnp.float32).reshape(8, 8, 128)
                for r in range(n_rep):
                    part_ref[r, pl.ds(pl.multiple_of(s * 8, 8), 8), :] = jnp.sum(wide * qs[r], axis=0)
                left = left - jnp.ones_like(left)
            return left

        lax.fori_loop(0, n_slots // unroll, k_step, left0)
        seen = lax.broadcasted_iota(jnp.int32, (n_slots, 128), 0) <= lens
        for r in range(n_rep):
            scores = part_ref[r, pl.ds(0, n_slots, stride=8), :]
            for sub in range(1, 8):
                scores = scores + part_ref[r, pl.ds(sub, n_slots, stride=8), :]
            scores = jnp.where(seen, scores * (q_ref.shape[1] ** -0.5), -1e30)
            expd = jnp.exp(scores - jnp.max(scores, axis=0, keepdims=True))
            prob = expd / jnp.sum(expd, axis=0, keepdims=True)
            p_ref[r] = prob.astype(jnp.bfloat16).astype(jnp.float32)

        def v_step(i, carry):
            left, accs = carry
            for u in range(unroll):
                s = i * unroll + u
                tile = jnp.where((left == 0)[None], v_new, vc_ref[s, 0, :, :, lanes])
                vo_ref[s, 0, :, :, lanes] = tile
                wide = tile.astype(jnp.float32).reshape(8, 8, 128)
                accs = tuple(accs[r] + wide * p_ref[r, pl.ds(s, 1), :][None] for r in range(n_rep))
                left = left - jnp.ones_like(left)
            return left, accs

        zero = jnp.zeros((8, 8, 128), jnp.float32)
        _, accs = lax.fori_loop(0, n_slots // unroll, v_step, (left0, (zero,) * n_rep))
        for r in range(n_rep):
            o_ref[r, :, lanes] = accs[r].reshape(64, 128).astype(jnp.bfloat16)


def project(x_in, cache_len, ln_attn, w_q, w_k, w_v, head_dim):
    n_batch = x_in.shape[0]
    normed = norm_scale(x_in.astype(jnp.float32), ln_attn).astype(jnp.bfloat16)

    def proj(w):
        out = with_layout_constraint(jnp.dot(normed, w, preferred_element_type=jnp.float32), Layout(major_to_minor=(1, 0)))
        return out.T.reshape(-1, head_dim, n_batch)

    freq = ROPE_BASE ** (-jnp.arange(head_dim // 2, dtype=jnp.float32) * 2.0 / head_dim)
    angles = freq[:, None] * cache_len.astype(jnp.float32)[None, :]
    return proj(w_q), proj(w_k), proj(w_v).astype(jnp.bfloat16), jnp.cos(angles), jnp.sin(angles)


def attend(chunk, n_chunks, q_t, k_t, v_t, cosine, sine, len_row, q_gain, k_gain, k_cache, v_cache, done):
    n_slots, kv_heads, _, _, n_all = k_cache.shape
    head_dim = q_t.shape[1]
    n_batch = n_all // n_chunks
    n_rep = q_t.shape[0] // kv_heads
    full = lambda *shape: pl.BlockSpec(shape, lambda g: (0,) * len(shape))
    lane = lambda n: pl.BlockSpec((n, n_batch), lambda g: (0, chunk))
    cache_spec = pl.BlockSpec((n_slots, 1, 4, 16, n_batch), lambda g: (0, g, 0, 0, chunk))
    head_spec = lambda n: pl.BlockSpec((n, head_dim, n_batch), lambda g: (g, 0, chunk))
    out_spec = pl.BlockSpec((n_rep, head_dim, n_batch), lambda g: (g, 0, 0))
    cache_shape = jax.ShapeDtypeStruct(k_cache.shape, jnp.bfloat16)
    n_done = len(done)

    def body(*refs):
        attend_kernel(*refs[n_done:])

    return pl.pallas_call(
        body,
        grid=(kv_heads,),
        in_specs=[pl.BlockSpec(memory_space=pl.ANY)] * n_done + [lane(1), lane(head_dim // 2), lane(head_dim // 2), full(head_dim, 1), full(head_dim, 1),
                  head_spec(n_rep), head_spec(1), head_spec(1), cache_spec, cache_spec],
        out_specs=[cache_spec, cache_spec, out_spec],
        out_shape=[cache_shape, cache_shape, jax.ShapeDtypeStruct((q_t.shape[0], head_dim, n_batch), jnp.bfloat16)],
        input_output_aliases={i: i for i in range(n_done)},
        scratch_shapes=[pltpu.VMEM((n_rep, n_slots * 8, 128), jnp.float32), pltpu.VMEM((n_rep, n_slots, 128), jnp.float32)],
        compiler_params=pltpu.CompilerParams(dimension_semantics=("arbitrary",), vmem_limit_bytes=40 * 2**20),
        cost_estimate=pl.CostEstimate(flops=30_000_000_000, bytes_accessed=70_000_000, transcendentals=0),
        name="attend",
    )(*done, len_row, cosine, sine, q_gain, k_gain, q_t, k_t, v_t, k_cache, v_cache)


def expert_kernel(n_sub, e_local, dev_ref, start_ref, count_ref, prow_ref, *refs):
    r_refs = refs[:2 * n_sub]
    h_refs = refs[2 * n_sub:4 * n_sub]
    w_refs = refs[4 * n_sub:4 * n_sub + 6]
    o_refs = refs[4 * n_sub + 6:8 * n_sub + 6]
    xs_ref, ys_ref, wg_ref, wu_ref, wd_ref, sem = refs[8 * n_sub + 6:]
    bufs = (wg_ref, wu_ref, wd_ref)
    ring = wg_ref.shape[0]
    step = pl.program_id(0)
    steps = 2 * e_local
    src = step // e_local
    half, hidden = h_refs[0].shape

    def copy(e, k, first):
        source = w_refs[k].at[e] if first else w_refs[3 + k].at[e - e_local]
        return pltpu.make_async_copy(source, bufs[k].at[lax.rem(e, ring)], sem.at[lax.rem(e, ring), k])

    def fetch(e):
        for first in (True, False):
            @pl.when((e < e_local) if first else ((e >= e_local) & (e < steps)))
            def _(first=first):
                for k in range(3):
                    copy(e, k, first).start()

    @pl.when(step == 0)
    def _():
        for e in range(ring - 1):
            fetch(jnp.int32(e))
        ys_ref[...] = jnp.zeros_like(ys_ref)
        for j in range(n_sub):
            xs_ref[j, SORTED:, :] = jnp.zeros((ROOM - SORTED, hidden), jnp.bfloat16)

    fetch(step + ring - 1)

    @pl.when(step % e_local == 0)
    def _():
        for j in range(n_sub):
            prow = prow_ref[pl.ds(2 * j + src, 1), :]
            for c in range(SORTED // PIECE):
                seat = lax.broadcasted_iota(jnp.int32, (PIECE, 2 * half), 0) + c * PIECE
                hot = jnp.where(seat == prow, 1.0, 0.0).astype(jnp.bfloat16)
                rows = jnp.dot(hot[:, :half], h_refs[2 * j][...], preferred_element_type=jnp.float32)
                rows = rows + jnp.dot(hot[:, half:], h_refs[2 * j + 1][...], preferred_element_type=jnp.float32)
                xs_ref[j, c * PIECE:(c + 1) * PIECE, :] = rows.astype(jnp.bfloat16)

    slot = lax.rem(step, ring)
    for k in range(3):
        pltpu.make_async_copy(w_refs[k].at[0], bufs[k].at[slot], sem.at[slot, k]).wait()
    counts = [count_ref[j * steps + step] for j in range(n_sub)]

    def piece(c, carry):
        offs = [pl.multiple_of(jnp.minimum(start_ref[j * steps + step] + c * PIECE, SORTED), 16) for j in range(n_sub)]
        rows = jnp.concatenate([xs_ref[j, pl.ds(offs[j], PIECE), :] for j in range(n_sub)], axis=0)
        gate = jnp.dot(rows, wg_ref[slot], preferred_element_type=jnp.float32)
        up = jnp.dot(rows, wu_ref[slot], preferred_element_type=jnp.float32)
        act = (jax.nn.silu(gate) * up).astype(jnp.bfloat16)
        out = jnp.dot(act, wd_ref[slot], preferred_element_type=jnp.float32).astype(jnp.bfloat16)
        for j in range(n_sub):
            @pl.when(c < counts[j])
            def _(j=j):
                ys_ref[j, pl.ds(offs[j], PIECE), :] = out[j * PIECE:(j + 1) * PIECE]
        return carry

    lax.fori_loop(0, functools.reduce(jnp.maximum, counts), piece, 0)

    def column(row):
        return jnp.broadcast_to(row, (128, row.shape[1])).T

    def back(which):
        dev = dev_ref[which]
        for j in range(n_sub):
            seat_col = column(prow_ref[pl.ds(2 * j + which, 1), :].astype(jnp.float32))
            for i in range(2):
                r_col = column(r_refs[2 * j + i][pl.ds(dev, 1), :])
                for c in range(half // PIECE):
                    at = seat_col[i * half + c * PIECE:i * half + (c + 1) * PIECE]
                    lane = lax.broadcasted_iota(jnp.int32, (PIECE, 128), 1).astype(jnp.float32)
                    hot = jnp.concatenate([jnp.where(at == lane + t * 128.0, 1.0, 0.0).astype(jnp.bfloat16) for t in range(SORTED // 128)], axis=1)
                    r_rows = r_col[c * PIECE:(c + 1) * PIECE]
                    mine = jnp.dot(hot, ys_ref[j, :SORTED, :], preferred_element_type=jnp.float32) * jnp.concatenate([r_rows] * (hidden // 128), axis=1)
                    o_ref = o_refs[4 * j + 2 * i + c]
                    o_ref[...] = mine if which == 0 else o_ref[...] + mine

    @pl.when(step == e_local - 1)
    def _():
        back(0)

    @pl.when(step == steps - 1)
    def _():
        back(1)


def experts(blocks, r_blocks, devs, starts, counts, seat, w_own, w_par):
    n_sub = len(blocks) // 2
    half, hidden = blocks[0].shape
    e_local, _, ff = w_own[0].shape
    ring = 4
    once = pl.Buffered(1)
    full = lambda *shape: pl.BlockSpec(shape, lambda e, *_: (0,) * len(shape), pipeline_mode=once)
    out = pl.pallas_call(
        functools.partial(expert_kernel, n_sub, e_local),
        grid_spec=pltpu.PrefetchScalarGridSpec(
            num_scalar_prefetch=3,
            grid=(2 * e_local,),
            in_specs=[full(2 * n_sub, 2 * half)] + [full(*r.shape) for r in r_blocks] + [full(half, hidden)] * (2 * n_sub)
            + [pl.BlockSpec(memory_space=pl.ANY)] * 6,
            out_specs=[full(PIECE, hidden)] * (4 * n_sub),
            scratch_shapes=[pltpu.VMEM((n_sub, ROOM, hidden), jnp.bfloat16)] * 2
            + [pltpu.VMEM((ring, hidden, ff), jnp.bfloat16)] * 2 + [pltpu.VMEM((ring, ff, hidden), jnp.bfloat16), pltpu.SemaphoreType.DMA((ring, 3))],
        ),
        out_shape=[jax.ShapeDtypeStruct((PIECE, hidden), jnp.float32)] * (4 * n_sub),
        compiler_params=pltpu.CompilerParams(dimension_semantics=("arbitrary",), vmem_limit_bytes=58 * 2**20),
        cost_estimate=pl.CostEstimate(flops=n_sub * 16_000_000_000, bytes_accessed=60_000_000, transcendentals=0),
        name="experts",
    )(devs, starts.reshape(-1), counts.reshape(-1), seat.reshape(2 * n_sub, 2 * half), *r_blocks, *blocks, *w_own, *w_par)
    return [(out[2 * i], out[2 * i + 1]) for i in range(2 * n_sub)]


def seats(topk_blocks, me, e_local):
    n_rows = topk_blocks.shape[1]
    dev = topk_blocks // e_local
    loc = topk_blocks % e_local
    both = jnp.stack([me, me ^ 1])
    loc_src = jnp.sum(jnp.where(dev[:, None] == both[None, :, None, None], loc[:, None], 0), axis=-1)
    hot = (loc_src[:, :, None, :] == jnp.arange(e_local)[None, None, :, None])
    before = (jnp.arange(n_rows)[:, None] < jnp.arange(n_rows)[None, :]).astype(jnp.bfloat16)
    rank = lax.dot_general(hot.astype(jnp.bfloat16), before, (((3,), (0,)), ((), ())), preferred_element_type=jnp.float32).astype(jnp.int32)
    count = jnp.sum(hot.astype(jnp.int32), axis=-1)
    padded = (count + 15) // 16 * 16
    starts = [jnp.zeros_like(count[..., 0])]
    for e in range(1, e_local):
        starts.append(starts[-1] + padded[..., e - 1])
    start = jnp.stack(starts, axis=-1)
    seat = jnp.sum(jnp.where(hot, start[..., None] + rank, 0), axis=2)
    return seat, start, (count + PIECE - 1) // PIECE


def solution(mesh):
    ep_size = mesh.shape['ep']
    row_spec = P(('dp', 'ep'))
    replicated = P()
    expert_spec = P('ep')
    in_specs = (row_spec, row_spec, row_spec, row_spec, row_spec, replicated, replicated, replicated, replicated, replicated, replicated, replicated, replicated, replicated, expert_spec, expert_spec, expert_spec)
    out_specs = (row_spec, row_spec, row_spec)

    def swap(value, bit):
        return lax.ppermute(value, 'ep', [(i, i ^ bit) for i in range(ep_size)])

    def device_step(x_in, k_cache, v_cache, cache_len, topk_idx, ln_attn, w_q, w_k, w_v, q_norm, k_norm, w_o, ln_moe, w_router, w_gate, w_up, w_down):
        me = lax.axis_index('ep')
        e_local = w_gate.shape[0]
        n_batch, n_slots, kv_heads, head_dim = k_cache.shape
        n_rows = n_batch // CHUNKS
        top_k = topk_idx.shape[1]
        w_own = (w_gate, w_up, w_down)
        w_par = tuple(swap(w, 1) for w in w_own)
        blocks = jnp.stack([topk_idx, swap(topk_idx, 2), swap(topk_idx, 4), swap(topk_idx, 6)])
        blocks = blocks.reshape(2, 2, CHUNKS, n_rows, top_k).transpose(2, 0, 1, 3, 4).reshape(2 * CHUNKS, 2 * n_rows, top_k)
        seat, start, count = seats(blocks, me, e_local)
        devs = jnp.stack([me, me ^ 1]).astype(jnp.int32)

        q_t, k_t, v_t, cosine, sine = project(x_in, cache_len, ln_attn, w_q, w_k, w_v, head_dim)
        by_slot = lambda c: c.transpose(1, 2, 3, 0).reshape(n_slots, kv_heads, 4, 16, n_batch)
        k_slots, v_slots = by_slot(k_cache), by_slot(v_cache)
        gains = (q_norm.astype(jnp.float32)[:, None], k_norm.astype(jnp.float32)[:, None])
        len_row, seat, start, count = lax.optimization_barrier((cache_len[None, :], seat, start, count))

        done, resid, own, far, gates = (), [], [], [], []
        for c in range(CHUNKS):
            if c:
                len_row, own[c - 1] = lax.optimization_barrier((len_row, own[c - 1]))
            k_full, v_full, attn_t = attend(c, CHUNKS, q_t, k_t, v_t, cosine, sine, len_row, *gains, k_slots, v_slots, done)
            done = (k_full, v_full)
            rows = slice(c * n_rows, (c + 1) * n_rows)
            o_proj = lax.dot_general(attn_t.reshape(-1, n_rows), w_o, (((0,), (0,)), ((), ())), preferred_element_type=jnp.float32)
            x_mid = (x_in[rows].astype(jnp.float32) + o_proj).astype(jnp.bfloat16)
            resid.append(x_mid.astype(jnp.float32))
            h_moe = norm_scale(resid[c], ln_moe).astype(jnp.bfloat16)
            own.append(h_moe)
            h_x = swap(h_moe, 2)
            h_y = swap(h_moe, 4)
            h_d = swap(h_moe, 6)
            far.append((h_x, h_y, h_d))

            logits = jnp.dot(h_moe, w_router, preferred_element_type=jnp.float32)
            chosen = jnp.any(topk_idx[rows][:, :, None] == jnp.arange(logits.shape[1])[None, None, :], axis=1)
            top = jnp.max(jnp.where(chosen, logits, -jnp.inf), axis=1, keepdims=True)
            expd = jnp.where(chosen, jnp.exp(jnp.where(chosen, logits - top, 0.0)), 0.0)
            gate = expd / jnp.sum(expd, axis=1, keepdims=True)
            r_dev = jnp.sum(gate.reshape(-1, ep_size, e_local), axis=-1).T
            gates.append((r_dev, swap(r_dev, 2), swap(r_dev, 4), swap(r_dev, 6)))

        sums = []
        for c in range(CHUNKS):
            h_o, h_far = own[c], far[c]
            if c == 0:
                h_o, own[-1] = lax.optimization_barrier((h_o, own[-1]))
            else:
                h_far, sums[c - 1] = lax.optimization_barrier((h_far, sums[c - 1]))
            pick = slice(2 * c, 2 * c + 2)
            s_o, s_x, s_y, s_d = experts([h_o, *h_far], gates[c], devs, start[pick], count[pick], seat[pick], w_own, w_par)
            sums.append((s_o, s_x, s_y, s_d))
        outs = []
        sent = []
        for c in range(CHUNKS):
            s_o, s_x, s_y, s_d = sums[c]
            d_x = swap(s_d[0], 2)
            d_y = swap(s_d[1], 4)
            u_x = swap(s_x[0], 2)
            u_y = swap(s_y[1], 4)
            sent.append((d_x, d_y, u_x, u_y))
        last = sums[-1][0][0]
        for c in range(CHUNKS):
            s_o, s_x, s_y, s_d = sums[c]
            d_x, d_y, u_x, u_y = sent[c]
            if c < CHUNKS - 1:
                d_x, d_y, last = lax.optimization_barrier((d_x, d_y, last))
                sums[-1] = ((last, sums[-1][0][1]), *sums[-1][1:])
            m_x, m_y = swap(s_x[1] + d_y, 2), swap(s_y[0] + d_x, 4)
            outs += [s_o[0] + u_x + m_y, s_o[1] + u_y + m_x]
        x_out = (jnp.concatenate(resid, axis=0) + jnp.concatenate(outs, axis=0)).astype(jnp.bfloat16)
        by_row = lambda c: c.reshape(n_slots, kv_heads, head_dim, n_batch).transpose(3, 0, 1, 2)
        return x_out, by_row(k_full), by_row(v_full)

    return jax.shard_map(device_step, mesh=mesh, in_specs=in_specs, out_specs=out_specs, check_vma=False)
```

time: 328 us -> 349 us (1.064)
  waiting for transfers between devices: 99.8 us -> 129 us
  Pallas kernels: 163 us -> 134 us
  starting transfers between devices: 20.8 us -> 37 us
  local copies, waits for them, and re-layouts: 20.1 us -> 13.9 us
  matrix products: 15.1 us -> 20.8 us
  other arithmetic: 7.76 us -> 12.8 us
    pallas_call x3 -> x2, Pallas kernels: 95.9 us -> 64.2 us  [experts(): pl.pallas_call(functools.partial(expert_kernel, n_sub, e_local), grid_spe...]
    ppermute x21 -> x30, waiting for transfers between devices: 99.8 us -> 129 us  [swap(): return lax.ppermute(value, 'ep', [(i, i ^ bit) for i in range(ep_size)])]
    ppermute x21 -> x30, starting transfers between devices: 20.8 us -> 37 us  [swap(): return lax.ppermute(value, 'ep', [(i, i ^ bit) for i in range(ep_size)])]
    unnamed x38 -> x90, local copies, waits for them, and re-layouts: 1.69 us -> 8.35 us
    reshape x5 -> x2, local copies, waits for them, and re-layouts: 6.48 us -> 1.22 us  [experts(): seat.reshape(2 * n_sub, 2 * half)]
    transpose x1 -> x0, local copies, waits for them, and re-layouts: 3.74 us -> none  [proj(): jnp.dot(normed, w, preferred_element_type=jnp.float32)]
    pallas_call x1 -> x2, Pallas kernels: 67 us -> 69.5 us  [attend(): pl.pallas_call(body, grid=(kv_heads,), in_specs=[pl.BlockSpec(memory_spac...]
    dot_general x1 -> x2, matrix products: 5.25 us -> 7.75 us  [device_step(): lax.dot_general(attn_t.reshape(-1, n_rows), w_o, (((0,), (0,)), ((), ()))...]
  transfers between devices with their start and end apart: 21 -> 30, of which waited for: 8 -> 10; matrix products, arithmetic and copies ran while one was open for 12% -> 11% of each run, Pallas kernels for 41% -> 29%
where the time goes in v2:
time: 349 us
  Pallas kernels  134 us (38%)
  waiting for transfers between devices  129 us (37%)
  starting transfers between devices  37 us (11%)
  matrix products  20.8 us (6%)
  local copies, waits for them, and re-layouts  13.9 us (4%)
  other arithmetic  12.8 us (4%)
    ppermute x30, waiting for transfers between devices, swap(): return lax.ppermute(value, 'ep', [(i, i ^ bit) for i in range(ep_size)])  129 us
    pallas_call x2, Pallas kernels, attend(): pl.pallas_call(body, grid=(kv_heads,), in_specs=[pl.BlockSpec(memory_spac...  69.5 us
    pallas_call x2, Pallas kernels, experts(): pl.pallas_call(functools.partial(expert_kernel, n_sub, e_local), grid_spe...  64.2 us
    ppermute x30, starting transfers between devices, swap(): return lax.ppermute(value, 'ep', [(i, i ^ bit) for i in range(ep_size)])  37 us
    dot_general x3, matrix products, proj(): jnp.dot(normed, w, preferred_element_type=jnp.float32)  11.5 us
    unnamed x90, local copies, waits for them, and re-layouts  8.35 us
    dot_general x2, matrix products, device_step(): lax.dot_general(attn_t.reshape(-1, n_rows), w_o, (((0,), (0,)), ((), ()))...  7.75 us
  transfers between devices with their start and end apart: 30, of which 10 were waited for; matrix products, arithmetic and copies ran while one was open for 11% of the time, Pallas kernels for 29%

profile of v2, /device:TPU:0, one launch (start us, length us, event | category | flops | bytes accessed | tf_op | source)
XLA Modules:
  0.0 348.7 jit_solution(1588766340809426533)
XLA Ops:
  0.6 4.3 %collective-permute-start.2 = (s32[512,8]{0,1:T(8,128)}, s32[512,8]{0,1:T(8,128)S(1)}, u32[]{:S(2)}, u32[]{:S(2)}) collective-permute-start(s32[512,8]{0,1:T(8,128)} %param.21), channel_id=1, source_target_pairs={{0,6},{1,7},{2,4},{3,5},{4,2},{5,3},{6,0},{7,1}} | collective-permute-start | bytes 49160 | tf_op jit(solution)/shard_map/ppermute | solution.py:275
  9.5 1.8 fusion
  11.3 7.3 %fusion.24 = f32[512,1536]{0,1:T(8,128)} fusion(bf16[1536,1536]{1,0:T(8,128)(2,1)} %param.23, bf16[512,1536]{1,0:T(8,128)(2,1)} %param.17, f32[1536]{0:T(1024)S(1)} %convert_element_type.65, f32[512]{0:T(512)S(1)} %add_rsqrt_fusion), kind=kOutput, calls=%fused_computation.73 | convolution fusion | flops 2419064832 | bytes 9445376 | tf_op jit(solution)/shard_map/dot_general | solution.py:90
  18.6 2.2 fusion.22
  20.8 2.0 convolution_convert_fusion
  24.9 0.9 fusion.10
  25.8 1.2 copy-done.3
  27.0 1.0 copy-done.5
  28.1 34.8 %attend.2 = (bf16[64,8,4,16,512]{4,3,2,1,0:T(8,128)(2,1)}, bf16[64,8,4,16,512]{4,3,2,1,0:T(8,128)(2,1)}, bf16[24,64,256]{2,1,0:T(8,128)(2,1)S(1)}) custom-call(s32[1,512]{1,0:T(1,128)S(1)} %bitcast.78, f32[32,512]{1,0:T(8,128)S(1)} %get-tuple-element.110.refs_1_.refs_3_, f32[32,512]{1,0:T(8,128)S(1)} %get-tuple-element.109.refs_2_.refs_4_, ...), custom_call_target="tpu_custom_call" | custom-call | flops 30000001024 | bytes 70000000 | tf_op jit(solution)/shard_map/attend/pallas_call | solution.py:114
  62.8 3.9 %multiply_reduce_fusion.1 = (f32[256]{0:T(256)S(1)}, f32[256,1536]{1,0:T(8,128)S(1)}) fusion(bf16[1536,256]{1,0:T(8,128)(2,1)S(1)} %bitcast.73, bf16[1536,1536]{1,0:T(8,128)(2,1)} %param.28, bf16[512,1536]{1,0:T(8,128)(2,1)S(1)} %copy-done.11), kind=kOutput, calls=%fused_computation.16 | convolution fusion | flops 1210318592 | bytes 7865344 | tf_op jit(solution)/shard_map/dot_general | solution.py:303
  66.7 1.1 copy-done.8
  68.1 0.9 copy-done.13
  70.0 0.8 reshape.148
  71.4 1.9 collective-permute-start.6
  73.3 1.5 collective-permute-start.7
  74.9 1.2 copy-done.4
  76.1 1.0 copy-done.6
  77.1 34.8 %attend.3 = (bf16[64,8,4,16,512]{4,3,2,1,0:T(8,128)(2,1)}, bf16[64,8,4,16,512]{4,3,2,1,0:T(8,128)(2,1)}, bf16[24,64,256]{2,1,0:T(8,128)(2,1)S(1)}) custom-call(bf16[64,8,4,16,512]{4,3,2,1,0:T(8,128)(2,1)} %get-tuple-element.49.refs_0_, bf16[64,8,4,16,512]{4,3,2,1,0:T(8,128)(2,1)} %get-tuple-element.50.refs_1_, ...), custom_call_target="tpu_custom_call", output_to_operand_aliasing={{0}: (0, {}), {1}: (1, {})} | custom-call | flops 30000001024 | bytes 70000000 | tf_op jit(solution)/shard_map/attend/pallas_call | solution.py:114
  111.9 3.9 %multiply_reduce_fusion = (f32[256]{0:T(256)S(1)}, f32[256,1536]{1,0:T(8,128)S(1)}) fusion(bf16[1536,256]{1,0:T(8,128)(2,1)S(1)} %bitcast.72, bf16[1536,1536]{1,0:T(8,128)(2,1)} %param.28, bf16[512,1536]{1,0:T(8,128)(2,1)S(1)} %copy-done.12), kind=kOutput, calls=%fused_computation.14 | convolution fusion | flops 1210318592 | bytes 7865344 | tf_op jit(solution)/shard_map/dot_general | solution.py:303
  116.2 2.0 collective-permute-start.3
  118.1 2.4 collective-permute-done.8.refs_3_
  122.2 14.4 %collective-permute-done.3.refs_5_ = bf16[256,1536]{1,0:T(8,128)(2,1)} collective-permute-done((bf16[256,1536]{1,0:T(8,128)(2,1)S(1)}, bf16[256,1536]{1,0:T(8,128)(2,1)}, u32[]{:S(2)}, u32[]{:S(2)}) %collective-permute-start.3) | collective-permute-done | bytes 786464 | tf_op jit(solution)/shard_map/ppermute | solution.py:275
  136.7 2.0 collective-permute-start.10
  138.7 13.9 %collective-permute-done.9.refs_5_ = bf16[256,1536]{1,0:T(8,128)(2,1)} collective-permute-done((bf16[256,1536]{1,0:T(8,128)(2,1)S(1)}, bf16[256,1536]{1,0:T(8,128)(2,1)}, u32[]{:S(2)}, u32[]{:S(2)}) %collective-permute-start.9) | collective-permute-done | bytes 786464 | tf_op jit(solution)/shard_map/ppermute | solution.py:275
  152.6 2.5 collective-permute-start.11
  158.7 13.6 %collective-permute-done.11.refs_7_ = bf16[256,1536]{1,0:T(8,128)(2,1)} collective-permute-done((bf16[256,1536]{1,0:T(8,128)(2,1)S(1)}, bf16[256,1536]{1,0:T(8,128)(2,1)}, u32[]{:S(2)}, u32[]{:S(2)}) %collective-permute-start.11) | collective-permute-done | bytes 786464 | tf_op jit(solution)/shard_map/ppermute | solution.py:275
  172.2 1.4 collective-permute-start.19
  173.7 1.3 collective-permute-start.20
  174.9 1.5 collective-permute-start.4
  177.2 32.1 %experts.2 = (f32[128,1536]{1,0:T(8,128)}, f32[128,1536]{1,0:T(8,128)}, f32[128,1536]{1,0:T(8,128)}, f32[128,1536]{1,0:T(8,128)}, f32[128,1536]{1,0:T(8,128)}, /...) custom-call(s32[2]{0:T(128)} %copy-done.31, s32[20]{0:T(128)} %reshape.145.start_ref, ...), custom_call_target="tpu_custom_call" | custom-call | flops 32000000000 | bytes 60000000 | tf_op jit(solution)/shard_map/experts/pallas_call | solution.py:228
  209.4 0.8 copy-done.37
  211.1 32.1 %experts.3 = (f32[128,1536]{1,0:T(8,128)}, f32[128,1536]{1,0:T(8,128)}, f32[128,1536]{1,0:T(8,128)}, f32[128,1536]{1,0:T(8,128)}, f32[128,1536]{1,0:T(8,128)}, /...) custom-call(s32[2]{0:T(128)} %copy-done.31, s32[20]{0:T(128)} %reshape.149.start_ref, ...), custom_call_target="tpu_custom_call" | custom-call | flops 32000000000 | bytes 60000000 | tf_op jit(solution)/shard_map/experts/pallas_call | solution.py:228
  243.3 1.5 collective-permute-start.28
  244.7 2.8 collective-permute-start.25
  247.6 2.0 collective-permute-start.27
  249.6 14.3 %collective-permute-done.28 = f32[128,1536]{1,0:T(8,128)S(1)} collective-permute-done((f32[128,1536]{1,0:T(8,128)}, f32[128,1536]{1,0:T(8,128)S(1)}, u32[]{:S(2)}, u32[]{:S(2)}) %collective-permute-start.28) | collective-permute-done | bytes 786464 | tf_op jit(solution)/shard_map/ppermute | solution.py:275
  263.9 1.3 add.147
  265.2 2.3 collective-permute-start.29
  268.2 1.3 add.144
  269.5 13.5 %collective-permute-done.16 = f32[128,1536]{1,0:T(8,128)S(1)} collective-permute-done((f32[128,1536]{1,0:T(8,128)S(1)}, f32[128,1536]{1,0:T(8,128)S(1)}, u32[]{:S(2)}, u32[]{:S(2)}) %collective-permute-start.16) | collective-permute-done | bytes 786464 | tf_op jit(solution)/shard_map/ppermute | solution.py:275
  283.0 2.0 collective-permute-start.22
  285.3 12.3 %collective-permute-done.27 = f32[128,1536]{1,0:T(8,128)S(1)} collective-permute-done((f32[128,1536]{1,0:T(8,128)}, f32[128,1536]{1,0:T(8,128)S(1)}, u32[]{:S(2)}, u32[]{:S(2)}) %collective-permute-start.27) | collective-permute-done | bytes 786464 | tf_op jit(solution)/shard_map/ppermute | solution.py:275
  297.6 2.3 collective-permute-start.15
  299.9 2.0 collective-permute-start.23
  302.0 14.7 %collective-permute-done.24 = f32[128,1536]{1,0:T(8,128)S(1)} collective-permute-done((f32[128,1536]{1,0:T(8,128)}, f32[128,1536]{1,0:T(8,128)S(1)}, u32[]{:S(2)}, u32[]{:S(2)}) %collective-permute-start.24) | collective-permute-done | bytes 786464 | tf_op jit(solution)/shard_map/ppermute | solution.py:275
  316.9 14.4 %collective-permute-done.22 = f32[128,1536]{1,0:T(8,128)S(1)} collective-permute-done((f32[128,1536]{1,0:T(8,128)S(1)}, f32[128,1536]{1,0:T(8,128)S(1)}, u32[]{:S(2)}, u32[]{:S(2)}) %collective-permute-start.22) | collective-permute-done | bytes 786464 | tf_op jit(solution)/shard_map/ppermute | solution.py:275
  331.3 15.5 %collective-permute-done.23 = f32[128,1536]{1,0:T(8,128)S(1)} collective-permute-done((f32[128,1536]{1,0:T(8,128)S(1)}, f32[128,1536]{1,0:T(8,128)S(1)}, u32[]{:S(2)}, u32[]{:S(2)}) %collective-permute-start.23) | collective-permute-done | bytes 786464 | tf_op jit(solution)/shard_map/ppermute | solution.py:275
  347.1 1.6 fusion.3
  (169 shorter events, 17.2 us)
Async XLA Ops:
  0.6 22.9 %collective-permute-start.2 = (s32[512,8]{0,1:T(8,128)}, s32[512,8]{0,1:T(8,128)S(1)}, u32[]{:S(2)}, u32[]{:S(2)}) collective-permute-start(s32[512,8]{0,1:T(8,128)} %param.21), channel_id=1, source_target_pairs={{0,6},{1,7},{2,4},{3,5},{4,2},{5,3},{6,0},{7,1}} | collective-permute-start | bytes 49160 | tf_op jit(solution)/shard_map/ppermute | solution.py:275
  4.9 18.6 %collective-permute-start.1 = (s32[512,8]{0,1:T(8,128)}, s32[512,8]{0,1:T(8,128)S(1)}, u32[]{:S(2)}, u32[]{:S(2)}) collective-permute-start(s32[512,8]{0,1:T(8,128)} %param.21), channel_id=1, source_target_pairs={{0,4},{1,5},{2,6},{3,7},{4,0},{5,1},{6,2},{7,3}} | collective-permute-start | bytes 49160 | tf_op jit(solution)/shard_map/ppermute | solution.py:275
  5.4 18.2 %collective-permute-start = (s32[512,8]{0,1:T(8,128)}, s32[512,8]{0,1:T(8,128)S(1)}, u32[]{:S(2)}, u32[]{:S(2)}) collective-permute-start(s32[512,8]{0,1:T(8,128)} %param.21), channel_id=1, source_target_pairs={{0,2},{1,3},{2,0},{3,1},{4,6},{5,7},{6,4},{7,5}} | collective-permute-start | bytes 49160 | tf_op jit(solution)/shard_map/ppermute | solution.py:275
  5.5 168.1 %collective-permute-start.12 = (bf16[5,1536,512]{2,1,0:T(8,128)(2,1)}, bf16[5,1536,512]{2,1,0:T(8,128)(2,1)}, u32[]{:S(2)}, u32[]{:S(2)}) collective-permute-start(bf16[5,1536,512]{2,1,0:T(8,128)(2,1)} %refs_8_.3), channel_id=1, source_target_pairs={{0,1},{1,0},{2,3},{3,2},{4,5},{5,4},{6,7},{7,6}} | collective-permute-start | bytes 23592968 | tf_op jit(solution)/shard_map/ppermute | solution.py:275
  5.5 169.4 %collective-permute-start.13 = (bf16[5,1536,512]{2,1,0:T(8,128)(2,1)}, bf16[5,1536,512]{2,1,0:T(8,128)(2,1)}, u32[]{:S(2)}, u32[]{:S(2)}) collective-permute-start(bf16[5,1536,512]{2,1,0:T(8,128)(2,1)} %refs_9_.3), channel_id=1, source_target_pairs={{0,1},{1,0},{2,3},{3,2},{4,5},{5,4},{6,7},{7,6}} | collective-permute-start | bytes 23592968 | tf_op jit(solution)/shard_map/ppermute | solution.py:275
  23.3 39.5 %copy-start.31 = (s32[2]{0:T(128)}, s32[2]{0:T(128)S(1)}, u32[]{:S(2)}) copy-start(s32[2]{0:T(128)S(1)} %pad_add_fusion.1.dev_ref) | copy-start | bytes 28
  23.5 152.9 %collective-permute-start.14 = (bf16[5,512,1536]{2,1,0:T(8,128)(2,1)}, bf16[5,512,1536]{2,1,0:T(8,128)(2,1)}, u32[]{:S(2)}, u32[]{:S(2)}) collective-permute-start(bf16[5,512,1536]{2,1,0:T(8,128)(2,1)} %refs_10_.3), channel_id=1, source_target_pairs={{0,1},{1,0},{2,3},{3,2},{4,5},{5,4},{6,7},{7,6}} | collective-permute-start | bytes 23592968 | tf_op jit(solution)/shard_map/ppermute | solution.py:275
  24.9 37.9 %copy-start.26 = (s32[4,2,5]{2,1,0:T(2,128)}, s32[4,2,5]{2,1,0:T(2,128)S(1)}, u32[]{:S(2)}) copy-start(s32[4,2,5]{2,1,0:T(2,128)S(1)} %stack.41) | copy-start | bytes 484
  28.1 34.8 %copy-start.11 = (bf16[512,1536]{1,0:T(8,128)(2,1)S(1)}, bf16[512,1536]{1,0:T(8,128)(2,1)}, u32[]{:S(2)}) copy-start(bf16[512,1536]{1,0:T(8,128)(2,1)} %param.17) | copy-start | bytes 4718596
  71.4 44.4 %collective-permute-start.6 = (f32[8,256]{1,0:T(8,128)}, f32[8,256]{1,0:T(8,128)S(1)}, u32[]{:S(2)}, u32[]{:S(2)}) collective-permute-start(f32[8,256]{1,0:T(8,128)} %bitcast.100), channel_id=1, source_target_pairs={{0,2},{1,3},{2,0},{3,1},{4,6},{5,7},{6,4},{7,5}} | collective-permute-start | bytes 24584 | tf_op jit(solution)/shard_map/ppermute | solution.py:275
  73.3 42.8 %collective-permute-start.7 = (f32[8,256]{1,0:T(8,128)}, f32[8,256]{1,0:T(8,128)S(1)}, u32[]{:S(2)}, u32[]{:S(2)}) collective-permute-start(f32[8,256]{1,0:T(8,128)} %bitcast.101), channel_id=1, source_target_pairs={{0,4},{1,5},{2,6},{3,7},{4,0},{5,1},{6,2},{7,3}} | collective-permute-start | bytes 24584 | tf_op jit(solution)/shard_map/ppermute | solution.py:275
  77.1 34.8 %copy-start.12 = (bf16[512,1536]{1,0:T(8,128)(2,1)S(1)}, bf16[512,1536]{1,0:T(8,128)(2,1)}, u32[]{:S(2)}) copy-start(bf16[512,1536]{1,0:T(8,128)(2,1)} %param.17) | copy-start | bytes 4718596
  111.9 43.2 %copy-start.24 = (s32[4,2,512]{2,1,0:T(2,128)S(1)}, s32[4,2,512]{2,1,0:T(2,128)}, u32[]{:S(2)}) copy-start(s32[4,2,512]{2,1,0:T(2,128)} %fusion.10) | copy-start | bytes 49156
  115.9 61.3 %copy-start.39 = (f32[8,256]{1,0:T(8,128)}, f32[8,256]{1,0:T(8,128)S(1)}, u32[]{:S(2)}) copy-start(f32[8,256]{1,0:T(8,128)S(1)} %collective-permute-done.6.refs_1_) | copy-start | bytes 24580
  115.9 4.7 %collective-permute-start.8 = (f32[8,256]{1,0:T(8,128)S(1)}, f32[8,256]{1,0:T(8,128)S(1)}, u32[]{:S(2)}, u32[]{:S(2)}) collective-permute-start(f32[8,256]{1,0:T(8,128)S(1)} %bitcast.103), channel_id=1, source_target_pairs={{0,6},{1,7},{2,4},{3,5},{4,2},{5,3},{6,0},{7,1}} | collective-permute-start | bytes 24584 | tf_op jit(solution)/shard_map/ppermute | solution.py:275
  116.1 93.2 %copy-start.15 = (bf16[256,1536]{1,0:T(8,128)(2,1)}, bf16[256,1536]{1,0:T(8,128)(2,1)S(1)}, u32[]{:S(2)}) copy-start(bf16[256,1536]{1,0:T(8,128)(2,1)S(1)} %multiply_convert_fusion.refs_4_) | copy-start | bytes 2359300
  116.1 61.1 %copy-start.40 = (f32[8,256]{1,0:T(8,128)}, f32[8,256]{1,0:T(8,128)S(1)}, u32[]{:S(2)}) copy-start(f32[8,256]{1,0:T(8,128)S(1)} %collective-permute-done.7.refs_2_) | copy-start | bytes 24580
  116.2 20.5 %collective-permute-start.3 = (bf16[256,1536]{1,0:T(8,128)(2,1)S(1)}, bf16[256,1536]{1,0:T(8,128)(2,1)}, u32[]{:S(2)}, u32[]{:S(2)}) collective-permute-start(bf16[256,1536]{1,0:T(8,128)(2,1)S(1)} %multiply_convert_fusion.refs_4_), channel_id=1, source_target_pairs={{0,2},{1,3},{2,0},{3,1},{4,6},{5,7},{6,4},{7,5}} | collective-permute-start | bytes 2359304 | tf_op jit(solution)/shard_map/ppermute | solution.py:275
  120.5 56.7 %copy-start.41 = (f32[8,256]{1,0:T(8,128)}, f32[8,256]{1,0:T(8,128)S(1)}, u32[]{:S(2)}) copy-start(f32[8,256]{1,0:T(8,128)S(1)} %collective-permute-done.8.refs_3_) | copy-start | bytes 24580
  120.5 32.0 %collective-permute-start.9 = (bf16[256,1536]{1,0:T(8,128)(2,1)S(1)}, bf16[256,1536]{1,0:T(8,128)(2,1)}, u32[]{:S(2)}, u32[]{:S(2)}) collective-permute-start(bf16[256,1536]{1,0:T(8,128)(2,1)S(1)} %copy-done.14), channel_id=1, source_target_pairs={{0,2},{1,3},{2,0},{3,1},{4,6},{5,7},{6,4},{7,5}} | collective-permute-start | bytes 2359304 | tf_op jit(solution)/shard_map/ppermute | solution.py:275
  136.7 21.4 %collective-permute-start.10 = (bf16[256,1536]{1,0:T(8,128)(2,1)S(1)}, bf16[256,1536]{1,0:T(8,128)(2,1)}, u32[]{:S(2)}, u32[]{:S(2)}) collective-permute-start(bf16[256,1536]{1,0:T(8,128)(2,1)S(1)} %copy-done.14), channel_id=1, source_target_pairs={{0,4},{1,5},{2,6},{3,7},{4,0},{5,1},{6,2},{7,3}} | collective-permute-start | bytes 2359304 | tf_op jit(solution)/shard_map/ppermute | solution.py:275
  152.6 19.7 %collective-permute-start.11 = (bf16[256,1536]{1,0:T(8,128)(2,1)S(1)}, bf16[256,1536]{1,0:T(8,128)(2,1)}, u32[]{:S(2)}, u32[]{:S(2)}) collective-permute-start(bf16[256,1536]{1,0:T(8,128)(2,1)S(1)} %copy-done.14), channel_id=1, source_target_pairs={{0,6},{1,7},{2,4},{3,5},{4,2},{5,3},{6,0},{7,1}} | collective-permute-start | bytes 2359304 | tf_op jit(solution)/shard_map/ppermute | solution.py:275
  156.2 53.1 %copy-start.29 = (f32[256,8]{0,1:T(8,128)}, f32[256,8]{0,1:T(8,128)S(1)}, u32[]{:S(2)}) copy-start(f32[256,8]{0,1:T(8,128)S(1)} %reduce_sum.99) | copy-start | bytes 24580
  158.1 51.3 %collective-permute-start.18 = (f32[8,256]{1,0:T(8,128)S(1)}, f32[8,256]{1,0:T(8,128)S(1)}, u32[]{:S(2)}, u32[]{:S(2)}) collective-permute-start(f32[8,256]{1,0:T(8,128)S(1)} %bitcast.104), channel_id=1, source_target_pairs={{0,2},{1,3},{2,0},{3,1},{4,6},{5,7},{6,4},{7,5}} | collective-permute-start | bytes 24584 | tf_op jit(solution)/shard_map/ppermute | solution.py:275
  172.2 37.2 %collective-permute-start.19 = (f32[8,256]{1,0:T(8,128)S(1)}, f32[8,256]{1,0:T(8,128)S(1)}, u32[]{:S(2)}, u32[]{:S(2)}) collective-permute-start(f32[8,256]{1,0:T(8,128)S(1)} %bitcast.105), channel_id=1, source_target_pairs={{0,4},{1,5},{2,6},{3,7},{4,0},{5,1},{6,2},{7,3}} | collective-permute-start | bytes 24584 | tf_op jit(solution)/shard_map/ppermute | solution.py:275
  173.7 35.8 %collective-permute-start.20 = (f32[8,256]{1,0:T(8,128)S(1)}, f32[8,256]{1,0:T(8,128)S(1)}, u32[]{:S(2)}, u32[]{:S(2)}) collective-permute-start(f32[8,256]{1,0:T(8,128)S(1)} %bitcast.106), channel_id=1, source_target_pairs={{0,6},{1,7},{2,4},{3,5},{4,2},{5,3},{6,0},{7,1}} | collective-permute-start | bytes 24584 | tf_op jit(solution)/shard_map/ppermute | solution.py:275
  174.9 34.4 %collective-permute-start.4 = (bf16[256,1536]{1,0:T(8,128)(2,1)S(1)}, bf16[256,1536]{1,0:T(8,128)(2,1)S(1)}, u32[]{:S(2)}, u32[]{:S(2)}) collective-permute-start(bf16[256,1536]{1,0:T(8,128)(2,1)S(1)} %multiply_convert_fusion.refs_4_), channel_id=1, source_target_pairs={{0,4},{1,5},{2,6},{3,7},{4,0},{5,1},{6,2},{7,3}} | collective-permute-start | bytes 2359304 | tf_op jit(solution)/shard_map/ppermute | solution.py:275
  176.5 32.9 %collective-permute-start.5 = (bf16[256,1536]{1,0:T(8,128)(2,1)S(1)}, bf16[256,1536]{1,0:T(8,128)(2,1)S(1)}, u32[]{:S(2)}, u32[]{:S(2)}) collective-permute-start(bf16[256,1536]{1,0:T(8,128)(2,1)S(1)} %multiply_convert_fusion.refs_4_), channel_id=1, source_target_pairs={{0,6},{1,7},{2,4},{3,5},{4,2},{5,3},{6,0},{7,1}} | collective-permute-start | bytes 2359304 | tf_op jit(solution)/shard_map/ppermute | solution.py:275
  209.4 38.2 %copy-start.36 = (f32[128,1536]{1,0:T(8,128)S(1)}, f32[128,1536]{1,0:T(8,128)}, u32[]{:S(2)}) copy-start(f32[128,1536]{1,0:T(8,128)} %get-tuple-element.69) | copy-start | bytes 2359300
  209.4 38.2 %copy-start.35 = (f32[128,1536]{1,0:T(8,128)S(1)}, f32[128,1536]{1,0:T(8,128)}, u32[]{:S(2)}) copy-start(f32[128,1536]{1,0:T(8,128)} %get-tuple-element.70) | copy-start | bytes 2359300
  243.2 39.8 %copy-start.34 = (f32[128,1536]{1,0:T(8,128)S(1)}, f32[128,1536]{1,0:T(8,128)}, u32[]{:S(2)}) copy-start(f32[128,1536]{1,0:T(8,128)} %get-tuple-element.78) | copy-start | bytes 2359300
  243.2 41.8 %copy-start.19 = (f32[128,1536]{1,0:T(8,128)S(1)}, f32[128,1536]{1,0:T(8,128)}, u32[]{:S(2)}) copy-start(f32[128,1536]{1,0:T(8,128)} %get-tuple-element.79) | copy-start | bytes 2359300
  243.3 20.6 %collective-permute-start.28 = (f32[128,1536]{1,0:T(8,128)}, f32[128,1536]{1,0:T(8,128)S(1)}, u32[]{:S(2)}, u32[]{:S(2)}) collective-permute-start(f32[128,1536]{1,0:T(8,128)} %get-tuple-element.88), channel_id=1, source_target_pairs={{0,4},{1,5},{2,6},{3,7},{4,0},{5,1},{6,2},{7,3}} | collective-permute-start | bytes 2359304 | tf_op jit(solution)/shard_map/ppermute | solution.py:275
  244.7 22.8 %collective-permute-start.25 = (f32[128,1536]{1,0:T(8,128)}, f32[128,1536]{1,0:T(8,128)S(1)}, u32[]{:S(2)}, u32[]{:S(2)}) collective-permute-start(f32[128,1536]{1,0:T(8,128)} %get-tuple-element.84), channel_id=1, source_target_pairs={{0,2},{1,3},{2,0},{3,1},{4,6},{5,7},{6,4},{7,5}} | collective-permute-start | bytes 2359304 | tf_op jit(solution)/shard_map/ppermute | solution.py:275
  247.6 35.5 %collective-permute-start.16 = (f32[128,1536]{1,0:T(8,128)S(1)}, f32[128,1536]{1,0:T(8,128)S(1)}, u32[]{:S(2)}, u32[]{:S(2)}) collective-permute-start(f32[128,1536]{1,0:T(8,128)S(1)} %copy-done.36), channel_id=1, source_target_pairs={{0,2},{1,3},{2,0},{3,1},{4,6},{5,7},{6,4},{7,5}} | collective-permute-start | bytes 2359304 | tf_op jit(solution)/shard_map/ppermute | solution.py:275
  247.6 35.5 %collective-permute-start.17 = (f32[128,1536]{1,0:T(8,128)S(1)}, f32[128,1536]{1,0:T(8,128)S(1)}, u32[]{:S(2)}, u32[]{:S(2)}) collective-permute-start(f32[128,1536]{1,0:T(8,128)S(1)} %copy-done.35), channel_id=1, source_target_pairs={{0,4},{1,5},{2,6},{3,7},{4,0},{5,1},{6,2},{7,3}} | collective-permute-start | bytes 2359304 | tf_op jit(solution)/shard_map/ppermute | solution.py:275
  247.6 50.0 %collective-permute-start.27 = (f32[128,1536]{1,0:T(8,128)}, f32[128,1536]{1,0:T(8,128)S(1)}, u32[]{:S(2)}, u32[]{:S(2)}) collective-permute-start(f32[128,1536]{1,0:T(8,128)} %get-tuple-element.86), channel_id=1, source_target_pairs={{0,4},{1,5},{2,6},{3,7},{4,0},{5,1},{6,2},{7,3}} | collective-permute-start | bytes 2359304 | tf_op jit(solution)/shard_map/ppermute | solution.py:275
  265.2 34.7 %collective-permute-start.29 = (f32[128,1536]{1,0:T(8,128)S(1)}, f32[128,1536]{1,0:T(8,128)S(1)}, u32[]{:S(2)}, u32[]{:S(2)}) collective-permute-start(f32[128,1536]{1,0:T(8,128)S(1)} %add.147), channel_id=1, source_target_pairs={{0,2},{1,3},{2,0},{3,1},{4,6},{5,7},{6,4},{7,5}} | collective-permute-start | bytes 2359304 | tf_op jit(solution)/shard_map/ppermute | solution.py:275
  267.5 49.2 %collective-permute-start.24 = (f32[128,1536]{1,0:T(8,128)}, f32[128,1536]{1,0:T(8,128)S(1)}, u32[]{:S(2)}, u32[]{:S(2)}) collective-permute-start(f32[128,1536]{1,0:T(8,128)} %get-tuple-element.82), channel_id=1, source_target_pairs={{0,2},{1,3},{2,0},{3,1},{4,6},{5,7},{6,4},{7,5}} | collective-permute-start | bytes 2359304 | tf_op jit(solution)/shard_map/ppermute | solution.py:275
  268.2 33.7 %copy-start.21 = (f32[128,1536]{1,0:T(8,128)S(1)}, f32[128,1536]{1,0:T(8,128)}, u32[]{:S(2)}) copy-start(f32[128,1536]{1,0:T(8,128)} %get-tuple-element.85) | copy-start | bytes 2359300
  283.0 33.7 %collective-permute-start.26 = (f32[128,1536]{1,0:T(8,128)S(1)}, f32[128,1536]{1,0:T(8,128)S(1)}, u32[]{:S(2)}, u32[]{:S(2)}) collective-permute-start(f32[128,1536]{1,0:T(8,128)S(1)} %add.144), channel_id=1, source_target_pairs={{0,4},{1,5},{2,6},{3,7},{4,0},{5,1},{6,2},{7,3}} | collective-permute-start | bytes 2359304 | tf_op jit(solution)/shard_map/ppermute | solution.py:275
  283.0 48.3 %collective-permute-start.22 = (f32[128,1536]{1,0:T(8,128)S(1)}, f32[128,1536]{1,0:T(8,128)S(1)}, u32[]{:S(2)}, u32[]{:S(2)}) collective-permute-start(f32[128,1536]{1,0:T(8,128)S(1)} %copy-done.34), channel_id=1, source_target_pairs={{0,4},{1,5},{2,6},{3,7},{4,0},{5,1},{6,2},{7,3}} | collective-permute-start | bytes 2359304 | tf_op jit(solution)/shard_map/ppermute | solution.py:275
  285.1 31.6 %copy-start.20 = (f32[128,1536]{1,0:T(8,128)S(1)}, f32[128,1536]{1,0:T(8,128)}, u32[]{:S(2)}) copy-start(f32[128,1536]{1,0:T(8,128)} %get-tuple-element.81) | copy-start | bytes 2359300
  297.6 49.3 %collective-permute-start.15 = (f32[128,1536]{1,0:T(8,128)S(1)}, f32[128,1536]{1,0:T(8,128)S(1)}, u32[]{:S(2)}, u32[]{:S(2)}) collective-permute-start(f32[128,1536]{1,0:T(8,128)S(1)} %copy-done.33), channel_id=1, source_target_pairs={{0,2},{1,3},{2,0},{3,1},{4,6},{5,7},{6,4},{7,5}} | collective-permute-start | bytes 2359304 | tf_op jit(solution)/shard_map/ppermute | solution.py:275
  299.9 46.9 %collective-permute-start.23 = (f32[128,1536]{1,0:T(8,128)S(1)}, f32[128,1536]{1,0:T(8,128)S(1)}, u32[]{:S(2)}, u32[]{:S(2)}) collective-permute-start(f32[128,1536]{1,0:T(8,128)S(1)} %add.141), channel_id=1, source_target_pairs={{0,2},{1,3},{2,0},{3,1},{4,6},{5,7},{6,4},{7,5}} | collective-permute-start | bytes 2359304 | tf_op jit(solution)/shard_map/ppermute | solution.py:275
  301.9 44.9 %copy-start.17 = (f32[128,1536]{1,0:T(8,128)S(1)}, f32[128,1536]{1,0:T(8,128)}, u32[]{:S(2)}) copy-start(f32[128,1536]{1,0:T(8,128)} %get-tuple-element.77) | copy-start | bytes 2359300
  302.0 44.9 %copy-start.16 = (f32[128,1536]{1,0:T(8,128)S(1)}, f32[128,1536]{1,0:T(8,128)}, u32[]{:S(2)}) copy-start(f32[128,1536]{1,0:T(8,128)} %get-tuple-element.66) | copy-start | bytes 2359300
  316.7 30.2 %collective-permute-start.21 = (f32[128,1536]{1,0:T(8,128)S(1)}, f32[128,1536]{1,0:T(8,128)S(1)}, u32[]{:S(2)}, u32[]{:S(2)}) collective-permute-start(f32[128,1536]{1,0:T(8,128)S(1)} %add.138), channel_id=1, source_target_pairs={{0,4},{1,5},{2,6},{3,7},{4,0},{5,1},{6,2},{7,3}} | collective-permute-start | bytes 2359304 | tf_op jit(solution)/shard_map/ppermute | solution.py:275
  (27 other events, 173.9 us)

commit v3 on v2

--- a/solution.py
+++ b/solution.py
@@ -25,7 +25,7 @@
     n_rep = q_ref.shape[0]
     n_slots = kc_ref.shape[0]
     n_batch = q_ref.shape[2]
-    unroll = 4
+    unroll = 16
 
     def norm_rope(values, gain, cosine, sine):
         ms = jnp.mean(values * values, axis=0, keepdims=True)
@@ -38,19 +38,26 @@
         lanes = pl.ds(bt * 128, 128)
         cosine, sine = cos_ref[:, lanes], sin_ref[:, lanes]
         lens = len_ref[:, lanes]
-        left0 = jnp.broadcast_to(lens.astype(jnp.float32), (16, 128)).astype(jnp.bfloat16)
-        k_new = norm_rope(k_ref[0, :, lanes], kn_ref[...], cosine, sine).reshape(4, 16, 128)
-        v_new = v_ref[0, :, lanes].reshape(4, 16, 128)
+        left0 = jnp.broadcast_to(lens.astype(jnp.float32), (8, 128)).astype(jnp.bfloat16)
+        k_new = norm_rope(k_ref[0, :, lanes], kn_ref[...], cosine, sine).reshape(8, 8, 128)
+        v_new = v_ref[0, :, lanes].reshape(8, 8, 128)
         qs = [norm_rope(q_ref[r, :, lanes], qn_ref[...], cosine, sine).astype(jnp.float32).reshape(8, 8, 128) for r in range(n_rep)]
 
         def k_step(i, left):
             for u in range(unroll):
                 s = i * unroll + u
-                tile = jnp.where((left == 0)[None], k_new, kc_ref[s, 0, :, :, lanes])
-                ko_ref[s, 0, :, :, lanes] = tile
-                wide = tile.astype(jnp.float32).reshape(8, 8, 128)
+                here = left == 0
+                sums = [None] * n_rep
+                for t in range(8):
+                    tile = jnp.where(here, k_new[t], kc_ref[s, 0, t, :, lanes])
+                    ko_ref[s, 0, t, :, lanes] = tile
+                    wide = tile.astype(jnp.float32)
+                    for v in range(1):
+                        for r in range(n_rep):
+                            term = wide[8 * v:8 * v + 8] * qs[r][1 * t + v]
+                            sums[r] = term if sums[r] is None else sums[r] + term
                 for r in range(n_rep):
-                    part_ref[r, pl.ds(pl.multiple_of(s * 8, 8), 8), :] = jnp.sum(wide * qs[r], axis=0)
+                    part_ref[r, pl.ds(pl.multiple_of(s * 8, 8), 8), :] = sums[r]
                 left = left - jnp.ones_like(left)
             return left
 
@@ -69,17 +76,25 @@
             left, accs = carry
             for u in range(unroll):
                 s = i * unroll + u
-                tile = jnp.where((left == 0)[None], v_new, vc_ref[s, 0, :, :, lanes])
-                vo_ref[s, 0, :, :, lanes] = tile
-                wide = tile.astype(jnp.float32).reshape(8, 8, 128)
-                accs = tuple(accs[r] + wide * p_ref[r, pl.ds(s, 1), :][None] for r in range(n_rep))
+                here = left == 0
+                probs = [jnp.broadcast_to(p_ref[r, pl.ds(s, 1), :], (8, 128)) for r in range(n_rep)]
+                accs = list(accs)
+                for t in range(8):
+                    tile = jnp.where(here, v_new[t], vc_ref[s, 0, t, :, lanes])
+                    vo_ref[s, 0, t, :, lanes] = tile
+                    wide = tile.astype(jnp.float32)
+                    for v in range(1):
+                        for r in range(n_rep):
+                            at = 8 * r + 1 * t + v
+                            accs[at] = accs[at] + wide[8 * v:8 * v + 8] * probs[r]
+                accs = tuple(accs)
                 left = left - jnp.ones_like(left)
             return left, accs
 
-        zero = jnp.zeros((8, 8, 128), jnp.float32)
-        _, accs = lax.fori_loop(0, n_slots // unroll, v_step, (left0, (zero,) * n_rep))
+        zero = jnp.zeros((8, 128), jnp.float32)
+        _, accs = lax.fori_loop(0, n_slots // unroll, v_step, (left0, (zero,) * (8 * n_rep)))
         for r in range(n_rep):
-            o_ref[r, :, lanes] = accs[r].reshape(64, 128).astype(jnp.bfloat16)
+            o_ref[r, :, lanes] = jnp.concatenate(accs[8 * r:8 * r + 8], axis=0).astype(jnp.bfloat16)
 
 
 def project(x_in, cache_len, ln_attn, w_q, w_k, w_v, head_dim):
@@ -102,7 +117,7 @@
     n_rep = q_t.shape[0] // kv_heads
     full = lambda *shape: pl.BlockSpec(shape, lambda g: (0,) * len(shape))
     lane = lambda n: pl.BlockSpec((n, n_batch), lambda g: (0, chunk))
-    cache_spec = pl.BlockSpec((n_slots, 1, 4, 16, n_batch), lambda g: (0, g, 0, 0, chunk))
+    cache_spec = pl.BlockSpec((n_slots, 1, 8, 8, n_batch), lambda g: (0, g, 0, 0, chunk))
     head_spec = lambda n: pl.BlockSpec((n, head_dim, n_batch), lambda g: (g, 0, chunk))
     out_spec = pl.BlockSpec((n_rep, head_dim, n_batch), lambda g: (g, 0, 0))
     cache_shape = jax.ShapeDtypeStruct(k_cache.shape, jnp.bfloat16)
@@ -126,12 +141,12 @@
     )(*done, len_row, cosine, sine, q_gain, k_gain, q_t, k_t, v_t, k_cache, v_cache)
 
 
-def expert_kernel(n_sub, e_local, dev_ref, start_ref, count_ref, prow_ref, *refs):
-    r_refs = refs[:2 * n_sub]
+def expert_kernel(n_sub, e_local, dev_ref, wr_ref, *refs):
+    t_refs = refs[:2 * n_sub]
     h_refs = refs[2 * n_sub:4 * n_sub]
     w_refs = refs[4 * n_sub:4 * n_sub + 6]
     o_refs = refs[4 * n_sub + 6:8 * n_sub + 6]
-    xs_ref, ys_ref, wg_ref, wu_ref, wd_ref, sem = refs[8 * n_sub + 6:]
+    xs_ref, ys_ref, wg_ref, wu_ref, wd_ref, prow_ref, r_ref, number_ref, number_smem, sem, number_sem = refs[8 * n_sub + 6:]
     bufs = (wg_ref, wu_ref, wd_ref)
     ring = wg_ref.shape[0]
     step = pl.program_id(0)
@@ -157,6 +172,43 @@
         ys_ref[...] = jnp.zeros_like(ys_ref)
         for j in range(n_sub):
             xs_ref[j, SORTED:, :] = jnp.zeros((ROOM - SORTED, hidden), jnp.bfloat16)
+
+        locals_of = {}
+        for q in range(2 * n_sub):
+            picks = t_refs[q][...]
+            n_experts = wr_ref.shape[0]
+            logits = lax.dot_general(wr_ref[...], h_refs[q][...], (((1,), (1,)), ((), ())), preferred_element_type=jnp.float32)
+            expert = lax.broadcasted_iota(jnp.int32, (n_experts, half), 0)
+            times = jnp.zeros((n_experts, half), jnp.float32)
+            for k in range(picks.shape[0]):
+                times = times + jnp.where(expert == picks[k:k + 1], 1.0, 0.0)
+            chosen = times > 0.0
+            top = jnp.max(jnp.where(chosen, logits, -3.4e38), axis=0, keepdims=True)
+            expd = jnp.where(chosen, jnp.exp(jnp.where(chosen, logits - top, 0.0)), 0.0)
+            gate = expd / jnp.sum(expd, axis=0, keepdims=True)
+            for which in range(2):
+                low = dev_ref[which] * e_local
+                r_ref[2 * q + which:2 * q + which + 1, :] = jnp.sum(jnp.where((expert >= low) & (expert < low + e_local), gate, 0.0), axis=0, keepdims=True)
+                here = (picks >= low) & (picks < low + e_local)
+                locals_of[q, which] = jnp.sum(jnp.where(here, (picks - low).astype(jnp.float32), 0.0), axis=0, keepdims=True)
+        lane_a = lax.broadcasted_iota(jnp.int32, (2 * half, 2 * half), 0)
+        lane_b = lax.broadcasted_iota(jnp.int32, (2 * half, 2 * half), 1)
+        before = jnp.where(lane_a < lane_b, 1.0, 0.0).astype(jnp.bfloat16)
+        local = lax.broadcasted_iota(jnp.int32, (16, 2 * half), 0).astype(jnp.float32)
+        for j in range(n_sub):
+            for which in range(2):
+                loc = jnp.concatenate([locals_of[2 * j, which], locals_of[2 * j + 1, which]], axis=1)
+                hot = jnp.where(local == loc, 1.0, 0.0)
+                rank = jnp.dot(hot.astype(jnp.bfloat16), before, preferred_element_type=jnp.float32)
+                number = jnp.sum(hot, axis=1, keepdims=True)
+                padded = ((number.astype(jnp.int32) + 15) // 16 * 16).astype(jnp.float32)
+                first = jnp.zeros((1, 1), jnp.float32)
+                seat = jnp.zeros((1, 2 * half), jnp.float32)
+                for e in range(e_local):
+                    seat = seat + hot[e:e + 1] * (rank[e:e + 1] + first)
+                    first = first + padded[e:e + 1]
+                prow_ref[2 * j + which:2 * j + which + 1, :] = seat.astype(jnp.int32)
+                number_ref[2 * j + which] = jnp.broadcast_to(number[:8], (8, 128)).astype(jnp.int32)
 
     fetch(step + ring - 1)
 
@@ -171,13 +223,26 @@
                 rows = rows + jnp.dot(hot[:, half:], h_refs[2 * j + 1][...], preferred_element_type=jnp.float32)
                 xs_ref[j, c * PIECE:(c + 1) * PIECE, :] = rows.astype(jnp.bfloat16)
 
+    @pl.when(step == 0)
+    def _():
+        to_scalars = pltpu.make_async_copy(number_ref, number_smem, number_sem)
+        to_scalars.start()
+        to_scalars.wait()
+
     slot = lax.rem(step, ring)
     for k in range(3):
         pltpu.make_async_copy(w_refs[k].at[0], bufs[k].at[slot], sem.at[slot, k]).wait()
-    counts = [count_ref[j * steps + step] for j in range(n_sub)]
+    mine_e = step - src * e_local
+    counts, starts = [], []
+    for j in range(n_sub):
+        counts.append((number_smem[2 * j + src, mine_e, 0] + PIECE - 1) // PIECE)
+        first = jnp.int32(0)
+        for e in range(e_local - 1):
+            first = first + jnp.where(e < mine_e, (number_smem[2 * j + src, e, 0] + 15) // 16 * 16, 0)
+        starts.append(first)
 
     def piece(c, carry):
-        offs = [pl.multiple_of(jnp.minimum(start_ref[j * steps + step] + c * PIECE, SORTED), 16) for j in range(n_sub)]
+        offs = [pl.multiple_of(jnp.minimum(starts[j] + c * PIECE, SORTED), 16) for j in range(n_sub)]
         rows = jnp.concatenate([xs_ref[j, pl.ds(offs[j], PIECE), :] for j in range(n_sub)], axis=0)
         gate = jnp.dot(rows, wg_ref[slot], preferred_element_type=jnp.float32)
         up = jnp.dot(rows, wu_ref[slot], preferred_element_type=jnp.float32)
@@ -195,11 +260,10 @@
         return jnp.broadcast_to(row, (128, row.shape[1])).T
 
     def back(which):
-        dev = dev_ref[which]
-        for j in range(n_sub):
-            seat_col = column(prow_ref[pl.ds(2 * j + which, 1), :].astype(jnp.float32))
+        for j in range(n_sub):
+            seat_col = column(prow_ref[2 * j + which:2 * j + which + 1, :].astype(jnp.float32))
             for i in range(2):
-                r_col = column(r_refs[2 * j + i][pl.ds(dev, 1), :])
+                r_col = column(r_ref[2 * (2 * j + i) + which:2 * (2 * j + i) + which + 1, :])
                 for c in range(half // PIECE):
                     at = seat_col[i * half + c * PIECE:i * half + (c + 1) * PIECE]
                     lane = lax.broadcasted_iota(jnp.int32, (PIECE, 128), 1).astype(jnp.float32)
@@ -218,7 +282,7 @@
         back(1)
 
 
-def experts(blocks, r_blocks, devs, starts, counts, seat, w_own, w_par):
+def experts(chunk, blocks, t_blocks, devs, w_r, w_own, w_par):
     n_sub = len(blocks) // 2
     half, hidden = blocks[0].shape
     e_local, _, ff = w_own[0].shape
@@ -228,39 +292,22 @@
     out = pl.pallas_call(
         functools.partial(expert_kernel, n_sub, e_local),
         grid_spec=pltpu.PrefetchScalarGridSpec(
-            num_scalar_prefetch=3,
+            num_scalar_prefetch=1,
             grid=(2 * e_local,),
-            in_specs=[full(2 * n_sub, 2 * half)] + [full(*r.shape) for r in r_blocks] + [full(half, hidden)] * (2 * n_sub)
+            in_specs=[full(*w_r.shape)] + [pl.BlockSpec((t_blocks[0].shape[0], half), lambda e, *_: (0, chunk))] * (2 * n_sub) + [full(half, hidden)] * (2 * n_sub)
             + [pl.BlockSpec(memory_space=pl.ANY)] * 6,
             out_specs=[full(PIECE, hidden)] * (4 * n_sub),
             scratch_shapes=[pltpu.VMEM((n_sub, ROOM, hidden), jnp.bfloat16)] * 2
-            + [pltpu.VMEM((ring, hidden, ff), jnp.bfloat16)] * 2 + [pltpu.VMEM((ring, ff, hidden), jnp.bfloat16), pltpu.SemaphoreType.DMA((ring, 3))],
+            + [pltpu.VMEM((ring, hidden, ff), jnp.bfloat16)] * 2 + [pltpu.VMEM((ring, ff, hidden), jnp.bfloat16)]
+            + [pltpu.VMEM((2 * n_sub, 2 * half), jnp.int32), pltpu.VMEM((4 * n_sub, half), jnp.float32), pltpu.VMEM((2 * n_sub, 8, 128), jnp.int32),
+               pltpu.SMEM((2 * n_sub, 8, 128), jnp.int32), pltpu.SemaphoreType.DMA((ring, 3)), pltpu.SemaphoreType.DMA],
         ),
         out_shape=[jax.ShapeDtypeStruct((PIECE, hidden), jnp.float32)] * (4 * n_sub),
         compiler_params=pltpu.CompilerParams(dimension_semantics=("arbitrary",), vmem_limit_bytes=58 * 2**20),
         cost_estimate=pl.CostEstimate(flops=n_sub * 16_000_000_000, bytes_accessed=60_000_000, transcendentals=0),
         name="experts",
-    )(devs, starts.reshape(-1), counts.reshape(-1), seat.reshape(2 * n_sub, 2 * half), *r_blocks, *blocks, *w_own, *w_par)
+    )(devs, w_r, *t_blocks, *blocks, *w_own, *w_par)
     return [(out[2 * i], out[2 * i + 1]) for i in range(2 * n_sub)]
-
-
-def seats(topk_blocks, me, e_local):
-    n_rows = topk_blocks.shape[1]
-    dev = topk_blocks // e_local
-    loc = topk_blocks % e_local
-    both = jnp.stack([me, me ^ 1])
-    loc_src = jnp.sum(jnp.where(dev[:, None] == both[None, :, None, None], loc[:, None], 0), axis=-1)
-    hot = (loc_src[:, :, None, :] == jnp.arange(e_local)[None, None, :, None])
-    before = (jnp.arange(n_rows)[:, None] < jnp.arange(n_rows)[None, :]).astype(jnp.bfloat16)
-    rank = lax.dot_general(hot.astype(jnp.bfloat16), before, (((3,), (0,)), ((), ())), preferred_element_type=jnp.float32).astype(jnp.int32)
-    count = jnp.sum(hot.astype(jnp.int32), axis=-1)
-    padded = (count + 15) // 16 * 16
-    starts = [jnp.zeros_like(count[..., 0])]
-    for e in range(1, e_local):
-        starts.append(starts[-1] + padded[..., e - 1])
-    start = jnp.stack(starts, axis=-1)
-    seat = jnp.sum(jnp.where(hot, start[..., None] + rank, 0), axis=2)
-    return seat, start, (count + PIECE - 1) // PIECE
 
 
 def solution(mesh):
@@ -276,24 +323,20 @@
 
     def device_step(x_in, k_cache, v_cache, cache_len, topk_idx, ln_attn, w_q, w_k, w_v, q_norm, k_norm, w_o, ln_moe, w_router, w_gate, w_up, w_down):
         me = lax.axis_index('ep')
-        e_local = w_gate.shape[0]
         n_batch, n_slots, kv_heads, head_dim = k_cache.shape
         n_rows = n_batch // CHUNKS
-        top_k = topk_idx.shape[1]
         w_own = (w_gate, w_up, w_down)
         w_par = tuple(swap(w, 1) for w in w_own)
-        blocks = jnp.stack([topk_idx, swap(topk_idx, 2), swap(topk_idx, 4), swap(topk_idx, 6)])
-        blocks = blocks.reshape(2, 2, CHUNKS, n_rows, top_k).transpose(2, 0, 1, 3, 4).reshape(2 * CHUNKS, 2 * n_rows, top_k)
-        seat, start, count = seats(blocks, me, e_local)
         devs = jnp.stack([me, me ^ 1]).astype(jnp.int32)
 
         q_t, k_t, v_t, cosine, sine = project(x_in, cache_len, ln_attn, w_q, w_k, w_v, head_dim)
-        by_slot = lambda c: c.transpose(1, 2, 3, 0).reshape(n_slots, kv_heads, 4, 16, n_batch)
+        by_slot = lambda c: c.transpose(1, 2, 3, 0).reshape(n_slots, kv_heads, 8, 8, n_batch)
         k_slots, v_slots = by_slot(k_cache), by_slot(v_cache)
         gains = (q_norm.astype(jnp.float32)[:, None], k_norm.astype(jnp.float32)[:, None])
-        len_row, seat, start, count = lax.optimization_barrier((cache_len[None, :], seat, start, count))
-
-        done, resid, own, far, gates = (), [], [], [], []
+        len_row = cache_len[None, :]
+        w_r = w_router.T
+
+        done, resid, own, far = (), [], [], []
         for c in range(CHUNKS):
             if c:
                 len_row, own[c - 1] = lax.optimization_barrier((len_row, own[c - 1]))
@@ -301,8 +344,7 @@
             done = (k_full, v_full)
             rows = slice(c * n_rows, (c + 1) * n_rows)
             o_proj = lax.dot_general(attn_t.reshape(-1, n_rows), w_o, (((0,), (0,)), ((), ())), preferred_element_type=jnp.float32)
-            x_mid = (x_in[rows].astype(jnp.float32) + o_proj).astype(jnp.bfloat16)
-            resid.append(x_mid.astype(jnp.float32))
+            resid.append(lax.reduce_precision(x_in[rows].astype(jnp.float32) + o_proj, 8, 7))
             h_moe = norm_scale(resid[c], ln_moe).astype(jnp.bfloat16)
             own.append(h_moe)
             h_x = swap(h_moe, 2)
@@ -310,13 +352,9 @@
             h_d = swap(h_moe, 6)
             far.append((h_x, h_y, h_d))
 
-            logits = jnp.dot(h_moe, w_router, preferred_element_type=jnp.float32)
-            chosen = jnp.any(topk_idx[rows][:, :, None] == jnp.arange(logits.shape[1])[None, None, :], axis=1)
-            top = jnp.max(jnp.where(chosen, logits, -jnp.inf), axis=1, keepdims=True)
-            expd = jnp.where(chosen, jnp.exp(jnp.where(chosen, logits - top, 0.0)), 0.0)
-            gate = expd / jnp.sum(expd, axis=1, keepdims=True)
-            r_dev = jnp.sum(gate.reshape(-1, ep_size, e_local), axis=-1).T
-            gates.append((r_dev, swap(r_dev, 2), swap(r_dev, 4), swap(r_dev, 6)))
+            if c == 0:
+                picks, own[0] = lax.optimization_barrier((topk_idx.T, own[0]))
+                t_blocks = [picks, swap(picks, 2), swap(picks, 4), swap(picks, 6)]
 
         sums = []
         for c in range(CHUNKS):
@@ -325,8 +363,7 @@
                 h_o, own[-1] = lax.optimization_barrier((h_o, own[-1]))
             else:
                 h_far, sums[c - 1] = lax.optimization_barrier((h_far, sums[c - 1]))
-            pick = slice(2 * c, 2 * c + 2)
-            s_o, s_x, s_y, s_d = experts([h_o, *h_far], gates[c], devs, start[pick], count[pick], seat[pick], w_own, w_par)
+            s_o, s_x, s_y, s_d = experts(c, [h_o, *h_far], t_blocks, devs, w_r, w_own, w_par)
             sums.append((s_o, s_x, s_y, s_d))
         outs = []
         sent = []

time: 349 us -> 295 us (0.85)
  waiting for transfers between devices: 129 us -> 105 us
  local copies, waits for them, and re-layouts: 13.9 us -> 4.82 us
  starting transfers between devices: 37 us -> 29.1 us
  other arithmetic: 12.8 us -> 7.43 us
  matrix products: 20.8 us -> 17 us
    ppermute x30 -> x24, waiting for transfers between devices: 129 us -> 105 us  [swap(): return lax.ppermute(value, 'ep', [(i, i ^ bit) for i in range(ep_size)])]
    pallas_call x2, Pallas kernels: 69.5 us -> 61.1 us  [attend(): pl.pallas_call(body, grid=(kv_heads,), in_specs=[pl.BlockSpec(memory_spac...]
    ppermute x30 -> x24, starting transfers between devices: 37 us -> 29.1 us  [swap(): return lax.ppermute(value, 'ep', [(i, i ^ bit) for i in range(ep_size)])]
    pallas_call x2, Pallas kernels: 64.2 us -> 69.5 us  [experts(): pl.pallas_call(functools.partial(expert_kernel, n_sub, e_local), grid_spe...]
    reshape x8 -> x0, local copies, waits for them, and re-layouts: 4.53 us -> none  [the longest x2 1.3 us: experts(): counts.reshape(-1)]
    unnamed x90 -> x70, local copies, waits for them, and re-layouts: 8.35 us -> 4.63 us
  transfers between devices with their start and end apart: 30 -> 24, of which waited for: 10 -> 10; matrix products, arithmetic and copies ran while one was open for 11% -> 8% of each run, Pallas kernels for 29% -> 44%
where the time goes in v3:
time: 295 us
  Pallas kernels  131 us (44%)
  waiting for transfers between devices  105 us (36%)
  starting transfers between devices  29.1 us (10%)
  matrix products  17 us (6%)
  other arithmetic  7.43 us (3%)
  local copies, waits for them, and re-layouts  4.82 us (2%)
    ppermute x24, waiting for transfers between devices, swap(): return lax.ppermute(value, 'ep', [(i, i ^ bit) for i in range(ep_size)])  105 us
    pallas_call x2, Pallas kernels, experts(): pl.pallas_call(functools.partial(expert_kernel, n_sub, e_local), grid_spe...  69.5 us
    pallas_call x2, Pallas kernels, attend(): pl.pallas_call(body, grid=(kv_heads,), in_specs=[pl.BlockSpec(memory_spac...  61.1 us
    ppermute x24, starting transfers between devices, swap(): return lax.ppermute(value, 'ep', [(i, i ^ bit) for i in range(ep_size)])  29.1 us
    dot_general x3, matrix products, proj(): jnp.dot(normed, w, preferred_element_type=jnp.float32)  11.4 us
  transfers between devices with their start and end apart: 24, of which 10 were waited for; matrix products, arithmetic and copies ran while one was open for 8% of the time, Pallas kernels for 44%

profile of v3, /device:TPU:0, one launch (start us, length us, event | category | flops | bytes accessed | tf_op | source)
XLA Modules:
  0.0 294.9 jit_solution(6773506505346412872)
XLA Ops:
  0.6 0.9 collective-permute-start.10
  1.5 0.5 collective-permute-start.9
  2.0 0.7 convert_element_type.43
  2.7 1.8 fusion
  4.5 7.3 %fusion.9 = f32[512,1536]{0,1:T(8,128)} fusion(bf16[1536,1536]{1,0:T(8,128)(2,1)} %param.23, bf16[512,1536]{1,0:T(8,128)(2,1)} %param.17, f32[1536]{0:T(1024)S(1)} %convert_element_type.43, f32[512]{0:T(512)S(1)} %add_rsqrt_fusion), kind=kOutput, calls=%fused_computation.30 | convolution fusion | flops 2419064832 | bytes 9445376 | tf_op jit(solution)/shard_map/dot_general | solution.py:105
  11.9 2.1 fusion.7
  14.0 1.9 convolution_convert_fusion
  16.5 1.2 copy-done.3
  17.7 1.0 copy-done.4
  18.8 30.6 %attend.2 = (bf16[64,8,8,8,512]{4,3,2,1,0:T(8,128)(2,1)}, bf16[64,8,8,8,512]{4,3,2,1,0:T(8,128)(2,1)}, bf16[24,64,256]{2,1,0:T(8,128)(2,1)S(1)}) custom-call(s32[1,512]{1,0:T(1,128)S(1)} %bitcast.49, f32[32,512]{1,0:T(8,128)S(1)} %get-tuple-element.88.refs_1_.refs_3_, f32[32,512]{1,0:T(8,128)S(1)} %get-tuple-element.87.refs_2_.refs_4_, ...), custom_call_target="tpu_custom_call" | custom-call | flops 30000001024 | bytes 70000000 | tf_op jit(solution)/shard_map/attend/pallas_call | solution.py:129
  49.4 4.0 %multiply_reduce_fusion.1 = (f32[256]{0:T(256)S(1)}, f32[256,1536]{1,0:T(8,128)S(1)}) fusion(bf16[1536,256]{1,0:T(8,128)(2,1)S(1)} %bitcast.44, bf16[1536,1536]{1,0:T(8,128)(2,1)} %param.28, bf16[512,1536]{1,0:T(8,128)(2,1)S(1)} %copy-done.9), kind=kOutput, calls=%fused_computation.14 | convolution fusion | flops 1209925376 | bytes 7865344 | tf_op jit(solution)/shard_map/dot_general | solution.py:346
  53.4 1.2 multiply_convert_fusion.1.refs_4_
  54.7 2.5 collective-permute-start.3
  57.2 1.5 collective-permute-start.4
  58.9 2.0 collective-permute-start.6
  60.9 30.5 %attend.3 = (bf16[64,8,8,8,512]{4,3,2,1,0:T(8,128)(2,1)}, bf16[64,8,8,8,512]{4,3,2,1,0:T(8,128)(2,1)}, bf16[24,64,256]{2,1,0:T(8,128)(2,1)S(1)}) custom-call(bf16[64,8,8,8,512]{4,3,2,1,0:T(8,128)(2,1)} %get-tuple-element.46.refs_0_, bf16[64,8,8,8,512]{4,3,2,1,0:T(8,128)(2,1)} %get-tuple-element.47.refs_1_, ...), custom_call_target="tpu_custom_call", output_to_operand_aliasing={{0}: (0, {}), {1}: (1, {})} | custom-call | flops 30000001024 | bytes 70000000 | tf_op jit(solution)/shard_map/attend/pallas_call | solution.py:129
  91.5 1.5 collective-permute-start.5
  93.0 1.5 multiply_reduce_fusion
  94.6 1.6 collective-permute-done.5.refs_3_
  96.1 1.5 collective-permute-start.7
  97.7 0.9 copy-done.23
  98.8 0.7 pad_add_fusion.dev_ref
  99.5 31.1 %collective-permute-done.7.refs_6_ = bf16[256,1536]{1,0:T(8,128)(2,1)} collective-permute-done((bf16[256,1536]{1,0:T(8,128)(2,1)}, bf16[256,1536]{1,0:T(8,128)(2,1)}, u32[]{:S(2)}, u32[]{:S(2)}) %collective-permute-start.7) | collective-permute-done | bytes 786464 | tf_op jit(solution)/shard_map/ppermute | solution.py:322
  130.7 0.8 collective-permute-start
  131.5 1.2 collective-permute-start.1
  132.7 1.4 collective-permute-start.2
  134.2 34.7 %experts.2 = (f32[128,1536]{1,0:T(8,128)}, f32[128,1536]{1,0:T(8,128)}, f32[128,1536]{1,0:T(8,128)}, f32[128,1536]{1,0:T(8,128)}, f32[128,1536]{1,0:T(8,128)}, /...) custom-call(s32[2]{0:T(128)} %pad_add_fusion.dev_ref, bf16[40,1536]{1,0:T(8,128)(2,1)} %bitcast.59, ...), custom_call_target="tpu_custom_call" | custom-call | flops 32000000000 | bytes 60000000 | tf_op jit(solution)/shard_map/experts/pallas_call | solution.py:292
  169.0 0.8 copy-done.24
  170.3 0.8 collective-permute-start.13
  171.1 1.2 collective-permute-start.14
  172.4 34.8 %experts.3 = (f32[128,1536]{1,0:T(8,128)}, f32[128,1536]{1,0:T(8,128)}, f32[128,1536]{1,0:T(8,128)}, f32[128,1536]{1,0:T(8,128)}, f32[128,1536]{1,0:T(8,128)}, /...) custom-call(s32[2]{0:T(128)} %pad_add_fusion.dev_ref, bf16[40,1536]{1,0:T(8,128)(2,1)} %bitcast.60, ...), custom_call_target="tpu_custom_call" | custom-call | flops 32000000000 | bytes 60000000 | tf_op jit(solution)/shard_map/experts/pallas_call | solution.py:292
  207.2 1.5 collective-permute-start.19
  208.7 0.5 collective-permute-start.12
  209.2 1.5 collective-permute-start.22
  210.9 0.5 collective-permute-start.15
  211.4 1.5 collective-permute-start.16
  213.1 14.8 %collective-permute-done.19 = f32[128,1536]{1,0:T(8,128)S(1)} collective-permute-done((f32[128,1536]{1,0:T(8,128)}, f32[128,1536]{1,0:T(8,128)S(1)}, u32[]{:S(2)}, u32[]{:S(2)}) %collective-permute-start.19) | collective-permute-done | bytes 786464 | tf_op jit(solution)/shard_map/ppermute | solution.py:322
  227.8 1.5 collective-permute-start.17
  229.9 1.5 collective-permute-start.18
  231.5 13.2 %collective-permute-done.12 = f32[128,1536]{1,0:T(8,128)S(1)} collective-permute-done((f32[128,1536]{1,0:T(8,128)}, f32[128,1536]{1,0:T(8,128)S(1)}, u32[]{:S(2)}, u32[]{:S(2)}) %collective-permute-start.12) | collective-permute-done | bytes 786464 | tf_op jit(solution)/shard_map/ppermute | solution.py:322
  244.7 1.5 collective-permute-start.21
  246.2 0.5 collective-permute-done.15
  246.7 1.5 collective-permute-start.20
  248.4 15.2 %collective-permute-done.16 = f32[128,1536]{1,0:T(8,128)S(1)} collective-permute-done((f32[128,1536]{1,0:T(8,128)}, f32[128,1536]{1,0:T(8,128)S(1)}, u32[]{:S(2)}, u32[]{:S(2)}) %collective-permute-start.16) | collective-permute-done | bytes 786464 | tf_op jit(solution)/shard_map/ppermute | solution.py:322
  263.6 1.5 collective-permute-start.23
  265.2 13.2 %collective-permute-done.18 = f32[128,1536]{1,0:T(8,128)S(1)} collective-permute-done((f32[128,1536]{1,0:T(8,128)S(1)}, f32[128,1536]{1,0:T(8,128)S(1)}, u32[]{:S(2)}, u32[]{:S(2)}) %collective-permute-start.18) | collective-permute-done | bytes 786464 | tf_op jit(solution)/shard_map/ppermute | solution.py:322
  278.4 14.6 %collective-permute-done.20 = f32[128,1536]{1,0:T(8,128)S(1)} collective-permute-done((f32[128,1536]{1,0:T(8,128)S(1)}, f32[128,1536]{1,0:T(8,128)S(1)}, u32[]{:S(2)}, u32[]{:S(2)}) %collective-permute-start.20) | collective-permute-done | bytes 786464 | tf_op jit(solution)/shard_map/ppermute | solution.py:322
  293.3 1.6 fusion.3
  (105 shorter events, 3.0 us)
Async XLA Ops:
  0.6 11.2 %copy-start = (bf16[1536,512]{1,0:T(8,128)(2,1)S(1)}, bf16[1536,512]{1,0:T(8,128)(2,1)}, u32[]{:S(2)}) copy-start(bf16[1536,512]{1,0:T(8,128)(2,1)} %param.24) | copy-start | bytes 4718596
  0.6 132.1 %collective-permute-start.10 = (bf16[5,1536,512]{2,1,0:T(8,128)(2,1)}, bf16[5,1536,512]{2,1,0:T(8,128)(2,1)}, u32[]{:S(2)}, u32[]{:S(2)}) collective-permute-start(bf16[5,1536,512]{2,1,0:T(8,128)(2,1)} %refs_9_.3), channel_id=1, source_target_pairs={{0,1},{1,0},{2,3},{3,2},{4,5},{5,4},{6,7},{7,6}} | collective-permute-start | bytes 23592968 | tf_op jit(solution)/shard_map/ppermute | solution.py:322
  1.5 132.7 %collective-permute-start.11 = (bf16[5,512,1536]{2,1,0:T(8,128)(2,1)}, bf16[5,512,1536]{2,1,0:T(8,128)(2,1)}, u32[]{:S(2)}, u32[]{:S(2)}) collective-permute-start(bf16[5,512,1536]{2,1,0:T(8,128)(2,1)} %refs_10_.3), channel_id=1, source_target_pairs={{0,1},{1,0},{2,3},{3,2},{4,5},{5,4},{6,7},{7,6}} | collective-permute-start | bytes 23592968 | tf_op jit(solution)/shard_map/ppermute | solution.py:322
  1.5 132.6 %collective-permute-start.9 = (bf16[5,1536,512]{2,1,0:T(8,128)(2,1)}, bf16[5,1536,512]{2,1,0:T(8,128)(2,1)}, u32[]{:S(2)}, u32[]{:S(2)}) collective-permute-start(bf16[5,1536,512]{2,1,0:T(8,128)(2,1)} %refs_8_.3), channel_id=1, source_target_pairs={{0,1},{1,0},{2,3},{3,2},{4,5},{5,4},{6,7},{7,6}} | collective-permute-start | bytes 23592968 | tf_op jit(solution)/shard_map/ppermute | solution.py:322
  4.5 7.4 %copy-start.8 = (bf16[512,1536]{1,0:T(8,128)(2,1)S(1)}, bf16[512,1536]{1,0:T(8,128)(2,1)}, u32[]{:S(2)}) copy-start(bf16[512,1536]{1,0:T(8,128)(2,1)} %param.17) | copy-start | bytes 4718596
  14.0 2.2 copy-start.19
  14.0 2.5 copy-start.2
  18.8 30.6 %copy-start.9 = (bf16[512,1536]{1,0:T(8,128)(2,1)S(1)}, bf16[512,1536]{1,0:T(8,128)(2,1)}, u32[]{:S(2)}) copy-start(bf16[512,1536]{1,0:T(8,128)(2,1)} %param.17) | copy-start | bytes 4718596
  49.4 5.3 %copy-start.27 = (s32[512,8]{0,1:T(8,128)S(1)}, s32[512,8]{0,1:T(8,128)}, u32[]{:S(2)}) copy-start(s32[512,8]{0,1:T(8,128)} %param.21) | copy-start | bytes 49156
  49.4 43.6 %slice-start = ((s8[4718592]{0:T(1024)(128)(4,1)}), s8[4194304]{0:T(1024)(128)(4,1)S(1)}, s32[]{:S(2)}) async-start(s8[4718592]{0:T(1024)(128)(4,1)} %bitcast.51), calls=%async_computation | async-start | bytes 8388608
  53.4 7.5 %copy-start.6 = (f32[256,1536]{1,0:T(8,128)}, f32[256,1536]{1,0:T(8,128)S(1)}, u32[]{:S(2)}) copy-start(f32[256,1536]{1,0:T(8,128)S(1)} %get-tuple-element.90) | copy-start | bytes 4718596
  54.7 4.2 %collective-permute-start.3 = (s32[8,512]{1,0:T(8,128)S(1)}, s32[8,512]{1,0:T(8,128)S(1)}, u32[]{:S(2)}, u32[]{:S(2)}) collective-permute-start(s32[8,512]{1,0:T(8,128)S(1)} %bitcast.63), channel_id=1, source_target_pairs={{0,2},{1,3},{2,0},{3,1},{4,6},{5,7},{6,4},{7,5}} | collective-permute-start | bytes 49160 | tf_op jit(solution)/shard_map/ppermute | solution.py:322
  57.2 34.3 %collective-permute-start.4 = (s32[8,512]{1,0:T(8,128)S(1)}, s32[8,512]{1,0:T(8,128)S(1)}, u32[]{:S(2)}, u32[]{:S(2)}) collective-permute-start(s32[8,512]{1,0:T(8,128)S(1)} %bitcast.64), channel_id=1, source_target_pairs={{0,4},{1,5},{2,6},{3,7},{4,0},{5,1},{6,2},{7,3}} | collective-permute-start | bytes 49160 | tf_op jit(solution)/shard_map/ppermute | solution.py:322
  58.9 32.6 %copy-start.28 = (s32[8,512]{1,0:T(8,128)}, s32[8,512]{1,0:T(8,128)S(1)}, u32[]{:S(2)}) copy-start(s32[8,512]{1,0:T(8,128)S(1)} %collective-permute-done.3.refs_1_) | copy-start | bytes 49156
  58.9 38.8 %collective-permute-start.6 = (bf16[256,1536]{1,0:T(8,128)(2,1)}, bf16[256,1536]{1,0:T(8,128)(2,1)S(1)}, u32[]{:S(2)}, u32[]{:S(2)}) collective-permute-start(bf16[256,1536]{1,0:T(8,128)(2,1)} %multiply_convert_fusion.1.refs_4_), channel_id=1, source_target_pairs={{0,2},{1,3},{2,0},{3,1},{4,6},{5,7},{6,4},{7,5}} | collective-permute-start | bytes 2359304 | tf_op jit(solution)/shard_map/ppermute | solution.py:322
  60.9 32.1 %slice-start.1 = ((s8[4718592]{0:T(1024)(128)(4,1)}), s8[524288]{0:T(1024)(128)(4,1)S(1)}, s32[]{:S(2)}) async-start(s8[4718592]{0:T(1024)(128)(4,1)} %bitcast.51), calls=%async_computation.1 | async-start | bytes 1048576
  91.5 3.1 %copy-start.29 = (s32[8,512]{1,0:T(8,128)}, s32[8,512]{1,0:T(8,128)S(1)}, u32[]{:S(2)}) copy-start(s32[8,512]{1,0:T(8,128)S(1)} %collective-permute-done.4.refs_2_) | copy-start | bytes 49156
  91.5 4.7 %collective-permute-start.5 = (s32[8,512]{1,0:T(8,128)S(1)}, s32[8,512]{1,0:T(8,128)S(1)}, u32[]{:S(2)}, u32[]{:S(2)}) collective-permute-start(s32[8,512]{1,0:T(8,128)S(1)} %bitcast.65), channel_id=1, source_target_pairs={{0,6},{1,7},{2,4},{3,5},{4,2},{5,3},{6,0},{7,1}} | collective-permute-start | bytes 49160 | tf_op jit(solution)/shard_map/ppermute | solution.py:322
  96.1 38.0 %copy-start.30 = (s32[8,512]{1,0:T(8,128)}, s32[8,512]{1,0:T(8,128)S(1)}, u32[]{:S(2)}) copy-start(s32[8,512]{1,0:T(8,128)S(1)} %collective-permute-done.5.refs_3_) | copy-start | bytes 49156
  96.1 34.5 %collective-permute-start.7 = (bf16[256,1536]{1,0:T(8,128)(2,1)}, bf16[256,1536]{1,0:T(8,128)(2,1)}, u32[]{:S(2)}, u32[]{:S(2)}) collective-permute-start(bf16[256,1536]{1,0:T(8,128)(2,1)} %multiply_convert_fusion.1.refs_4_), channel_id=1, source_target_pairs={{0,4},{1,5},{2,6},{3,7},{4,0},{5,1},{6,2},{7,3}} | collective-permute-start | bytes 2359304 | tf_op jit(solution)/shard_map/ppermute | solution.py:322
  97.7 33.8 %collective-permute-start.8 = (bf16[256,1536]{1,0:T(8,128)(2,1)}, bf16[256,1536]{1,0:T(8,128)(2,1)}, u32[]{:S(2)}, u32[]{:S(2)}) collective-permute-start(bf16[256,1536]{1,0:T(8,128)(2,1)} %multiply_convert_fusion.1.refs_4_), channel_id=1, source_target_pairs={{0,6},{1,7},{2,4},{3,5},{4,2},{5,3},{6,0},{7,1}} | collective-permute-start | bytes 2359304 | tf_op jit(solution)/shard_map/ppermute | solution.py:322
  98.8 70.1 %copy-start.14 = (bf16[256,1536]{1,0:T(8,128)(2,1)}, bf16[256,1536]{1,0:T(8,128)(2,1)S(1)}, u32[]{:S(2)}) copy-start(bf16[256,1536]{1,0:T(8,128)(2,1)S(1)} %multiply_convert_fusion.refs_4_) | copy-start | bytes 2359300
  130.7 38.3 %collective-permute-start = (bf16[256,1536]{1,0:T(8,128)(2,1)S(1)}, bf16[256,1536]{1,0:T(8,128)(2,1)S(1)}, u32[]{:S(2)}, u32[]{:S(2)}) collective-permute-start(bf16[256,1536]{1,0:T(8,128)(2,1)S(1)} %multiply_convert_fusion.refs_4_), channel_id=1, source_target_pairs={{0,2},{1,3},{2,0},{3,1},{4,6},{5,7},{6,4},{7,5}} | collective-permute-start | bytes 2359304 | tf_op jit(solution)/shard_map/ppermute | solution.py:322
  131.5 37.5 %collective-permute-start.1 = (bf16[256,1536]{1,0:T(8,128)(2,1)S(1)}, bf16[256,1536]{1,0:T(8,128)(2,1)S(1)}, u32[]{:S(2)}, u32[]{:S(2)}) collective-permute-start(bf16[256,1536]{1,0:T(8,128)(2,1)S(1)} %multiply_convert_fusion.refs_4_), channel_id=1, source_target_pairs={{0,4},{1,5},{2,6},{3,7},{4,0},{5,1},{6,2},{7,3}} | collective-permute-start | bytes 2359304 | tf_op jit(solution)/shard_map/ppermute | solution.py:322
  132.7 36.2 %collective-permute-start.2 = (bf16[256,1536]{1,0:T(8,128)(2,1)S(1)}, bf16[256,1536]{1,0:T(8,128)(2,1)S(1)}, u32[]{:S(2)}, u32[]{:S(2)}) collective-permute-start(bf16[256,1536]{1,0:T(8,128)(2,1)S(1)} %multiply_convert_fusion.refs_4_), channel_id=1, source_target_pairs={{0,6},{1,7},{2,4},{3,5},{4,2},{5,3},{6,0},{7,1}} | collective-permute-start | bytes 2359304 | tf_op jit(solution)/shard_map/ppermute | solution.py:322
  170.3 40.5 %copy-start.17 = (f32[128,1536]{1,0:T(8,128)S(1)}, f32[128,1536]{1,0:T(8,128)}, u32[]{:S(2)}) copy-start(f32[128,1536]{1,0:T(8,128)} %get-tuple-element.64) | copy-start | bytes 2359300
  170.3 42.6 %copy-start.15 = (f32[128,1536]{1,0:T(8,128)S(1)}, f32[128,1536]{1,0:T(8,128)}, u32[]{:S(2)}) copy-start(f32[128,1536]{1,0:T(8,128)} %get-tuple-element.75) | copy-start | bytes 2359300
  170.3 40.4 %collective-permute-start.13 = (f32[128,1536]{1,0:T(8,128)}, f32[128,1536]{1,0:T(8,128)S(1)}, u32[]{:S(2)}, u32[]{:S(2)}) collective-permute-start(f32[128,1536]{1,0:T(8,128)} %get-tuple-element.65), channel_id=1, source_target_pairs={{0,2},{1,3},{2,0},{3,1},{4,6},{5,7},{6,4},{7,5}} | collective-permute-start | bytes 2359304 | tf_op jit(solution)/shard_map/ppermute | solution.py:322
  171.1 39.6 %collective-permute-start.14 = (f32[128,1536]{1,0:T(8,128)}, f32[128,1536]{1,0:T(8,128)S(1)}, u32[]{:S(2)}, u32[]{:S(2)}) collective-permute-start(f32[128,1536]{1,0:T(8,128)} %get-tuple-element.66), channel_id=1, source_target_pairs={{0,4},{1,5},{2,6},{3,7},{4,0},{5,1},{6,2},{7,3}} | collective-permute-start | bytes 2359304 | tf_op jit(solution)/shard_map/ppermute | solution.py:322
  207.2 22.1 %copy-start.18 = (f32[128,1536]{1,0:T(8,128)S(1)}, f32[128,1536]{1,0:T(8,128)}, u32[]{:S(2)}) copy-start(f32[128,1536]{1,0:T(8,128)} %get-tuple-element.79) | copy-start | bytes 2359300
  207.2 20.6 %collective-permute-start.19 = (f32[128,1536]{1,0:T(8,128)}, f32[128,1536]{1,0:T(8,128)S(1)}, u32[]{:S(2)}, u32[]{:S(2)}) collective-permute-start(f32[128,1536]{1,0:T(8,128)} %get-tuple-element.80), channel_id=1, source_target_pairs={{0,2},{1,3},{2,0},{3,1},{4,6},{5,7},{6,4},{7,5}} | collective-permute-start | bytes 2359304 | tf_op jit(solution)/shard_map/ppermute | solution.py:322
  208.7 36.0 %collective-permute-start.12 = (f32[128,1536]{1,0:T(8,128)}, f32[128,1536]{1,0:T(8,128)S(1)}, u32[]{:S(2)}, u32[]{:S(2)}) collective-permute-start(f32[128,1536]{1,0:T(8,128)} %get-tuple-element.63), channel_id=1, source_target_pairs={{0,2},{1,3},{2,0},{3,1},{4,6},{5,7},{6,4},{7,5}} | collective-permute-start | bytes 2359304 | tf_op jit(solution)/shard_map/ppermute | solution.py:322
  209.2 20.6 %collective-permute-start.22 = (f32[128,1536]{1,0:T(8,128)}, f32[128,1536]{1,0:T(8,128)S(1)}, u32[]{:S(2)}, u32[]{:S(2)}) collective-permute-start(f32[128,1536]{1,0:T(8,128)} %get-tuple-element.84), channel_id=1, source_target_pairs={{0,4},{1,5},{2,6},{3,7},{4,0},{5,1},{6,2},{7,3}} | collective-permute-start | bytes 2359304 | tf_op jit(solution)/shard_map/ppermute | solution.py:322
  210.8 19.1 %copy-start.22 = (f32[128,1536]{1,0:T(8,128)S(1)}, f32[128,1536]{1,0:T(8,128)}, u32[]{:S(2)}) copy-start(f32[128,1536]{1,0:T(8,128)} %get-tuple-element.78) | copy-start | bytes 2359300
  210.8 20.6 %copy-start.16 = (f32[128,1536]{1,0:T(8,128)S(1)}, f32[128,1536]{1,0:T(8,128)}, u32[]{:S(2)}) copy-start(f32[128,1536]{1,0:T(8,128)} %get-tuple-element.83) | copy-start | bytes 2359300
  210.9 33.8 %copy-start.21 = (f32[128,1536]{1,0:T(8,128)S(1)}, f32[128,1536]{1,0:T(8,128)}, u32[]{:S(2)}) copy-start(f32[128,1536]{1,0:T(8,128)} %get-tuple-element.82) | copy-start | bytes 2359300
  210.9 37.3 %copy-start.12 = (f32[128,1536]{1,0:T(8,128)S(1)}, f32[128,1536]{1,0:T(8,128)}, u32[]{:S(2)}) copy-start(f32[128,1536]{1,0:T(8,128)} %get-tuple-element.62) | copy-start | bytes 2359300
  210.9 35.8 %collective-permute-start.15 = (f32[128,1536]{1,0:T(8,128)S(1)}, f32[128,1536]{1,0:T(8,128)S(1)}, u32[]{:S(2)}, u32[]{:S(2)}) collective-permute-start(f32[128,1536]{1,0:T(8,128)S(1)} %add.79), channel_id=1, source_target_pairs={{0,4},{1,5},{2,6},{3,7},{4,0},{5,1},{6,2},{7,3}} | collective-permute-start | bytes 2359304 | tf_op jit(solution)/shard_map/ppermute | solution.py:322
  211.4 52.1 %collective-permute-start.16 = (f32[128,1536]{1,0:T(8,128)}, f32[128,1536]{1,0:T(8,128)S(1)}, u32[]{:S(2)}, u32[]{:S(2)}) collective-permute-start(f32[128,1536]{1,0:T(8,128)} %get-tuple-element.74), channel_id=1, source_target_pairs={{0,4},{1,5},{2,6},{3,7},{4,0},{5,1},{6,2},{7,3}} | collective-permute-start | bytes 2359304 | tf_op jit(solution)/shard_map/ppermute | solution.py:322
  227.8 37.2 %collective-permute-start.17 = (f32[128,1536]{1,0:T(8,128)S(1)}, f32[128,1536]{1,0:T(8,128)S(1)}, u32[]{:S(2)}, u32[]{:S(2)}) collective-permute-start(f32[128,1536]{1,0:T(8,128)S(1)} %add.82), channel_id=1, source_target_pairs={{0,2},{1,3},{2,0},{3,1},{4,6},{5,7},{6,4},{7,5}} | collective-permute-start | bytes 2359304 | tf_op jit(solution)/shard_map/ppermute | solution.py:322
  229.4 35.6 %copy-start.10 = (f32[128,1536]{1,0:T(8,128)S(1)}, f32[128,1536]{1,0:T(8,128)}, u32[]{:S(2)}) copy-start(f32[128,1536]{1,0:T(8,128)} %get-tuple-element.73) | copy-start | bytes 2359300
  229.9 48.5 %collective-permute-start.18 = (f32[128,1536]{1,0:T(8,128)S(1)}, f32[128,1536]{1,0:T(8,128)S(1)}, u32[]{:S(2)}, u32[]{:S(2)}) collective-permute-start(f32[128,1536]{1,0:T(8,128)S(1)} %copy-done.22), channel_id=1, source_target_pairs={{0,2},{1,3},{2,0},{3,1},{4,6},{5,7},{6,4},{7,5}} | collective-permute-start | bytes 2359304 | tf_op jit(solution)/shard_map/ppermute | solution.py:322
  244.7 48.3 %copy-start.13 = (f32[128,1536]{1,0:T(8,128)S(1)}, f32[128,1536]{1,0:T(8,128)}, u32[]{:S(2)}) copy-start(f32[128,1536]{1,0:T(8,128)} %get-tuple-element.77) | copy-start | bytes 2359300
  244.7 48.4 %collective-permute-start.21 = (f32[128,1536]{1,0:T(8,128)S(1)}, f32[128,1536]{1,0:T(8,128)S(1)}, u32[]{:S(2)}, u32[]{:S(2)}) collective-permute-start(f32[128,1536]{1,0:T(8,128)S(1)} %copy-done.21), channel_id=1, source_target_pairs={{0,4},{1,5},{2,6},{3,7},{4,0},{5,1},{6,2},{7,3}} | collective-permute-start | bytes 2359304 | tf_op jit(solution)/shard_map/ppermute | solution.py:322
  246.7 46.3 %collective-permute-start.20 = (f32[128,1536]{1,0:T(8,128)S(1)}, f32[128,1536]{1,0:T(8,128)S(1)}, u32[]{:S(2)}, u32[]{:S(2)}) collective-permute-start(f32[128,1536]{1,0:T(8,128)S(1)} %add.85), channel_id=1, source_target_pairs={{0,4},{1,5},{2,6},{3,7},{4,0},{5,1},{6,2},{7,3}} | collective-permute-start | bytes 2359304 | tf_op jit(solution)/shard_map/ppermute | solution.py:322
  248.4 44.8 %copy-start.11 = (f32[128,1536]{1,0:T(8,128)S(1)}, f32[128,1536]{1,0:T(8,128)}, u32[]{:S(2)}) copy-start(f32[128,1536]{1,0:T(8,128)} %get-tuple-element.81) | copy-start | bytes 2359300
  263.6 29.6 %collective-permute-start.23 = (f32[128,1536]{1,0:T(8,128)S(1)}, f32[128,1536]{1,0:T(8,128)S(1)}, u32[]{:S(2)}, u32[]{:S(2)}) collective-permute-start(f32[128,1536]{1,0:T(8,128)S(1)} %add.88), channel_id=1, source_target_pairs={{0,2},{1,3},{2,0},{3,1},{4,6},{5,7},{6,4},{7,5}} | collective-permute-start | bytes 2359304 | tf_op jit(solution)/shard_map/ppermute | solution.py:322
  265.2 28.1 %copy-start.7 = (f32[256,1536]{1,0:T(8,128)S(1)}, f32[256,1536]{1,0:T(8,128)}, u32[]{:S(2)}) copy-start(f32[256,1536]{1,0:T(8,128)} %copy-done.6) | copy-start | bytes 4718596
  (11 other events, 16.4 us)

commit v4 on v3

--- a/solution.py
+++ b/solution.py
@@ -99,7 +99,7 @@
 
 def project(x_in, cache_len, ln_attn, w_q, w_k, w_v, head_dim):
     n_batch = x_in.shape[0]
-    normed = norm_scale(x_in.astype(jnp.float32), ln_attn).astype(jnp.bfloat16)
+    normed = lax.optimization_barrier(norm_scale(x_in.astype(jnp.float32), ln_attn).astype(jnp.bfloat16))
 
     def proj(w):
         out = with_layout_constraint(jnp.dot(normed, w, preferred_element_type=jnp.float32), Layout(major_to_minor=(1, 0)))
@@ -356,33 +356,37 @@
                 picks, own[0] = lax.optimization_barrier((topk_idx.T, own[0]))
                 t_blocks = [picks, swap(picks, 2), swap(picks, 4), swap(picks, 6)]
 
-        sums = []
+        def sums_of(c, names):
+            ids = ["oxyd".index(n) for n in names]
+            blocks = [(own[c], *far[c])[i] for i in ids]
+            return experts(c, blocks, [t_blocks[i] for i in ids], devs, w_r, w_own, w_par)
+
+        outs = []
+        waiting = None
         for c in range(CHUNKS):
-            h_o, h_far = own[c], far[c]
             if c == 0:
-                h_o, own[-1] = lax.optimization_barrier((h_o, own[-1]))
+                far[0], own[-1] = lax.optimization_barrier((far[0], own[-1]))
             else:
-                h_far, sums[c - 1] = lax.optimization_barrier((h_far, sums[c - 1]))
-            s_o, s_x, s_y, s_d = experts(c, [h_o, *h_far], t_blocks, devs, w_r, w_own, w_par)
-            sums.append((s_o, s_x, s_y, s_d))
-        outs = []
-        sent = []
-        for c in range(CHUNKS):
-            s_o, s_x, s_y, s_d = sums[c]
-            d_x = swap(s_d[0], 2)
-            d_y = swap(s_d[1], 4)
+                far[c], s_x = lax.optimization_barrier((far[c], s_x))
+                waiting[1] = s_x
+            if c:
+                s_y, s_d = sums_of(c, "yd")
+            else:
+                s_o, s_x, s_y, s_d = sums_of(c, "oxyd")
+            if c:
+                p_o, p_x, p_y, d_x, d_y, u_x, u_y = waiting
+                d_x, d_y, s_y = lax.optimization_barrier((d_x, d_y, s_y))
+                m_x, m_y = swap(p_x[1] + d_y, 2), swap(p_y[0] + d_x, 4)
+                outs += [p_o[0] + u_x + m_y, p_o[1] + u_y + m_x]
+            d_x, d_y = swap(s_d[0], 2), swap(s_d[1], 4)
+            u_y = swap(s_y[1], 4)
+            if c:
+                own[c], s_y = lax.optimization_barrier((own[c], s_y))
+                s_o, s_x = sums_of(c, "ox")
             u_x = swap(s_x[0], 2)
-            u_y = swap(s_y[1], 4)
-            sent.append((d_x, d_y, u_x, u_y))
-        last = sums[-1][0][0]
-        for c in range(CHUNKS):
-            s_o, s_x, s_y, s_d = sums[c]
-            d_x, d_y, u_x, u_y = sent[c]
-            if c < CHUNKS - 1:
-                d_x, d_y, last = lax.optimization_barrier((d_x, d_y, last))
-                sums[-1] = ((last, sums[-1][0][1]), *sums[-1][1:])
-            m_x, m_y = swap(s_x[1] + d_y, 2), swap(s_y[0] + d_x, 4)
-            outs += [s_o[0] + u_x + m_y, s_o[1] + u_y + m_x]
+            waiting = [s_o, s_x, s_y, d_x, d_y, u_x, u_y]
+        m_x, m_y = swap(s_x[1] + d_y, 2), swap(s_y[0] + d_x, 4)
+        outs += [s_o[0] + u_x + m_y, s_o[1] + u_y + m_x]
         x_out = (jnp.concatenate(resid, axis=0) + jnp.concatenate(outs, axis=0)).astype(jnp.bfloat16)
         by_row = lambda c: c.reshape(n_slots, kv_heads, head_dim, n_batch).transpose(3, 0, 1, 2)
         return x_out, by_row(k_full), by_row(v_full)

time: 295 us -> 282 us (0.956)
  waiting for transfers between devices: 105 us -> 76.9 us
  Pallas kernels: 131 us -> 140 us
  other arithmetic: 7.43 us -> 13.4 us
    ppermute x24, waiting for transfers between devices: 105 us -> 76.9 us  [swap(): return lax.ppermute(value, 'ep', [(i, i ^ bit) for i in range(ep_size)])]
    pallas_call x2 -> x3, Pallas kernels: 69.5 us -> 79.2 us  [experts(): pl.pallas_call(functools.partial(expert_kernel, n_sub, e_local), grid_spe...]
    add x0 -> x4, other arithmetic: none -> 3.69 us  [the longest x2 2.23 us: device_step(): m_x, m_y = (swap(p_x[1] + d_y, 2), swap(p_y[0] + d_x, 4))]
  transfers between devices with their start and end apart: 24 -> 24, of which waited for: 10 -> 5; matrix products, arithmetic and copies ran while one was open for 8% -> 10% of each run, Pallas kernels for 44% -> 50%
where the time goes in v4:
time: 282 us; the launch traced here: 281 us
  Pallas kernels  140 us (50%)
  waiting for transfers between devices  76.9 us (27%)
  starting transfers between devices  28.7 us (10%)
  matrix products  16.1 us (6%)
  other arithmetic  13.4 us (5%)
  local copies, waits for them, and re-layouts  4.85 us (2%)
    pallas_call x3, Pallas kernels, experts(): pl.pallas_call(functools.partial(expert_kernel, n_sub, e_local), grid_spe...  79.2 us
    ppermute x24, waiting for transfers between devices, swap(): return lax.ppermute(value, 'ep', [(i, i ^ bit) for i in range(ep_size)])  76.9 us
    pallas_call x2, Pallas kernels, attend(): pl.pallas_call(body, grid=(kv_heads,), in_specs=[pl.BlockSpec(memory_spac...  61.1 us
    ppermute x24, starting transfers between devices, swap(): return lax.ppermute(value, 'ep', [(i, i ^ bit) for i in range(ep_size)])  28.7 us
    dot_general x3, matrix products, proj(): jnp.dot(normed, w, preferred_element_type=jnp.float32)  10.5 us
  transfers between devices with their start and end apart: 24, of which 5 were waited for; matrix products, arithmetic and copies ran while one was open for 10% of the time, Pallas kernels for 50%

profile of v4, /device:TPU:0, one launch (start us, length us, event | category | flops | bytes accessed | tf_op | source)
XLA Modules:
  0.0 281.4 jit_solution(1187777620325368857)
XLA Ops:
  0.7 0.9 collective-permute-start.6
  1.6 0.5 collective-permute-start.8
  2.0 0.7 convert_element_type.43
  2.7 1.8 fusion
  4.5 0.4 fusion.2
  5.0 6.7 %fusion.6 = f32[512,1536]{0,1:T(8,128)} fusion(bf16[512,1536]{1,0:T(8,128)(2,1)S(1)} %fusion.2, bf16[1536,1536]{1,0:T(8,128)(2,1)} %param.23), kind=kOutput, calls=%fused_computation.29 | convolution fusion | flops 2415919104 | bytes 9437184 | tf_op jit(solution)/shard_map/dot_general | solution.py:105
  11.7 2.0 fusion.7
  13.7 1.8 convolution_convert_fusion
  16.1 1.2 copy-done.3
  17.3 1.0 copy-done.4
  18.3 30.6 %attend.2 = (bf16[64,8,8,8,512]{4,3,2,1,0:T(8,128)(2,1)}, bf16[64,8,8,8,512]{4,3,2,1,0:T(8,128)(2,1)}, bf16[24,64,256]{2,1,0:T(8,128)(2,1)S(1)}) custom-call(s32[1,512]{1,0:T(1,128)S(1)} %bitcast.52, f32[32,512]{1,0:T(8,128)S(1)} %get-tuple-element.84.refs_1_.refs_3_, f32[32,512]{1,0:T(8,128)S(1)} %get-tuple-element.83.refs_2_.refs_4_, ...), custom_call_target="tpu_custom_call" | custom-call | flops 30000001024 | bytes 70000000 | tf_op jit(solution)/shard_map/attend/pallas_call | solution.py:129
  48.9 4.0 %multiply_reduce_fusion.1 = (f32[256]{0:T(256)S(1)}, f32[256,1536]{1,0:T(8,128)S(1)}) fusion(bf16[1536,256]{1,0:T(8,128)(2,1)S(1)} %bitcast.47, bf16[1536,1536]{1,0:T(8,128)(2,1)} %param.28, bf16[512,1536]{1,0:T(8,128)(2,1)S(1)} %copy-done.7), kind=kOutput, calls=%fused_computation.14 | convolution fusion | flops 1209925376 | bytes 7865344 | tf_op jit(solution)/shard_map/dot_general | solution.py:346
  53.0 1.3 multiply_convert_fusion.1.refs_4_
  54.3 2.5 collective-permute-start.3
  56.8 30.5 %attend.3 = (bf16[64,8,8,8,512]{4,3,2,1,0:T(8,128)(2,1)}, bf16[64,8,8,8,512]{4,3,2,1,0:T(8,128)(2,1)}, bf16[24,64,256]{2,1,0:T(8,128)(2,1)S(1)}) custom-call(bf16[64,8,8,8,512]{4,3,2,1,0:T(8,128)(2,1)} %get-tuple-element.44.refs_0_, bf16[64,8,8,8,512]{4,3,2,1,0:T(8,128)(2,1)} %get-tuple-element.45.refs_1_, ...), custom_call_target="tpu_custom_call", output_to_operand_aliasing={{0}: (0, {}), {1}: (1, {})} | custom-call | flops 30000001024 | bytes 70000000 | tf_op jit(solution)/shard_map/attend/pallas_call | solution.py:129
  87.3 2.0 collective-permute-start.4
  89.4 1.4 collective-permute-start.5
  90.8 1.5 multiply_reduce_fusion
  92.6 31.4 %collective-permute-done.4.refs_6_ = bf16[256,1536]{1,0:T(8,128)(2,1)S(1)} collective-permute-done((bf16[256,1536]{1,0:T(8,128)(2,1)}, bf16[256,1536]{1,0:T(8,128)(2,1)S(1)}, u32[]{:S(2)}, u32[]{:S(2)}) %collective-permute-start.4) | collective-permute-done | bytes 786464 | tf_op jit(solution)/shard_map/ppermute | solution.py:322
  124.1 1.7 collective-permute-start.1
  125.8 1.4 collective-permute-start.2
  127.3 0.6 pad_add_fusion.dev_ref
  127.9 1.7 collective-permute-start.12
  129.5 1.1 collective-permute-done.2.refs_3_.refs_1_
  130.6 0.4 collective-permute-start.13
  131.1 2.5 collective-permute-start.14
  133.6 34.7 %experts.3 = (f32[128,1536]{1,0:T(8,128)}, f32[128,1536]{1,0:T(8,128)}, f32[128,1536]{1,0:T(8,128)}, f32[128,1536]{1,0:T(8,128)}, f32[128,1536]{1,0:T(8,128)}, /...) custom-call(s32[2]{0:T(128)} %pad_add_fusion.dev_ref, bf16[40,1536]{1,0:T(8,128)(2,1)} %bitcast.62, ...), custom_call_target="tpu_custom_call" | custom-call | flops 32000000000 | bytes 60000000 | tf_op jit(solution)/shard_map/experts/pallas_call | solution.py:292
  168.4 0.5 collective-permute-start.10
  169.0 0.4 collective-permute-start.11
  169.4 22.4 %experts.4 = (f32[128,1536]{1,0:T(8,128)}, f32[128,1536]{1,0:T(8,128)}, f32[128,1536]{1,0:T(8,128)}, f32[128,1536]{1,0:T(8,128)}) custom-call(s32[2]{0:T(128)} %pad_add_fusion.dev_ref, bf16[40,1536]{1,0:T(8,128)(2,1)} %bitcast.63, s32[8,512]{1,0:T(8,128)} %copy-done.30, s32[8,512]{1,0:T(8,128)} %copy-done.31, bf16[256,1536]{1,0:T(8,128)(2,1)} %copy-done.27, ...), custom_call_target="tpu_custom_call" | custom-call | flops 16000000000 | bytes 60000000 | tf_op jit(solution)/shard_map/experts/pallas_call | solution.py:292
  191.8 1.7 collective-permute-start.19
  193.4 0.4 collective-permute-start.9
  193.8 2.1 collective-permute-start.16
  195.9 2.1 add.79
  198.1 2.0 collective-permute-start.15
  200.2 12.4 %collective-permute-done.19 = f32[128,1536]{1,0:T(8,128)} collective-permute-done((f32[128,1536]{1,0:T(8,128)}, f32[128,1536]{1,0:T(8,128)}, u32[]{:S(2)}, u32[]{:S(2)}) %collective-permute-start.19) | collective-permute-done | bytes 786464 | tf_op jit(solution)/shard_map/ppermute | solution.py:322
  212.5 1.6 collective-permute-start.17
  214.2 22.2 %experts.5 = (f32[128,1536]{1,0:T(8,128)}, f32[128,1536]{1,0:T(8,128)}, f32[128,1536]{1,0:T(8,128)}, f32[128,1536]{1,0:T(8,128)}) custom-call(s32[2]{0:T(128)} %pad_add_fusion.dev_ref, bf16[40,1536]{1,0:T(8,128)(2,1)} %bitcast.64, s32[8,512]{1,0:T(8,128)} %bitcast.66, s32[8,512]{1,0:T(8,128)} %copy-done.29, bf16[256,1536]{1,0:T(8,128)(2,1)} %copy-done.10, ...), custom_call_target="tpu_custom_call" | custom-call | flops 16000000000 | bytes 60000000 | tf_op jit(solution)/shard_map/experts/pallas_call | solution.py:292
  236.4 1.3 add.85
  237.8 2.4 collective-permute-start.21
  240.2 1.2 add.88
  241.8 6.5 %collective-permute-done.15 = f32[128,1536]{1,0:T(8,128)} collective-permute-done((f32[128,1536]{1,0:T(8,128)}, f32[128,1536]{1,0:T(8,128)}, u32[]{:S(2)}, u32[]{:S(2)}) %collective-permute-start.15) | collective-permute-done | bytes 786464 | tf_op jit(solution)/shard_map/ppermute | solution.py:322
  248.3 2.0 collective-permute-start.18
  250.3 1.3 add_add_fusion.3
  251.9 25.4 %collective-permute-done.20 = f32[128,1536]{1,0:T(8,128)S(1)} collective-permute-done((f32[128,1536]{1,0:T(8,128)S(1)}, f32[128,1536]{1,0:T(8,128)S(1)}, u32[]{:S(2)}, u32[]{:S(2)}) %collective-permute-start.20) | collective-permute-done | bytes 786464 | tf_op jit(solution)/shard_map/ppermute | solution.py:322
  277.4 1.0 copy-done.13
  278.5 1.3 copy-done.9
  279.8 1.6 fusion.3
  (109 shorter events, 1.9 us)
Async XLA Ops:
  0.6 11.0 %copy-start = (bf16[1536,512]{1,0:T(8,128)(2,1)S(1)}, bf16[1536,512]{1,0:T(8,128)(2,1)}, u32[]{:S(2)}) copy-start(bf16[1536,512]{1,0:T(8,128)(2,1)} %param.24) | copy-start | bytes 4718596
  0.6 3.9 %copy-start.6 = (bf16[512,1536]{1,0:T(8,128)(2,1)S(1)}, bf16[512,1536]{1,0:T(8,128)(2,1)}, u32[]{:S(2)}) copy-start(bf16[512,1536]{1,0:T(8,128)(2,1)} %param.17) | copy-start | bytes 4718596
  0.7 130.4 %collective-permute-start.6 = (bf16[5,1536,512]{2,1,0:T(8,128)(2,1)}, bf16[5,1536,512]{2,1,0:T(8,128)(2,1)}, u32[]{:S(2)}, u32[]{:S(2)}) collective-permute-start(bf16[5,1536,512]{2,1,0:T(8,128)(2,1)} %refs_4_.3), channel_id=1, source_target_pairs={{0,1},{1,0},{2,3},{3,2},{4,5},{5,4},{6,7},{7,6}} | collective-permute-start | bytes 23592968 | tf_op jit(solution)/shard_map/ppermute | solution.py:322
  1.5 132.1 %collective-permute-start.7 = (bf16[5,1536,512]{2,1,0:T(8,128)(2,1)}, bf16[5,1536,512]{2,1,0:T(8,128)(2,1)}, u32[]{:S(2)}, u32[]{:S(2)}) collective-permute-start(bf16[5,1536,512]{2,1,0:T(8,128)(2,1)} %refs_5_.3), channel_id=1, source_target_pairs={{0,1},{1,0},{2,3},{3,2},{4,5},{5,4},{6,7},{7,6}} | collective-permute-start | bytes 23592968 | tf_op jit(solution)/shard_map/ppermute | solution.py:322
  1.6 132.1 %collective-permute-start.8 = (bf16[5,512,1536]{2,1,0:T(8,128)(2,1)}, bf16[5,512,1536]{2,1,0:T(8,128)(2,1)}, u32[]{:S(2)}, u32[]{:S(2)}) collective-permute-start(bf16[5,512,1536]{2,1,0:T(8,128)(2,1)} %refs_6_.3), channel_id=1, source_target_pairs={{0,1},{1,0},{2,3},{3,2},{4,5},{5,4},{6,7},{7,6}} | collective-permute-start | bytes 23592968 | tf_op jit(solution)/shard_map/ppermute | solution.py:322
  13.7 2.1 copy-start.19
  13.7 2.4 copy-start.2
  18.3 30.6 %copy-start.7 = (bf16[512,1536]{1,0:T(8,128)(2,1)S(1)}, bf16[512,1536]{1,0:T(8,128)(2,1)}, u32[]{:S(2)}) copy-start(bf16[512,1536]{1,0:T(8,128)(2,1)} %param.17) | copy-start | bytes 4718596
  48.9 41.9 %slice-start = ((s8[4718592]{0:T(1024)(128)(4,1)}), s8[4194304]{0:T(1024)(128)(4,1)S(1)}, s32[]{:S(2)}) async-start(s8[4718592]{0:T(1024)(128)(4,1)} %bitcast.54), calls=%async_computation | async-start | bytes 8388608
  53.0 34.4 %copy-start.8 = (f32[256,1536]{1,0:T(8,128)}, f32[256,1536]{1,0:T(8,128)S(1)}, u32[]{:S(2)}) copy-start(f32[256,1536]{1,0:T(8,128)S(1)} %get-tuple-element.86) | copy-start | bytes 4718596
  53.0 3.8 %copy-start.28 = (s32[512,8]{0,1:T(8,128)S(1)}, s32[512,8]{0,1:T(8,128)}, u32[]{:S(2)}) copy-start(s32[512,8]{0,1:T(8,128)} %param.21) | copy-start | bytes 49156
  54.3 35.1 %collective-permute-start.3 = (bf16[256,1536]{1,0:T(8,128)(2,1)}, bf16[256,1536]{1,0:T(8,128)(2,1)S(1)}, u32[]{:S(2)}, u32[]{:S(2)}) collective-permute-start(bf16[256,1536]{1,0:T(8,128)(2,1)} %multiply_convert_fusion.1.refs_4_), channel_id=1, source_target_pairs={{0,2},{1,3},{2,0},{3,1},{4,6},{5,7},{6,4},{7,5}} | collective-permute-start | bytes 2359304 | tf_op jit(solution)/shard_map/ppermute | solution.py:322
  56.8 30.6 %collective-permute-start = (s32[8,512]{1,0:T(8,128)S(1)}, s32[8,512]{1,0:T(8,128)S(1)}, u32[]{:S(2)}, u32[]{:S(2)}) collective-permute-start(s32[8,512]{1,0:T(8,128)S(1)} %bitcast.67), channel_id=1, source_target_pairs={{0,2},{1,3},{2,0},{3,1},{4,6},{5,7},{6,4},{7,5}} | collective-permute-start | bytes 49160 | tf_op jit(solution)/shard_map/ppermute | solution.py:322
  56.8 34.0 %slice-start.1 = ((s8[4718592]{0:T(1024)(128)(4,1)}), s8[524288]{0:T(1024)(128)(4,1)S(1)}, s32[]{:S(2)}) async-start(s8[4718592]{0:T(1024)(128)(4,1)} %bitcast.54), calls=%async_computation.1 | async-start | bytes 1048576
  87.3 5.0 %copy-start.29 = (s32[8,512]{1,0:T(8,128)}, s32[8,512]{1,0:T(8,128)S(1)}, u32[]{:S(2)}) copy-start(s32[8,512]{1,0:T(8,128)S(1)} %collective-permute-done.refs_1_) | copy-start | bytes 49156
  87.3 36.7 %collective-permute-start.4 = (bf16[256,1536]{1,0:T(8,128)(2,1)}, bf16[256,1536]{1,0:T(8,128)(2,1)S(1)}, u32[]{:S(2)}, u32[]{:S(2)}) collective-permute-start(bf16[256,1536]{1,0:T(8,128)(2,1)} %multiply_convert_fusion.1.refs_4_), channel_id=1, source_target_pairs={{0,4},{1,5},{2,6},{3,7},{4,0},{5,1},{6,2},{7,3}} | collective-permute-start | bytes 2359304 | tf_op jit(solution)/shard_map/ppermute | solution.py:322
  89.4 3.0 %copy-start.23 = (bf16[256,1536]{1,0:T(8,128)(2,1)}, bf16[256,1536]{1,0:T(8,128)(2,1)S(1)}, u32[]{:S(2)}) copy-start(bf16[256,1536]{1,0:T(8,128)(2,1)S(1)} %collective-permute-done.3.refs_5_) | copy-start | bytes 2359300
  89.4 36.4 %collective-permute-start.5 = (bf16[256,1536]{1,0:T(8,128)(2,1)}, bf16[256,1536]{1,0:T(8,128)(2,1)S(1)}, u32[]{:S(2)}, u32[]{:S(2)}) collective-permute-start(bf16[256,1536]{1,0:T(8,128)(2,1)} %multiply_convert_fusion.1.refs_4_), channel_id=1, source_target_pairs={{0,6},{1,7},{2,4},{3,5},{4,2},{5,3},{6,0},{7,1}} | collective-permute-start | bytes 2359304 | tf_op jit(solution)/shard_map/ppermute | solution.py:322
  92.6 75.7 %copy-start.10 = (bf16[256,1536]{1,0:T(8,128)(2,1)}, bf16[256,1536]{1,0:T(8,128)(2,1)S(1)}, u32[]{:S(2)}) copy-start(bf16[256,1536]{1,0:T(8,128)(2,1)S(1)} %multiply_convert_fusion.refs_2_) | copy-start | bytes 2359300
  124.1 9.5 %copy-start.24 = (bf16[256,1536]{1,0:T(8,128)(2,1)}, bf16[256,1536]{1,0:T(8,128)(2,1)S(1)}, u32[]{:S(2)}) copy-start(bf16[256,1536]{1,0:T(8,128)(2,1)S(1)} %collective-permute-done.4.refs_6_) | copy-start | bytes 2359300
  124.1 3.8 %collective-permute-start.1 = (s32[8,512]{1,0:T(8,128)S(1)}, s32[8,512]{1,0:T(8,128)S(1)}, u32[]{:S(2)}, u32[]{:S(2)}) collective-permute-start(s32[8,512]{1,0:T(8,128)S(1)} %bitcast.68), channel_id=1, source_target_pairs={{0,4},{1,5},{2,6},{3,7},{4,0},{5,1},{6,2},{7,3}} | collective-permute-start | bytes 49160 | tf_op jit(solution)/shard_map/ppermute | solution.py:322
  125.8 7.8 %copy-start.25 = (bf16[256,1536]{1,0:T(8,128)(2,1)}, bf16[256,1536]{1,0:T(8,128)(2,1)S(1)}, u32[]{:S(2)}) copy-start(bf16[256,1536]{1,0:T(8,128)(2,1)S(1)} %collective-permute-done.5.refs_7_) | copy-start | bytes 2359300
  125.8 4.8 %collective-permute-start.2 = (s32[8,512]{1,0:T(8,128)S(1)}, s32[8,512]{1,0:T(8,128)S(1)}, u32[]{:S(2)}, u32[]{:S(2)}) collective-permute-start(s32[8,512]{1,0:T(8,128)S(1)} %bitcast.69), channel_id=1, source_target_pairs={{0,6},{1,7},{2,4},{3,5},{4,2},{5,3},{6,0},{7,1}} | collective-permute-start | bytes 49160 | tf_op jit(solution)/shard_map/ppermute | solution.py:322
  127.9 5.8 %copy-start.30 = (s32[8,512]{1,0:T(8,128)}, s32[8,512]{1,0:T(8,128)S(1)}, u32[]{:S(2)}) copy-start(s32[8,512]{1,0:T(8,128)S(1)} %collective-permute-done.1.refs_2_.refs_0_) | copy-start | bytes 49156
  127.9 40.5 %collective-permute-start.12 = (bf16[256,1536]{1,0:T(8,128)(2,1)S(1)}, bf16[256,1536]{1,0:T(8,128)(2,1)S(1)}, u32[]{:S(2)}, u32[]{:S(2)}) collective-permute-start(bf16[256,1536]{1,0:T(8,128)(2,1)S(1)} %multiply_convert_fusion.refs_2_), channel_id=1, source_target_pairs={{0,2},{1,3},{2,0},{3,1},{4,6},{5,7},{6,4},{7,5}} | collective-permute-start | bytes 2359304 | tf_op jit(solution)/shard_map/ppermute | solution.py:322
  130.6 3.0 %copy-start.31 = (s32[8,512]{1,0:T(8,128)}, s32[8,512]{1,0:T(8,128)S(1)}, u32[]{:S(2)}) copy-start(s32[8,512]{1,0:T(8,128)S(1)} %collective-permute-done.2.refs_3_.refs_1_) | copy-start | bytes 49156
  130.6 37.8 %collective-permute-start.13 = (bf16[256,1536]{1,0:T(8,128)(2,1)S(1)}, bf16[256,1536]{1,0:T(8,128)(2,1)S(1)}, u32[]{:S(2)}, u32[]{:S(2)}) collective-permute-start(bf16[256,1536]{1,0:T(8,128)(2,1)S(1)} %multiply_convert_fusion.refs_2_), channel_id=1, source_target_pairs={{0,4},{1,5},{2,6},{3,7},{4,0},{5,1},{6,2},{7,3}} | collective-permute-start | bytes 2359304 | tf_op jit(solution)/shard_map/ppermute | solution.py:322
  131.1 37.3 %collective-permute-start.14 = (bf16[256,1536]{1,0:T(8,128)(2,1)S(1)}, bf16[256,1536]{1,0:T(8,128)(2,1)}, u32[]{:S(2)}, u32[]{:S(2)}) collective-permute-start(bf16[256,1536]{1,0:T(8,128)(2,1)S(1)} %multiply_convert_fusion.refs_2_), channel_id=1, source_target_pairs={{0,6},{1,7},{2,4},{3,5},{4,2},{5,3},{6,0},{7,1}} | collective-permute-start | bytes 2359304 | tf_op jit(solution)/shard_map/ppermute | solution.py:322
  168.4 23.4 %copy-start.22 = (bf16[256,1536]{1,0:T(8,128)(2,1)}, bf16[256,1536]{1,0:T(8,128)(2,1)S(1)}, u32[]{:S(2)}) copy-start(bf16[256,1536]{1,0:T(8,128)(2,1)S(1)} %collective-permute-done.12.refs_3_) | copy-start | bytes 2359300
  168.4 27.5 %collective-permute-start.10 = (f32[128,1536]{1,0:T(8,128)}, f32[128,1536]{1,0:T(8,128)}, u32[]{:S(2)}, u32[]{:S(2)}) collective-permute-start(f32[128,1536]{1,0:T(8,128)} %get-tuple-element.57), channel_id=1, source_target_pairs={{0,2},{1,3},{2,0},{3,1},{4,6},{5,7},{6,4},{7,5}} | collective-permute-start | bytes 2359304 | tf_op jit(solution)/shard_map/ppermute | solution.py:322
  169.0 27.0 %copy-start.16 = (f32[128,1536]{1,0:T(8,128)S(1)}, f32[128,1536]{1,0:T(8,128)}, u32[]{:S(2)}) copy-start(f32[128,1536]{1,0:T(8,128)} %get-tuple-element.56) | copy-start | bytes 2359300
  169.0 27.0 %collective-permute-start.11 = (f32[128,1536]{1,0:T(8,128)}, f32[128,1536]{1,0:T(8,128)S(1)}, u32[]{:S(2)}, u32[]{:S(2)}) collective-permute-start(f32[128,1536]{1,0:T(8,128)} %get-tuple-element.58), channel_id=1, source_target_pairs={{0,4},{1,5},{2,6},{3,7},{4,0},{5,1},{6,2},{7,3}} | collective-permute-start | bytes 2359304 | tf_op jit(solution)/shard_map/ppermute | solution.py:322
  191.8 8.3 %copy-start.15 = (f32[128,1536]{1,0:T(8,128)S(1)}, f32[128,1536]{1,0:T(8,128)}, u32[]{:S(2)}) copy-start(f32[128,1536]{1,0:T(8,128)} %get-tuple-element.67) | copy-start | bytes 2359300
  191.8 20.8 %collective-permute-start.19 = (f32[128,1536]{1,0:T(8,128)}, f32[128,1536]{1,0:T(8,128)}, u32[]{:S(2)}, u32[]{:S(2)}) collective-permute-start(f32[128,1536]{1,0:T(8,128)} %get-tuple-element.77), channel_id=1, source_target_pairs={{0,2},{1,3},{2,0},{3,1},{4,6},{5,7},{6,4},{7,5}} | collective-permute-start | bytes 2359304 | tf_op jit(solution)/shard_map/ppermute | solution.py:322
  193.4 48.0 %collective-permute-start.9 = (f32[128,1536]{1,0:T(8,128)}, f32[128,1536]{1,0:T(8,128)S(1)}, u32[]{:S(2)}, u32[]{:S(2)}) collective-permute-start(f32[128,1536]{1,0:T(8,128)} %get-tuple-element.55), channel_id=1, source_target_pairs={{0,2},{1,3},{2,0},{3,1},{4,6},{5,7},{6,4},{7,5}} | collective-permute-start | bytes 2359304 | tf_op jit(solution)/shard_map/ppermute | solution.py:322
  193.8 57.8 %collective-permute-start.16 = (f32[128,1536]{1,0:T(8,128)}, f32[128,1536]{1,0:T(8,128)S(1)}, u32[]{:S(2)}, u32[]{:S(2)}) collective-permute-start(f32[128,1536]{1,0:T(8,128)} %get-tuple-element.66), channel_id=1, source_target_pairs={{0,4},{1,5},{2,6},{3,7},{4,0},{5,1},{6,2},{7,3}} | collective-permute-start | bytes 2359304 | tf_op jit(solution)/shard_map/ppermute | solution.py:322
  195.9 41.8 %collective-permute-start.22 = (f32[128,1536]{1,0:T(8,128)}, f32[128,1536]{1,0:T(8,128)}, u32[]{:S(2)}, u32[]{:S(2)}) collective-permute-start(f32[128,1536]{1,0:T(8,128)} %get-tuple-element.80), channel_id=1, source_target_pairs={{0,4},{1,5},{2,6},{3,7},{4,0},{5,1},{6,2},{7,3}} | collective-permute-start | bytes 2359304 | tf_op jit(solution)/shard_map/ppermute | solution.py:322
  198.1 50.2 %collective-permute-start.15 = (f32[128,1536]{1,0:T(8,128)}, f32[128,1536]{1,0:T(8,128)}, u32[]{:S(2)}, u32[]{:S(2)}) collective-permute-start(f32[128,1536]{1,0:T(8,128)} %add.79), channel_id=1, source_target_pairs={{0,4},{1,5},{2,6},{3,7},{4,0},{5,1},{6,2},{7,3}} | collective-permute-start | bytes 2359304 | tf_op jit(solution)/shard_map/ppermute | solution.py:322
  200.2 36.2 %copy-start.17 = (f32[128,1536]{1,0:T(8,128)S(1)}, f32[128,1536]{1,0:T(8,128)}, u32[]{:S(2)}) copy-start(f32[128,1536]{1,0:T(8,128)} %get-tuple-element.76) | copy-start | bytes 2359300
  212.5 39.2 %collective-permute-start.17 = (f32[128,1536]{1,0:T(8,128)S(1)}, f32[128,1536]{1,0:T(8,128)S(1)}, u32[]{:S(2)}, u32[]{:S(2)}) collective-permute-start(f32[128,1536]{1,0:T(8,128)S(1)} %add.82), channel_id=1, source_target_pairs={{0,2},{1,3},{2,0},{3,1},{4,6},{5,7},{6,4},{7,5}} | collective-permute-start | bytes 2359304 | tf_op jit(solution)/shard_map/ppermute | solution.py:322
  236.4 3.8 %copy-start.18 = (f32[128,1536]{1,0:T(8,128)S(1)}, f32[128,1536]{1,0:T(8,128)}, u32[]{:S(2)}) copy-start(f32[128,1536]{1,0:T(8,128)} %get-tuple-element.79) | copy-start | bytes 2359300
  237.7 10.6 %copy-start.26 = (f32[128,1536]{1,0:T(8,128)S(1)}, f32[128,1536]{1,0:T(8,128)}, u32[]{:S(2)}) copy-start(f32[128,1536]{1,0:T(8,128)} %get-tuple-element.75) | copy-start | bytes 2359300
  237.7 12.6 %copy-start.12 = (f32[128,1536]{1,0:T(8,128)S(1)}, f32[128,1536]{1,0:T(8,128)}, u32[]{:S(2)}) copy-start(f32[128,1536]{1,0:T(8,128)} %get-tuple-element.54) | copy-start | bytes 2359300
  237.8 39.7 %collective-permute-start.21 = (f32[128,1536]{1,0:T(8,128)S(1)}, f32[128,1536]{1,0:T(8,128)S(1)}, u32[]{:S(2)}, u32[]{:S(2)}) collective-permute-start(f32[128,1536]{1,0:T(8,128)S(1)} %copy-done.21), channel_id=1, source_target_pairs={{0,4},{1,5},{2,6},{3,7},{4,0},{5,1},{6,2},{7,3}} | collective-permute-start | bytes 2359304 | tf_op jit(solution)/shard_map/ppermute | solution.py:322
  241.4 35.8 %collective-permute-start.20 = (f32[128,1536]{1,0:T(8,128)S(1)}, f32[128,1536]{1,0:T(8,128)S(1)}, u32[]{:S(2)}, u32[]{:S(2)}) collective-permute-start(f32[128,1536]{1,0:T(8,128)S(1)} %add.85), channel_id=1, source_target_pairs={{0,4},{1,5},{2,6},{3,7},{4,0},{5,1},{6,2},{7,3}} | collective-permute-start | bytes 2359304 | tf_op jit(solution)/shard_map/ppermute | solution.py:322
  248.3 28.9 %collective-permute-start.18 = (f32[128,1536]{1,0:T(8,128)S(1)}, f32[128,1536]{1,0:T(8,128)S(1)}, u32[]{:S(2)}, u32[]{:S(2)}) collective-permute-start(f32[128,1536]{1,0:T(8,128)S(1)} %copy-done.26), channel_id=1, source_target_pairs={{0,2},{1,3},{2,0},{3,1},{4,6},{5,7},{6,4},{7,5}} | collective-permute-start | bytes 2359304 | tf_op jit(solution)/shard_map/ppermute | solution.py:322
  251.7 25.7 %collective-permute-start.23 = (f32[128,1536]{1,0:T(8,128)S(1)}, f32[128,1536]{1,0:T(8,128)S(1)}, u32[]{:S(2)}, u32[]{:S(2)}) collective-permute-start(f32[128,1536]{1,0:T(8,128)S(1)} %add.88), channel_id=1, source_target_pairs={{0,2},{1,3},{2,0},{3,1},{4,6},{5,7},{6,4},{7,5}} | collective-permute-start | bytes 2359304 | tf_op jit(solution)/shard_map/ppermute | solution.py:322
  251.7 25.5 %copy-start.14 = (f32[128,1536]{1,0:T(8,128)S(1)}, f32[128,1536]{1,0:T(8,128)}, u32[]{:S(2)}) copy-start(f32[128,1536]{1,0:T(8,128)} %get-tuple-element.74) | copy-start | bytes 2359300
  (12 other events, 17.9 us)
